TPU v7x, 32 devices: a whole 2x2x4 slice. The times are simulated.
32 devices in a mesh: section: 8 (over z, x), dp: 4 (over y, core).
Axes of the slice: x: 2, y: 2, z: 4, core: 2. Of those that a mesh axis runs over, the one named last changes fastest.
Arguments:
- carry_act: bfloat16 [8, 32, 2304], P('section', 'dp'), may hold values from -6 to 6
- carry_act_tan: bfloat16 [8, 32, 2304], P('section', 'dp'), may hold values from -6 to 6
- carry_adj: bfloat16 [8, 32, 2304], P('section', 'dp'), may hold values from -0.75 to 0.75
- carry_adj_tan: bfloat16 [8, 32, 2304], P('section', 'dp'), may hold values from -0.75 to 0.75
- fresh_act: bfloat16 [2, 32, 2304], P(None, 'dp'), may hold values from -6 to 6
- loss_cot: bfloat16 [2, 32, 2304], P(None, 'dp'), may hold values from -0.75 to 0.75
- stash_act: bfloat16 [8, 2, 32, 2304], P('section', None, 'dp'), may hold values from -6 to 6
- stash_act_tan: bfloat16 [8, 2, 32, 2304], P('section', None, 'dp'), may hold values from -6 to 6
- norm_gain: bfloat16 [8, 2304], P('section'), may hold values from 0.25 to 1.75
- up_weight: bfloat16 [8, 2304, 4608], P('section', None, 'dp'), may hold values from -0.125 to 0.125
- down_weight: bfloat16 [8, 4608, 2304], P('section', 'dp'), may hold values from -0.09375 to 0.09375
- up_dir: bfloat16 [8, 2304, 4608], P('section', None, 'dp'), may hold values from -0.125 to 0.125
- down_dir: bfloat16 [8, 4608, 2304], P('section', 'dp'), may hold values from -0.09375 to 0.09375
Outputs:
- next_act: bfloat16 [8, 32, 2304], P('section', 'dp')
- next_act_tan: bfloat16 [8, 32, 2304], P('section', 'dp')
- next_adj: bfloat16 [8, 32, 2304], P('section', 'dp')
- next_adj_tan: bfloat16 [8, 32, 2304], P('section', 'dp')
- hvp_up: bfloat16 [8, 2304, 4608], P('section', None, 'dp')
- hvp_down: bfloat16 [8, 4608, 2304], P('section', 'dp')
All inputs are finite; a program needn't handle non-finite values.
Results may differ from a plain program's by a relative error of at most 0.02.
Values may be sent and summed in bfloat16 or wider, within the bound.
No kernel may reach another device: no remote copies, remote signals or barrier semaphores. Data moves between devices by JAX's collectives and lax.ppermute only.
A program may use at most 128 MiB of HBM per device.

v0:
```python
import jax
import jax.numpy as jnp
from jax import lax
from jax.sharding import PartitionSpec as P

TICKS = 2


sqrt_two_over_pi = 0.7978845608028654
cubic_coef = 0.044715
norm_eps = 1e-06


def passed_along(value, axis, steps):
    count = lax.axis_size(axis)
    leading, last = (max(0, -steps), min(count, count - steps))
    return lax.ppermute(value, axis, [(source, source + steps) for source in range(leading, last)])


def gelu_parts(linear):
    inner_arg = sqrt_two_over_pi * (linear + cubic_coef * linear * linear * linear)
    first_slope = sqrt_two_over_pi * (1.0 + 3.0 * cubic_coef * linear * linear)
    second_slope = 6.0 * sqrt_two_over_pi * cubic_coef * linear
    tanh_value = jnp.tanh(inner_arg)
    sech_square = 1.0 - tanh_value * tanh_value
    gelu_value = 0.5 * linear * (1.0 + tanh_value)
    gelu_first = 0.5 * (1.0 + tanh_value) + 0.5 * linear * sech_square * first_slope
    gelu_second = sech_square * (
        first_slope - linear * tanh_value * first_slope * first_slope + 0.5 * linear * second_slope
    )
    return (gelu_value, gelu_first, gelu_second)


def matrix_product(left, right):
    return jnp.dot(left, right, preferred_element_type=jnp.float32)


def product_last(left, right):
    return lax.dot_general(
        left, right, (((1,), (1,)), ((), ())), preferred_element_type=jnp.float32
    )


def product_first(left, right):
    return lax.dot_general(
        left, right, (((0,), (0,)), ((), ())), preferred_element_type=jnp.float32
    )


def norm_stats(rows, rows_tan):
    values = rows.astype(jnp.float32)
    values_tan = rows_tan.astype(jnp.float32)
    inverse = lax.rsqrt(jnp.mean(values * values, axis=-1, keepdims=True) + norm_eps)
    inverse_tan = -(inverse * inverse * inverse) * jnp.mean(
        values * values_tan, axis=-1, keepdims=True
    )
    return (values, values_tan, inverse, inverse_tan)


def norm_rows(rows, rows_tan, gain_row):
    values, values_tan, inverse, inverse_tan = norm_stats(rows, rows_tan)
    gain_wide = gain_row.astype(jnp.float32)
    normed = (values * inverse * gain_wide).astype(jnp.bfloat16)
    normed_tan = ((values_tan * inverse + values * inverse_tan) * gain_wide).astype(jnp.bfloat16)
    return (normed, normed_tan)


def norm_back(rows, rows_tan, gain_row, arriving, arriving_tan, summed, summed_tan):
    values, values_tan, inverse, inverse_tan = norm_stats(rows, rows_tan)
    gain_wide = gain_row.astype(jnp.float32)
    weighted = summed * gain_wide
    weighted_tan = summed_tan * gain_wide
    moment = jnp.mean(values * weighted, axis=-1, keepdims=True)
    moment_tan = jnp.mean(values_tan * weighted + values * weighted_tan, axis=-1, keepdims=True)
    inverse_cube = inverse * inverse * inverse
    returned = arriving.astype(jnp.float32) + inverse * weighted - inverse_cube * values * moment
    returned_tan = (
        arriving_tan.astype(jnp.float32)
        + inverse_tan * weighted
        + inverse * weighted_tan
        - 3.0 * inverse * inverse * inverse_tan * values * moment
        - inverse_cube * values_tan * moment
        - inverse_cube * values * moment_tan
    )
    return (returned.astype(jnp.bfloat16), returned_tan.astype(jnp.bfloat16))


def branch_forward(normed, normed_tan, up_local, down_local, up_direction, down_direction):
    linear = matrix_product(normed, up_local)
    linear_tan = matrix_product(normed_tan, up_local) + matrix_product(normed, up_direction)
    gelu_value, gelu_first, gelu_second = gelu_parts(linear)
    hidden = gelu_value.astype(jnp.bfloat16)
    hidden_tan = (gelu_first * linear_tan).astype(jnp.bfloat16)
    partial_value = matrix_product(hidden, down_local)
    partial_tan = matrix_product(hidden_tan, down_local) + matrix_product(hidden, down_direction)
    return (partial_value, partial_tan)


def branch_backward(
    stash_normed,
    stash_normed_tan,
    adjoint_all,
    adjoint_all_tan,
    up_local,
    down_local,
    up_direction,
    down_direction,
):
    linear = matrix_product(stash_normed, up_local)
    linear_tan = matrix_product(stash_normed_tan, up_local) + matrix_product(
        stash_normed, up_direction
    )
    gelu_value, gelu_first, gelu_second = gelu_parts(linear)
    hidden = gelu_value.astype(jnp.bfloat16)
    hidden_tan = (gelu_first * linear_tan).astype(jnp.bfloat16)
    upstream = product_last(adjoint_all, down_local)
    upstream_tan = product_last(adjoint_all_tan, down_local) + product_last(
        adjoint_all, down_direction
    )
    deltas = (upstream * gelu_first).astype(jnp.bfloat16)
    deltas_tan = (upstream_tan * gelu_first + upstream * gelu_second * linear_tan).astype(
        jnp.bfloat16
    )
    curvature_down = product_first(hidden_tan, adjoint_all) + product_first(hidden, adjoint_all_tan)
    curvature_up = product_first(stash_normed_tan, deltas) + product_first(stash_normed, deltas_tan)
    partial_value = product_last(deltas, up_local)
    partial_tan = product_last(deltas_tan, up_local) + product_last(deltas, up_direction)
    return (partial_value, partial_tan, curvature_up, curvature_down)


def gather_rows(lead_rows, lead_tan, stash_rows, stash_tan, adjoint_rows, adjoint_tan):
    forward_rows = (
        lax.all_gather(lead_rows, "dp", axis=0, tiled=True),
        lax.all_gather(lead_tan, "dp", axis=0, tiled=True),
    )
    backward_rows = (
        lax.all_gather(stash_rows, "dp", axis=0, tiled=True),
        lax.all_gather(stash_tan, "dp", axis=0, tiled=True),
        lax.all_gather(adjoint_rows, "dp", axis=0, tiled=True),
        lax.all_gather(adjoint_tan, "dp", axis=0, tiled=True),
    )
    return (forward_rows, backward_rows)


def reduce_rows(forward_term, forward_tan, backward_term, backward_tan):
    summed_forward = (
        lax.psum_scatter(
            forward_term.astype(jnp.bfloat16), "dp", scatter_dimension=0, tiled=True
        ).astype(jnp.float32),
        lax.psum_scatter(
            forward_tan.astype(jnp.bfloat16), "dp", scatter_dimension=0, tiled=True
        ).astype(jnp.float32),
    )
    summed_backward = (
        lax.psum_scatter(
            backward_term.astype(jnp.bfloat16), "dp", scatter_dimension=0, tiled=True
        ).astype(jnp.float32),
        lax.psum_scatter(
            backward_tan.astype(jnp.bfloat16), "dp", scatter_dimension=0, tiled=True
        ).astype(jnp.float32),
    )
    return (summed_forward, summed_backward)


def shards(
    carry_act,
    carry_act_tan,
    carry_adj,
    carry_adj_tan,
    fresh_act,
    loss_cot,
    stash_act,
    stash_act_tan,
    norm_gain,
    up_weight,
    down_weight,
    up_dir,
    down_dir,
):
    section_index = lax.axis_index("section")
    section_count = lax.axis_size("section")
    at_first = section_index == 0
    at_last = section_index == section_count - 1
    gain_row = norm_gain[0]
    up_local = up_weight[0]
    down_local = down_weight[0]
    up_direction = up_dir[0]
    down_direction = down_dir[0]
    activation, activation_tan = (carry_act[0], carry_act_tan[0])
    adjoint, adjoint_tan = (carry_adj[0], carry_adj_tan[0])
    total_up = jnp.zeros(up_local.shape, jnp.float32)
    total_down = jnp.zeros(down_local.shape, jnp.float32)
    for tick_index in range(TICKS):
        fresh_rows = fresh_act[tick_index]
        cotangent = loss_cot[tick_index]
        zero_rows = jnp.zeros_like(fresh_rows)
        stash_rows = stash_act[0, tick_index]
        stash_tan = stash_act_tan[0, tick_index]
        moved_forward = passed_along((activation, activation_tan), "section", 1)
        moved_backward = passed_along((adjoint, adjoint_tan), "section", -1)
        input_rows = jnp.where(at_first, fresh_rows, moved_forward[0])
        input_tan = jnp.where(at_first, zero_rows, moved_forward[1])
        arriving = jnp.where(at_last, cotangent, moved_backward[0])
        arriving_tan = jnp.where(at_last, zero_rows, moved_backward[1])
        normed, normed_tan = norm_rows(input_rows, input_tan, gain_row)
        stash_normed, stash_normed_tan = norm_rows(stash_rows, stash_tan, gain_row)
        forward_rows, backward_rows = gather_rows(
            normed, normed_tan, stash_normed, stash_normed_tan, arriving, arriving_tan
        )
        normed_all, normed_all_tan = (forward_rows[0], forward_rows[1])
        stash_all, stash_all_tan = (backward_rows[0], backward_rows[1])
        adjoint_all, adjoint_all_tan = (backward_rows[2], backward_rows[3])
        partial_value, partial_tan = branch_forward(
            normed_all, normed_all_tan, up_local, down_local, up_direction, down_direction
        )
        back_partial, back_partial_tan, curvature_up, curvature_down = branch_backward(
            stash_all,
            stash_all_tan,
            adjoint_all,
            adjoint_all_tan,
            up_local,
            down_local,
            up_direction,
            down_direction,
        )
        summed_forward, summed_backward = reduce_rows(
            partial_value, partial_tan, back_partial, back_partial_tan
        )
        total_up = total_up + curvature_up
        total_down = total_down + curvature_down
        activation = (input_rows.astype(jnp.float32) + summed_forward[0]).astype(jnp.bfloat16)
        activation_tan = (input_tan.astype(jnp.float32) + summed_forward[1]).astype(jnp.bfloat16)
        adjoint, adjoint_tan = norm_back(
            stash_rows,
            stash_tan,
            gain_row,
            arriving,
            arriving_tan,
            summed_backward[0],
            summed_backward[1],
        )
    return (
        activation[None],
        activation_tan[None],
        adjoint[None],
        adjoint_tan[None],
        total_up.astype(jnp.bfloat16)[None],
        total_down.astype(jnp.bfloat16)[None],
    )


def solution(mesh):
    in_specs = (
        P("section", "dp", None),
        P("section", "dp", None),
        P("section", "dp", None),
        P("section", "dp", None),
        P(None, "dp", None),
        P(None, "dp", None),
        P("section", None, "dp", None),
        P("section", None, "dp", None),
        P("section", None),
        P("section", None, "dp"),
        P("section", "dp", None),
        P("section", None, "dp"),
        P("section", "dp", None),
    )
    out_specs = (
        P("section", "dp", None),
        P("section", "dp", None),
        P("section", "dp", None),
        P("section", "dp", None),
        P("section", None, "dp"),
        P("section", "dp", None),
    )
    return jax.shard_map(shards, mesh=mesh, in_specs=in_specs, out_specs=out_specs, check_vma=False)
```

profile of v0, /device:TPU:0, one launch (start us, length us, event | category | flops | bytes accessed | tf_op | source)
XLA Modules:
  0.0 396.7 jit_solution(5366362785262543976)
XLA Ops:
  7.2 1.6 collective-permute-start.4
  8.8 1.3 collective-permute-start.6
  10.1 6.3 %collective-permute-start.2 = (bf16[8,2304]{1,0:T(8,128)(2,1)}, bf16[8,2304]{1,0:T(8,128)(2,1)S(1)}, u32[]{:S(2)}, u32[]{:S(2)}) collective-permute-start(bf16[8,2304]{1,0:T(8,128)(2,1)} %bitcast.246), channel_id=1, source_target_pairs={{0,4},{4,8},{8,12},{12,16},{16,20},{20,24},{24,28},{1,5},{5,9},{9,... | collective-permute-start | bytes 110600 | tf_op jit(solution)/shard_map/ppermute | solution.py:17
  16.4 4.8 %collective-permute-start = (bf16[8,2304]{1,0:T(8,128)(2,1)}, bf16[8,2304]{1,0:T(8,128)(2,1)S(1)}, u32[]{:S(2)}, u32[]{:S(2)}) collective-permute-start(bf16[8,2304]{1,0:T(8,128)(2,1)} %bitcast.247), channel_id=1, source_target_pairs={{0,4},{4,8},{8,12},{12,16},{16,20},{20,24},{24,28},{1,5},{5,9},{9,... | collective-permute-start | bytes 110600 | tf_op jit(solution)/shard_map/ppermute | solution.py:17
  23.8 5.5 %all_gather.41 = bf16[32,2304]{1,0:T(8,128)(2,1)S(1)} all-gather(bf16[8,2304]{1,0:T(8,128)(2,1)S(1)} %get-tuple-element.31), channel_id=1, replica_groups=mesh['section'=8,'dp'=4] {'dp'}, dimensions={0}, use_global_device_ids=true | all-gather | bytes 184320 | tf_op jit(solution)/shard_map/all_gather | solution.py:137
  29.3 5.6 %all_gather.45 = bf16[32,2304]{1,0:T(8,128)(2,1)S(1)} all-gather(bf16[8,2304]{1,0:T(8,128)(2,1)S(1)} %get-tuple-element.30), channel_id=1, replica_groups=mesh['section'=8,'dp'=4] {'dp'}, dimensions={0}, use_global_device_ids=true | all-gather | bytes 184320 | tf_op jit(solution)/shard_map/all_gather | solution.py:138
  34.9 3.5 fusion.20
  39.4 1.0 fusion.56
  40.5 5.5 %all_gather.40 = bf16[32,2304]{1,0:T(8,128)(2,1)S(1)} all-gather(bf16[8,2304]{1,0:T(8,128)(2,1)S(1)} %bitcast_select_fusion), channel_id=1, replica_groups=mesh['section'=8,'dp'=4] {'dp'}, dimensions={0}, use_global_device_ids=true | all-gather | bytes 184320 | tf_op jit(solution)/shard_map/all_gather | solution.py:139
  46.0 4.1 %fusion.8 = f32[32,1152]{1,0:T(8,128)S(1)} fusion(bf16[32,2304]{1,0:T(8,128)(2,1)S(1)} %all_gather.40, bf16[1,1152,2304]{2,1,0:T(8,128)(2,1)} %param.25), kind=kOutput, calls=%fused_computation.12 | convolution fusion | flops 169869312 | bytes 5603328 | tf_op jit(solution)/shard_map/dot_general | solution.py:39
  50.1 4.3 %multiply_convert_fusion.5 = (bf16[32,1152]{1,0:T(8,128)(2,1)S(1)}, f32[32,1152]{1,0:T(8,128)S(1)}) fusion(f32[32,1152]{1,0:T(8,128)S(1)} %fusion.56, bf16[32,2304]{1,0:T(8,128)(2,1)S(1)} %all_gather.40, bf16[1,1152,2304]{2,1,0:T(8,128)(2,1)} %param.23), kind=kOutput, calls=%fused_computation.159 | convolution fusion | flops 170569728 | bytes 5824512 | tf_op jit(solution)/shard_map/dot_general | solution.py:39
  54.4 5.6 %fusion.304 = f32[2304,1152]{1,0:T(8,128)} fusion(bf16[32,2304]{1,0:T(8,128)(2,1)S(1)} %all_gather.45, bf16[32,1152]{1,0:T(8,128)(2,1)S(1)} %get-tuple-element.48), kind=kOutput, calls=%fused_computation.331 | convolution fusion | flops 169869312 | bytes 10838016 | tf_op jit(solution)/shard_map/dot_general | solution.py:45
  60.1 1.5 fusion.18
  61.6 5.6 %all_gather.44 = bf16[32,2304]{1,0:T(8,128)(2,1)S(1)} all-gather(bf16[8,2304]{1,0:T(8,128)(2,1)S(1)} %broadcast_select_fusion.1), channel_id=1, replica_groups=mesh['section'=8,'dp'=4] {'dp'}, dimensions={0}, use_global_device_ids=true | all-gather | bytes 184320 | tf_op jit(solution)/shard_map/all_gather | solution.py:140
  67.2 5.5 %fusion.242 = f32[1152,2304]{1,0:T(8,128)} fusion(bf16[32,2304]{1,0:T(8,128)(2,1)S(1)} %all_gather.44, f32[32,1152]{1,0:T(8,128)S(1)} %fusion.56), kind=kOutput, calls=%fused_computation.240 | convolution fusion | flops 170201088 | bytes 10911744 | tf_op jit(solution)/shard_map/dot_general | solution.py:45
  72.7 1.7 fusion.141
  74.5 2.2 fusion.87
  76.8 4.7 %fusion.90 = bf16[32,2304]{1,0:T(8,128)(2,1)} fusion(bf16[32,1152]{1,0:T(8,128)(2,1)S(1)} %get-tuple-element.48, bf16[1,2304,1152]{2,1,0:T(8,128)(2,1)} %param.22), kind=kOutput, calls=%fused_computation.78 | convolution fusion | flops 169943040 | bytes 5529600 | tf_op jit(solution)/shard_map/dot_general | solution.py:39
  81.8 15.2 %reduce-scatter.21.cloned.1.call-done = bf16[8,2304]{1,0:T(8,128)(2,1)} async-done(((bf16[32,2304]{1,0:T(8,128)(2,1)}), bf16[8,2304]{1,0:T(8,128)(2,1)}) %reduce-scatter.21.cloned.1.call-update) | async-done | bytes 36880 | tf_op jit(solution)/shard_map/reduce_scatter | solution.py:158
  97.0 22.7 %reduce-scatter.17.cloned.1.call-done = bf16[8,2304]{1,0:T(8,128)(2,1)} async-done(((bf16[32,2304]{1,0:T(8,128)(2,1)}), bf16[8,2304]{1,0:T(8,128)(2,1)}) %reduce-scatter.17.cloned.1.call-update) | async-done | bytes 36880 | tf_op jit(solution)/shard_map/reduce_scatter | solution.py:155
  121.7 16.8 %all_gather.43 = bf16[32,2304]{1,0:T(8,128)(2,1)S(1)} all-gather(bf16[8,2304]{1,0:T(8,128)(2,1)S(1)} %get-tuple-element.29), channel_id=1, replica_groups=mesh['section'=8,'dp'=4] {'dp'}, dimensions={0}, use_global_device_ids=true | all-gather | bytes 184320 | tf_op jit(solution)/shard_map/all_gather | solution.py:137
  138.5 3.7 fusion.52
  142.2 3.9 fusion.16
  146.0 1.3 collective-permute-start.7
  147.4 5.6 %all_gather.47 = bf16[32,2304]{1,0:T(8,128)(2,1)S(1)} all-gather(bf16[8,2304]{1,0:T(8,128)(2,1)S(1)} %get-tuple-element.24), channel_id=1, replica_groups=mesh['section'=8,'dp'=4] {'dp'}, dimensions={0}, use_global_device_ids=true | all-gather | bytes 184320 | tf_op jit(solution)/shard_map/all_gather | solution.py:138
  153.0 1.4 collective-permute-start.5
  155.4 4.2 %collective-permute-done.5 = bf16[8,2304]{1,0:T(8,128)(2,1)S(1)} collective-permute-done((bf16[8,2304]{1,0:T(8,128)(2,1)S(1)}, bf16[8,2304]{1,0:T(8,128)(2,1)S(1)}, u32[]{:S(2)}, u32[]{:S(2)}) %collective-permute-start.5) | collective-permute-done | bytes 36896 | tf_op jit(solution)/shard_map/ppermute | solution.py:17
  159.6 5.5 %all_gather.42 = bf16[32,2304]{1,0:T(8,128)(2,1)S(1)} all-gather(bf16[8,2304]{1,0:T(8,128)(2,1)S(1)} %bitcast_select_fusion.1), channel_id=1, replica_groups=mesh['section'=8,'dp'=4] {'dp'}, dimensions={0}, use_global_device_ids=true | all-gather | bytes 184320 | tf_op jit(solution)/shard_map/all_gather | solution.py:139
  165.1 1.6 fusion.6
  166.7 1.6 multiply_convert_fusion.4
  168.4 1.6 fusion.305
  170.0 1.5 fusion.14
  171.6 5.5 %all_gather.46 = bf16[32,2304]{1,0:T(8,128)(2,1)S(1)} all-gather(bf16[8,2304]{1,0:T(8,128)(2,1)S(1)} %broadcast_select_fusion), channel_id=1, replica_groups=mesh['section'=8,'dp'=4] {'dp'}, dimensions={0}, use_global_device_ids=true | all-gather | bytes 184320 | tf_op jit(solution)/shard_map/all_gather | solution.py:140
  177.0 5.5 %fusion.243 = f32[1152,2304]{1,0:T(8,128)} fusion(bf16[32,2304]{1,0:T(8,128)(2,1)S(1)} %all_gather.46, f32[32,1152]{1,0:T(8,128)S(1)} %fusion.52), kind=kOutput, calls=%fused_computation.241 | convolution fusion | flops 170201088 | bytes 10911744 | tf_op jit(solution)/shard_map/dot_general | solution.py:45
  182.5 9.5 %convolution_add_fusion = f32[1152,2304]{1,0:T(8,128)} fusion(f32[1152,2304]{1,0:T(8,128)} %fusion.243, bf16[32,2304]{1,0:T(8,128)(2,1)S(1)} %all_gather.42, f32[32,1152]{1,0:T(8,128)S(1)} %fusion.117, f32[32,1152]{1,0:T(8,128)S(1)} %fusion.52), kind=kOutput, calls=%fused_computation | convolution fusion | flops 173223936 | bytes 21676032 | tf_op jit(solution)/shard_map/dot_general | solution.py:45
  192.1 1.7 fusion.138
  193.8 5.6 %convolution_add_fusion.2 = f32[2304,1152]{1,0:T(8,128)} fusion(f32[2304,1152]{1,0:T(8,128)S(1)} %fusion.305, bf16[32,2304]{1,0:T(8,128)(2,1)S(1)} %all_gather.43, bf16[32,1152]{1,0:T(8,128)(2,1)S(1)} %fusion.138), kind=kOutput, calls=%fused_computation.2 | convolution fusion | flops 172523520 | bytes 21454848 | tf_op jit(solution)/shard_map/dot_general | solution.py:45
  199.3 2.2 fusion.84
  201.7 11.1 %fusion.5 = bf16[1,1152,2304]{2,1,0:T(8,128)(2,1)} fusion(f32[1152,2304]{1,0:T(8,128)} %convolution_add_fusion, f32[1152,2304]{1,0:T(8,128)} %fusion.242, bf16[32,2304]{1,0:T(8,128)(2,1)S(1)} %all_gather.40, f32[32,1152]{1,0:T(8,128)S(1)} %fusion.114, f32[32,1152]{1,0:T(8,128)S(1)} %fusion.56), kind=kOutput, calls=%fused_computation.9 | convolution fusion | flops 178532352 | bytes 26984448 | tf_op jit(solution)/shard_map/dot_general | solution.py:45
  212.7 4.7 %fusion.93 = bf16[32,2304]{1,0:T(8,128)(2,1)} fusion(bf16[32,1152]{1,0:T(8,128)(2,1)S(1)} %get-tuple-element.50, bf16[1,2304,1152]{2,1,0:T(8,128)(2,1)} %param.22), kind=kOutput, calls=%fused_computation.79 | convolution fusion | flops 169943040 | bytes 5529600 | tf_op jit(solution)/shard_map/dot_general | solution.py:39
  217.5 11.0 %fusion.4 = bf16[1,2304,1152]{2,1,0:T(8,128)(2,1)} fusion(f32[2304,1152]{1,0:T(8,128)} %convolution_add_fusion.2, f32[2304,1152]{1,0:T(8,128)} %fusion.304, bf16[32,2304]{1,0:T(8,128)(2,1)S(1)} %all_gather.41, bf16[32,1152]{1,0:T(8,128)(2,1)S(1)} %fusion.141), kind=kOutput, calls=%fused_computation.8 | convolution fusion | flops 177831936 | bytes 26763264 | tf_op jit(solution)/shard_map/dot_general | solution.py:45
  228.5 15.4 %reduce-scatter.19.cloned.1.call-done = bf16[8,2304]{1,0:T(8,128)(2,1)} async-done(((bf16[32,2304]{1,0:T(8,128)(2,1)}), bf16[8,2304]{1,0:T(8,128)(2,1)}) %reduce-scatter.19.cloned.1.call-update) | async-done | bytes 36880 | tf_op jit(solution)/shard_map/reduce_scatter | solution.py:155
  243.9 1.0 fusion.231
  245.0 5.8 %all_gather.36 = bf16[32,2304]{1,0:T(8,128)(2,1)S(1)} all-gather(bf16[8,2304]{1,0:T(8,128)(2,1)S(1)} %get-tuple-element.38), channel_id=1, replica_groups=mesh['section'=8,'dp'=4] {'dp'}, dimensions={0}, use_global_device_ids=true | all-gather | bytes 184320 | tf_op jit(solution)/shard_map/all_gather | solution.py:133
  250.7 3.6 fusion.64
  254.3 3.5 fusion.24
  258.7 5.5 %all_gather.38 = bf16[32,2304]{1,0:T(8,128)(2,1)S(1)} all-gather(bf16[8,2304]{1,0:T(8,128)(2,1)S(1)} %get-tuple-element.39), channel_id=1, replica_groups=mesh['section'=8,'dp'=4] {'dp'}, dimensions={0}, use_global_device_ids=true | all-gather | bytes 184320 | tf_op jit(solution)/shard_map/all_gather | solution.py:134
  264.2 6.7 %fusion.81 = bf16[32,2304]{1,0:T(8,128)(2,1)} fusion(f32[32,2304]{1,0:T(8,128)S(1)} %fusion.12, bf16[1,1152,2304]{2,1,0:T(8,128)(2,1)} %param.23, f32[32,1152]{1,0:T(8,128)S(1)} %fusion.24, bf16[32,2304]{1,0:T(8,128)(2,1)S(1)} %all_gather.38, bf16[1,2304,1152]{2,1,0:T(8,128)(2,1)} %param.22, f32[32,1152]{1,0:T(8,128)S(1)} %fusion.64), kind=kOutput, calls=%fused_computation.75 | convolution fusion | flops 340623360 | bytes 11501568 | tf_op jit(solution)/shard_map/dot_general | solution.py:35
  271.0 4.0 %fusion.96 = bf16[32,2304]{1,0:T(8,128)(2,1)} fusion(bf16[1,1152,2304]{2,1,0:T(8,128)(2,1)} %param.23, f32[32,1152]{1,0:T(8,128)S(1)} %fusion.64), kind=kOutput, calls=%fused_computation.80 | convolution fusion | flops 170274816 | bytes 5603328 | tf_op jit(solution)/shard_map/dot_general | solution.py:35
  275.0 15.7 %reduce-scatter.13.cloned.1.call-done = bf16[8,2304]{1,0:T(8,128)(2,1)} async-done(((bf16[32,2304]{1,0:T(8,128)(2,1)}), bf16[8,2304]{1,0:T(8,128)(2,1)}) %reduce-scatter.13.cloned.1.call-update) | async-done | bytes 36880 | tf_op jit(solution)/shard_map/reduce_scatter | solution.py:150
  291.5 3.4 collective-permute-start.3
  294.9 17.8 %reduce-scatter.9.cloned.1.call-done = bf16[8,2304]{1,0:T(8,128)(2,1)} async-done(((bf16[32,2304]{1,0:T(8,128)(2,1)}), bf16[8,2304]{1,0:T(8,128)(2,1)}) %reduce-scatter.9.cloned.1.call-update) | async-done | bytes 36880 | tf_op jit(solution)/shard_map/reduce_scatter | solution.py:147
  313.5 3.4 collective-permute-start.1
  316.9 1.6 collective-permute-done.1
  319.5 5.6 %all_gather.37 = bf16[32,2304]{1,0:T(8,128)(2,1)S(1)} all-gather(bf16[8,2304]{1,0:T(8,128)(2,1)S(1)} %get-tuple-element.36), channel_id=1, replica_groups=mesh['section'=8,'dp'=4] {'dp'}, dimensions={0}, use_global_device_ids=true | all-gather | bytes 184320 | tf_op jit(solution)/shard_map/all_gather | solution.py:133
  325.1 3.6 fusion.62
  328.7 3.5 fusion.22
  333.1 5.5 %all_gather.39 = bf16[32,2304]{1,0:T(8,128)(2,1)S(1)} all-gather(bf16[8,2304]{1,0:T(8,128)(2,1)S(1)} %get-tuple-element.37), channel_id=1, replica_groups=mesh['section'=8,'dp'=4] {'dp'}, dimensions={0}, use_global_device_ids=true | all-gather | bytes 184320 | tf_op jit(solution)/shard_map/all_gather | solution.py:134
  338.5 6.7 %fusion.78 = bf16[32,2304]{1,0:T(8,128)(2,1)} fusion(f32[32,2304]{1,0:T(8,128)S(1)} %fusion.10, bf16[1,1152,2304]{2,1,0:T(8,128)(2,1)} %param.23, f32[32,1152]{1,0:T(8,128)S(1)} %fusion.22, bf16[32,2304]{1,0:T(8,128)(2,1)S(1)} %all_gather.39, bf16[1,2304,1152]{2,1,0:T(8,128)(2,1)} %param.22, f32[32,1152]{1,0:T(8,128)S(1)} %fusion.62), kind=kOutput, calls=%fused_computation.74 | convolution fusion | flops 340623360 | bytes 11501568 | tf_op jit(solution)/shard_map/dot_general | solution.py:35
  345.3 4.0 %fusion.99 = bf16[32,2304]{1,0:T(8,128)(2,1)} fusion(bf16[1,1152,2304]{2,1,0:T(8,128)(2,1)} %param.23, f32[32,1152]{1,0:T(8,128)S(1)} %fusion.62), kind=kOutput, calls=%fused_computation.81 | convolution fusion | flops 170274816 | bytes 5603328 | tf_op jit(solution)/shard_map/dot_general | solution.py:35
  349.3 16.6 %reduce-scatter.15.cloned.1.call-done = bf16[8,2304]{1,0:T(8,128)(2,1)} async-done(((bf16[32,2304]{1,0:T(8,128)(2,1)}), bf16[8,2304]{1,0:T(8,128)(2,1)}) %reduce-scatter.15.cloned.1.call-update) | async-done | bytes 36880 | tf_op jit(solution)/shard_map/reduce_scatter | solution.py:150
  365.9 1.4 fusion.277
  367.3 20.7 %reduce-scatter.11.cloned.1.call-done = bf16[8,2304]{1,0:T(8,128)(2,1)} async-done(((bf16[32,2304]{1,0:T(8,128)(2,1)}), bf16[8,2304]{1,0:T(8,128)(2,1)}) %reduce-scatter.11.cloned.1.call-update) | async-done | bytes 36880 | tf_op jit(solution)/shard_map/reduce_scatter | solution.py:147
  388.1 1.4 fusion.276
  (107 shorter events, 11.6 us)
Async XLA Ops:
  7.2 89.8 %reduce-scatter.21.cloned.1.call-start = ((), (), s32[]{:S(2)}) async-start(), calls=%async_computation.14 | async-start | bytes 184320 | tf_op jit(solution)/shard_map/reduce_scatter | solution.py:158
  7.2 31.2 %copy-start = (bf16[1,2304,1152]{2,1,0:T(8,128)(2,1)S(1)}, bf16[1,2304,1152]{2,1,0:T(8,128)(2,1)}, u32[]{:S(2)}) copy-start(bf16[1,2304,1152]{2,1,0:T(8,128)(2,1)} %param.22) | copy-start | bytes 15925252
  7.2 33.2 %collective-permute-start.4 = (bf16[8,2304]{1,0:T(8,128)(2,1)}, bf16[8,2304]{1,0:T(8,128)(2,1)S(1)}, u32[]{:S(2)}, u32[]{:S(2)}) collective-permute-start(bf16[8,2304]{1,0:T(8,128)(2,1)} %bitcast.244), channel_id=1, source_target_pairs={{4,0},{8,4},{12,8},{16,12},{20,16},{24,20},{28,24},{5,1},{9,5},{13... | collective-permute-start | bytes 110600 | tf_op jit(solution)/shard_map/ppermute | solution.py:17
  8.8 52.8 %collective-permute-start.6 = (bf16[8,2304]{1,0:T(8,128)(2,1)}, bf16[8,2304]{1,0:T(8,128)(2,1)S(1)}, u32[]{:S(2)}, u32[]{:S(2)}) collective-permute-start(bf16[8,2304]{1,0:T(8,128)(2,1)} %bitcast.245), channel_id=1, source_target_pairs={{4,0},{8,4},{12,8},{16,12},{20,16},{24,20},{28,24},{5,1},{9,5},{13... | collective-permute-start | bytes 110600 | tf_op jit(solution)/shard_map/ppermute | solution.py:17
  10.1 71.5 %collective-permute-start.2 = (bf16[8,2304]{1,0:T(8,128)(2,1)}, bf16[8,2304]{1,0:T(8,128)(2,1)S(1)}, u32[]{:S(2)}, u32[]{:S(2)}) collective-permute-start(bf16[8,2304]{1,0:T(8,128)(2,1)} %bitcast.246), channel_id=1, source_target_pairs={{0,4},{4,8},{8,12},{12,16},{16,20},{20,24},{24,28},{1,5},{5,9},{9,... | collective-permute-start | bytes 110600 | tf_op jit(solution)/shard_map/ppermute | solution.py:17
  16.4 65.3 %collective-permute-start = (bf16[8,2304]{1,0:T(8,128)(2,1)}, bf16[8,2304]{1,0:T(8,128)(2,1)S(1)}, u32[]{:S(2)}, u32[]{:S(2)}) collective-permute-start(bf16[8,2304]{1,0:T(8,128)(2,1)} %bitcast.247), channel_id=1, source_target_pairs={{0,4},{4,8},{8,12},{12,16},{16,20},{20,24},{24,28},{1,5},{5,9},{9,... | collective-permute-start | bytes 110600 | tf_op jit(solution)/shard_map/ppermute | solution.py:17
  38.4 2.1 copy-start.5
  50.1 10.0 %slice-start.8 = ((s8[5308416]{0:T(1024)(128)(4,1)}), s8[4194304]{0:T(1024)(128)(4,1)S(1)}, s32[]{:S(2)}) async-start(s8[5308416]{0:T(1024)(128)(4,1)} %bitcast.234), calls=%async_computation.24 | async-start | bytes 8388608
  54.4 5.6 %slice-start.9 = ((s8[5308416]{0:T(1024)(128)(4,1)}), s8[1114112]{0:T(1024)(128)(4,1)S(1)}, s32[]{:S(2)}) async-start(s8[5308416]{0:T(1024)(128)(4,1)} %bitcast.234), calls=%async_computation.25 | async-start | bytes 2228224
  60.0 12.7 %slice-start.4 = ((s8[5308416]{0:T(1024)(128)(4,1)}), s8[4194304]{0:T(1024)(128)(4,1)S(1)}, s32[]{:S(2)}) async-start(s8[5308416]{0:T(1024)(128)(4,1)} %bitcast.230), calls=%async_computation.20 | async-start | bytes 8388608
  60.1 14.4 %slice-start = ((s8[5308416]{0:T(1024)(128)(4,1)}), s8[4194304]{0:T(1024)(128)(4,1)S(1)}, s32[]{:S(2)}) async-start(s8[5308416]{0:T(1024)(128)(4,1)} %bitcast.226), calls=%async_computation.16 | async-start | bytes 8388608
  67.2 5.5 %slice-start.5 = ((s8[5308416]{0:T(1024)(128)(4,1)}), s8[1114112]{0:T(1024)(128)(4,1)S(1)}, s32[]{:S(2)}) async-start(s8[5308416]{0:T(1024)(128)(4,1)} %bitcast.230), calls=%async_computation.21 | async-start | bytes 2228224
  67.2 7.2 %slice-start.1 = ((s8[5308416]{0:T(1024)(128)(4,1)}), s8[1114112]{0:T(1024)(128)(4,1)S(1)}, s32[]{:S(2)}) async-start(s8[5308416]{0:T(1024)(128)(4,1)} %bitcast.226), calls=%async_computation.17 | async-start | bytes 2228224
  74.5 7.2 %copy-start.6 = (bf16[2,8,2304]{2,1,0:T(8,128)(2,1)S(1)}, bf16[2,8,2304]{2,1,0:T(8,128)(2,1)}, u32[]{:S(2)}) copy-start(bf16[2,8,2304]{2,1,0:T(8,128)(2,1)} %param.17) | copy-start | bytes 221188
  74.5 45.3 %copy-start.1 = (bf16[1,2,8,2304]{3,2,1,0:T(8,128)(2,1)S(1)}, bf16[1,2,8,2304]{3,2,1,0:T(8,128)(2,1)}, u32[]{:S(2)}) copy-start(bf16[1,2,8,2304]{3,2,1,0:T(8,128)(2,1)} %param.19) | copy-start | bytes 221188
  74.5 45.3 %copy-start.2 = (bf16[1,2,8,2304]{3,2,1,0:T(8,128)(2,1)S(1)}, bf16[1,2,8,2304]{3,2,1,0:T(8,128)(2,1)}, u32[]{:S(2)}) copy-start(bf16[1,2,8,2304]{3,2,1,0:T(8,128)(2,1)} %param.20) | copy-start | bytes 221188
  76.7 43.0 %reduce-scatter.17.cloned.1.call-start = ((), (), s32[]{:S(2)}) async-start(), calls=%async_computation.12 | async-start | bytes 184320 | tf_op jit(solution)/shard_map/reduce_scatter | solution.py:155
  81.5 72.9 %slice-start.2 = ((s8[5308416]{0:T(1024)(128)(4,1)}), s8[1114112]{0:T(1024)(128)(4,1)S(1)}, s32[]{:S(2)}) async-start(s8[5308416]{0:T(1024)(128)(4,1)} %bitcast.228), calls=%async_computation.18 | async-start | bytes 2228224
  81.5 147.0 %reduce-scatter.23.cloned.1.call-start = ((), (), s32[]{:S(2)}) async-start(), calls=%async_computation.15 | async-start | bytes 184320 | tf_op jit(solution)/shard_map/reduce_scatter | solution.py:158
  138.5 15.9 %slice-start.3 = ((s8[5308416]{0:T(1024)(128)(4,1)}), s8[4194304]{0:T(1024)(128)(4,1)S(1)}, s32[]{:S(2)}) async-start(s8[5308416]{0:T(1024)(128)(4,1)} %bitcast.228), calls=%async_computation.19 | async-start | bytes 8388608
  138.5 26.6 %slice-start.12 = ((s8[5308416]{0:T(1024)(128)(4,1)}), s8[4194304]{0:T(1024)(128)(4,1)S(1)}, s32[]{:S(2)}) async-start(s8[5308416]{0:T(1024)(128)(4,1)} %bitcast.238), calls=%async_computation.28 | async-start | bytes 8388608
  142.2 22.9 %slice-start.13 = ((s8[5308416]{0:T(1024)(128)(4,1)}), s8[1114112]{0:T(1024)(128)(4,1)S(1)}, s32[]{:S(2)}) async-start(s8[5308416]{0:T(1024)(128)(4,1)} %bitcast.238), calls=%async_computation.29 | async-start | bytes 2228224
  146.0 25.5 %collective-permute-start.7 = (bf16[8,2304]{1,0:T(8,128)(2,1)S(1)}, bf16[8,2304]{1,0:T(8,128)(2,1)S(1)}, u32[]{:S(2)}, u32[]{:S(2)}) collective-permute-start(bf16[8,2304]{1,0:T(8,128)(2,1)S(1)} %get-tuple-element.25), channel_id=1, source_target_pairs={{4,0},{8,4},{12,8},{16,12},{20,16},{24,20},{28,24},{5,1},{9,5},{13... | collective-permute-start | bytes 110600 | tf_op jit(solution)/shard_map/ppermute | solution.py:17
  147.3 19.4 %slice-start.6 = ((s8[5308416]{0:T(1024)(128)(4,1)}), s8[4194304]{0:T(1024)(128)(4,1)S(1)}, s32[]{:S(2)}) async-start(s8[5308416]{0:T(1024)(128)(4,1)} %bitcast.232), calls=%async_computation.22 | async-start | bytes 8388608
  153.0 13.7 %slice-start.7 = ((s8[5308416]{0:T(1024)(128)(4,1)}), s8[1114112]{0:T(1024)(128)(4,1)S(1)}, s32[]{:S(2)}) async-start(s8[5308416]{0:T(1024)(128)(4,1)} %bitcast.232), calls=%async_computation.23 | async-start | bytes 2228224
  153.0 6.6 %collective-permute-start.5 = (bf16[8,2304]{1,0:T(8,128)(2,1)S(1)}, bf16[8,2304]{1,0:T(8,128)(2,1)S(1)}, u32[]{:S(2)}, u32[]{:S(2)}) collective-permute-start(bf16[8,2304]{1,0:T(8,128)(2,1)S(1)} %get-tuple-element.26), channel_id=1, source_target_pairs={{4,0},{8,4},{12,8},{16,12},{20,16},{24,20},{28,24},{5,1},{9,5},{13... | collective-permute-start | bytes 110600 | tf_op jit(solution)/shard_map/ppermute | solution.py:17
  166.7 3.3 slice-start.10
  168.4 1.6 slice-start.11
  201.6 42.3 %reduce-scatter.19.cloned.1.call-start = ((), (), s32[]{:S(2)}) async-start(), calls=%async_computation.13 | async-start | bytes 184320 | tf_op jit(solution)/shard_map/reduce_scatter | solution.py:155
  217.5 73.3 %reduce-scatter.13.cloned.1.call-start = ((), (), s32[]{:S(2)}) async-start(), calls=%async_computation.10 | async-start | bytes 184320 | tf_op jit(solution)/shard_map/reduce_scatter | solution.py:150
  244.9 12.9 %slice-start.14 = ((s8[5308416]{0:T(1024)(128)(4,1)}), s8[4194304]{0:T(1024)(128)(4,1)S(1)}, s32[]{:S(2)}) async-start(s8[5308416]{0:T(1024)(128)(4,1)} %bitcast.240), calls=%async_computation.30 | async-start | bytes 8388608
  250.7 7.1 %slice-start.15 = ((s8[5308416]{0:T(1024)(128)(4,1)}), s8[1114112]{0:T(1024)(128)(4,1)S(1)}, s32[]{:S(2)}) async-start(s8[5308416]{0:T(1024)(128)(4,1)} %bitcast.240), calls=%async_computation.31 | async-start | bytes 2228224
  270.9 47.8 %copy-start.3 = (bf16[8,2304]{1,0:T(8,128)(2,1)S(1)}, bf16[8,2304]{1,0:T(8,128)(2,1)}, u32[]{:S(2)}) copy-start(bf16[8,2304]{1,0:T(8,128)(2,1)} %reduce-scatter.23.cloned.1.call-done) | copy-start | bytes 110596
  270.9 47.8 %copy-start.4 = (bf16[8,2304]{1,0:T(8,128)(2,1)S(1)}, bf16[8,2304]{1,0:T(8,128)(2,1)}, u32[]{:S(2)}) copy-start(bf16[8,2304]{1,0:T(8,128)(2,1)} %reduce-scatter.19.cloned.1.call-done) | copy-start | bytes 110596
  270.9 41.8 %reduce-scatter.9.cloned.1.call-start = ((), (), s32[]{:S(2)}) async-start(), calls=%async_computation.8 | async-start | bytes 184320 | tf_op jit(solution)/shard_map/reduce_scatter | solution.py:147
  275.0 90.9 %reduce-scatter.15.cloned.1.call-start = ((), (), s32[]{:S(2)}) async-start(), calls=%async_computation.11 | async-start | bytes 184320 | tf_op jit(solution)/shard_map/reduce_scatter | solution.py:150
  291.5 25.4 %collective-permute-start.3 = (bf16[8,2304]{1,0:T(8,128)(2,1)S(1)}, bf16[8,2304]{1,0:T(8,128)(2,1)S(1)}, u32[]{:S(2)}, u32[]{:S(2)}) collective-permute-start(bf16[8,2304]{1,0:T(8,128)(2,1)S(1)} %fusion.213), channel_id=1, source_target_pairs={{0,4},{4,8},{8,12},{12,16},{16,20},{20,24},{24,28},{1,5},{5,9},{9,... | collective-permute-start | bytes 110600 | tf_op jit(solution)/shard_map/ppermute | solution.py:17
  313.5 5.0 %collective-permute-start.1 = (bf16[8,2304]{1,0:T(8,128)(2,1)S(1)}, bf16[8,2304]{1,0:T(8,128)(2,1)S(1)}, u32[]{:S(2)}, u32[]{:S(2)}) collective-permute-start(bf16[8,2304]{1,0:T(8,128)(2,1)S(1)} %fusion.235), channel_id=1, source_target_pairs={{0,4},{4,8},{8,12},{12,16},{16,20},{20,24},{24,28},{1,5},{5,9},{9,... | collective-permute-start | bytes 110600 | tf_op jit(solution)/shard_map/ppermute | solution.py:17
  319.5 12.7 %slice-start.16 = ((s8[5308416]{0:T(1024)(128)(4,1)}), s8[4194304]{0:T(1024)(128)(4,1)S(1)}, s32[]{:S(2)}) async-start(s8[5308416]{0:T(1024)(128)(4,1)} %bitcast.242), calls=%async_computation.32 | async-start | bytes 8388608
  325.1 7.1 %slice-start.17 = ((s8[5308416]{0:T(1024)(128)(4,1)}), s8[1114112]{0:T(1024)(128)(4,1)S(1)}, s32[]{:S(2)}) async-start(s8[5308416]{0:T(1024)(128)(4,1)} %bitcast.242), calls=%async_computation.33 | async-start | bytes 2228224
  345.2 42.8 %reduce-scatter.11.cloned.1.call-start = ((), (), s32[]{:S(2)}) async-start(), calls=%async_computation.9 | async-start | bytes 184320 | tf_op jit(solution)/shard_map/reduce_scatter | solution.py:147
Sparse Core Ops, SparseCore 0:
  76.9 20.0 reduce-scatter.20
  100.0 19.6 reduce-scatter.16
  201.7 20.1 reduce-scatter.22
  224.2 19.6 reduce-scatter.18
  271.0 19.6 reduce-scatter.12
  293.0 19.6 reduce-scatter.8
  345.4 20.5 reduce-scatter.14
  368.4 19.6 reduce-scatter.10
where the time goes:
time: 400 us; the launch traced here: 397 us
  matrix products  139 us (35%)
  waiting for transfers between devices  130 us (32%)
  blocking collectives  77.8 us (19%)
  starting transfers between devices  23.7 us (6%)
  between operations  15.1 us (4%)
  other arithmetic  11.1 us (3%)
    dot_general x8, matrix products, product_first(): lax.dot_general(left, right, (((0,), (0,)), ((), ())), preferred_element_...  55.4 us
    dot_general x16, matrix products, matrix_product(): return jnp.dot(left, right, preferred_element_type=jnp.float32)  51.3 us
    reduce_scatter x2, waiting for transfers between devices, reduce_rows(): lax.psum_scatter(forward_term.astype(jnp.bfloat16), 'dp', scatter_dimensi...  38.6 us
    reduce_scatter x2, waiting for transfers between devices, reduce_rows(): lax.psum_scatter(backward_term.astype(jnp.bfloat16), 'dp', scatter_dimens...  38.1 us
    reduce_scatter x2, waiting for transfers between devices, reduce_rows(): lax.psum_scatter(forward_tan.astype(jnp.bfloat16), 'dp', scatter_dimensio...  32.3 us
    dot_general x12, matrix products, product_last(): lax.dot_general(left, right, (((1,), (1,)), ((), ())), preferred_element_...  32.1 us
    ppermute x8, starting transfers between devices, passed_along(): lax.ppermute(value, axis, [(source, source + steps) for source in range(l...  23.4 us
    all_gather x2, blocking collectives, gather_rows(): lax.all_gather(stash_rows, 'dp', axis=0, tiled=True)  22.4 us
  transfers between devices with their start and end apart: 16, of which 9 were waited for; matrix products, arithmetic and copies ran while one was open for 21% of the time, Pallas kernels for 0%

commit v1 on v0

v1 whole, which is shorter than its diff:
```python
import jax
import jax.numpy as jnp
from jax import lax
from jax.experimental import pallas as pl
from jax.experimental.pallas import tpu as pltpu
from jax.sharding import PartitionSpec as P

TICKS = 2


sqrt_two_over_pi = 0.7978845608028654
cubic_coef = 0.044715
norm_eps = 1e-06

bf16 = jnp.bfloat16
f32 = jnp.float32
VM = pl.BlockSpec(memory_space=pltpu.VMEM)


def params(mib):
    return pltpu.CompilerParams(vmem_limit_bytes=mib * 2**20)


def passed_along(value, axis, steps):
    count = lax.axis_size(axis)
    leading, last = (max(0, -steps), min(count, count - steps))
    return lax.ppermute(value, axis, [(source, source + steps) for source in range(leading, last)])


def swapped(value, bit):
    count = lax.axis_size("dp")
    return lax.ppermute(value, "dp", [(source, source ^ bit) for source in range(count)])


def dp_bits():
    count = lax.axis_size("dp")
    bits = []
    bit = count // 2
    while bit:
        bits.append(bit)
        bit //= 2
    return bits


def gather_blocks(block):
    blocks = [block]
    for bit in dp_bits():
        blocks = blocks + [swapped(b, bit) for b in blocks]
    return blocks


def gelu_parts(linear):
    inner_arg = sqrt_two_over_pi * (linear + cubic_coef * linear * linear * linear)
    first_slope = sqrt_two_over_pi * (1.0 + 3.0 * cubic_coef * linear * linear)
    second_slope = 6.0 * sqrt_two_over_pi * cubic_coef * linear
    tanh_value = jnp.tanh(inner_arg)
    sech_square = 1.0 - tanh_value * tanh_value
    gelu_value = 0.5 * linear * (1.0 + tanh_value)
    gelu_first = 0.5 * (1.0 + tanh_value) + 0.5 * linear * sech_square * first_slope
    gelu_second = sech_square * (
        first_slope - linear * tanh_value * first_slope * first_slope + 0.5 * linear * second_slope
    )
    return (gelu_value, gelu_first, gelu_second)


def matrix_product(left, right):
    return jnp.dot(left, right, preferred_element_type=f32)


def product_last(left, right):
    return lax.dot_general(left, right, (((1,), (1,)), ((), ())), preferred_element_type=f32)


def product_first(left, right):
    return lax.dot_general(left, right, (((0,), (0,)), ((), ())), preferred_element_type=f32)


def norm_stats(values, values_tan):
    inverse = lax.rsqrt(jnp.mean(values * values, axis=-1, keepdims=True) + norm_eps)
    inverse_tan = -(inverse * inverse * inverse) * jnp.mean(
        values * values_tan, axis=-1, keepdims=True
    )
    return (inverse, inverse_tan)


def norm_rows(values, values_tan, gain_wide):
    inverse, inverse_tan = norm_stats(values, values_tan)
    normed = values * inverse * gain_wide
    normed_tan = (values_tan * inverse + values * inverse_tan) * gain_wide
    return (normed, normed_tan)


def pick(blocks, index, rows):
    return jnp.concatenate(
        [b[index * rows : (index + 1) * rows, :].astype(f32) for b in blocks], axis=0
    )


def stash_kernel(count, rows):
    def body(*refs):
        blocks = refs[:count]
        gain_ref, up_ref, dup_ref = refs[count : count + 3]
        m_ref, q_ref, slope_ref, bend_ref = refs[count + 3 :]
        gain_wide = gain_ref[...].astype(f32)
        tokens = count * rows
        for tick in range(TICKS):
            normed, normed_tan = norm_rows(
                pick(blocks, 2 * tick, rows), pick(blocks, 2 * tick + 1, rows), gain_wide
            )
            base = 2 * tick * tokens
            m_ref[base : base + tokens, :] = normed_tan.astype(bf16)
            m_ref[base + tokens : base + 2 * tokens, :] = normed.astype(bf16)
        both = matrix_product(m_ref[...], up_ref[...])
        plain = jnp.concatenate(
            [m_ref[(2 * t + 1) * tokens : (2 * t + 2) * tokens, :] for t in range(TICKS)], axis=0
        )
        side = matrix_product(plain, dup_ref[...])
        for tick in range(TICKS):
            base = 2 * tick * tokens
            linear = both[base + tokens : base + 2 * tokens]
            linear_tan = both[base : base + tokens] + side[tick * tokens : (tick + 1) * tokens]
            value, first, second = gelu_parts(linear)
            q_ref[base : base + tokens, :] = (first * linear_tan).astype(bf16)
            q_ref[base + tokens : base + 2 * tokens, :] = value.astype(bf16)
            slope_ref[tick * tokens : (tick + 1) * tokens, :] = first
            bend_ref[tick * tokens : (tick + 1) * tokens, :] = second * linear_tan

    return body


def tick_kernel(count, rows, tick):
    tokens = count * rows
    half = count // 2

    def body(*refs):
        blocks = refs[:count]
        gain_ref, up_ref, down_ref, dup_ref, ddown_ref, slope_ref, bend_ref = refs[
            count : count + 7
        ]
        keep_ref, send_ref, z_ref, adj_ref = refs[count + 7 :]
        gain_wide = gain_ref[...].astype(f32)
        normed, normed_tan = norm_rows(pick(blocks, 0, rows), pick(blocks, 1, rows), gain_wide)
        pair = jnp.concatenate([normed, normed_tan], axis=0).astype(bf16)
        both = matrix_product(pair, up_ref[...])
        linear = both[:tokens]
        linear_tan = both[tokens:] + matrix_product(pair[:tokens], dup_ref[...])
        value, first, _ = gelu_parts(linear)
        hidden = jnp.concatenate([value, first * linear_tan], axis=0).astype(bf16)
        p_both = matrix_product(hidden, down_ref[...])
        p_tan = p_both[tokens:] + matrix_product(hidden[:tokens], ddown_ref[...])
        adj = jnp.concatenate([pick(blocks, 2, rows), pick(blocks, 3, rows)], axis=0).astype(bf16)
        adj_ref[...] = adj
        e_both = product_last(adj, down_ref[...])
        e_tan = e_both[tokens:] + product_last(adj[:tokens], ddown_ref[...])
        upstream = e_both[:tokens]
        span = slice(tick * tokens, (tick + 1) * tokens)
        slope = slope_ref[span, :]
        z_pair = jnp.concatenate(
            [upstream * slope, e_tan * slope + upstream * bend_ref[span, :]], axis=0
        ).astype(bf16)
        z_ref[...] = z_pair
        t_both = product_last(z_pair, up_ref[...])
        t_tan = t_both[tokens:] + product_last(z_pair[:tokens], dup_ref[...])
        parts = (p_both[:tokens], p_tan, t_both[:tokens], t_tan)
        for k in range(count):
            for a in range(4):
                piece = parts[a][k * rows : (k + 1) * rows]
                if k < half:
                    at = (4 * k + a) * rows
                    keep_ref[at : at + rows, :] = piece
                else:
                    at = (4 * (k - half) + a) * rows
                    send_ref[at : at + rows, :] = piece.astype(bf16)

    return body


def add_body(keep_ref, got_ref, low_ref, high_ref):
    half = keep_ref.shape[0] // 2
    low_ref[...] = keep_ref[:half, :] + got_ref[:half, :].astype(f32)
    high_ref[...] = (keep_ref[half:, :] + got_ref[half:, :].astype(f32)).astype(bf16)


def finish_kernel(rows):
    def body(keep_ref, got_ref, own_ref, stash_ref, stash_tan_ref, gain_ref, fwd_ref, bwd_ref):
        total = keep_ref[...] + got_ref[...].astype(f32)
        own = own_ref[...].astype(f32)
        values = stash_ref[...].astype(f32)
        values_tan = stash_tan_ref[...].astype(f32)
        gain_wide = gain_ref[...].astype(f32)
        fwd_ref[...] = (own[: 2 * rows] + total[: 2 * rows]).astype(bf16)
        inverse, inverse_tan = norm_stats(values, values_tan)
        weighted = total[2 * rows : 3 * rows] * gain_wide
        weighted_tan = total[3 * rows :] * gain_wide
        moment = jnp.mean(values * weighted, axis=-1, keepdims=True)
        moment_tan = jnp.mean(
            values_tan * weighted + values * weighted_tan, axis=-1, keepdims=True
        )
        inverse_cube = inverse * inverse * inverse
        returned = own[2 * rows : 3 * rows] + inverse * weighted - inverse_cube * values * moment
        returned_tan = (
            own[3 * rows :]
            + inverse_tan * weighted
            + inverse * weighted_tan
            - 3.0 * inverse * inverse * inverse_tan * values * moment
            - inverse_cube * values_tan * moment
            - inverse_cube * values * moment_tan
        )
        bwd_ref[:rows, :] = returned.astype(bf16)
        bwd_ref[rows:, :] = returned_tan.astype(bf16)

    return body


def curvature_body(m_ref, z_refs, q_ref, adj_refs, up_ref, down_ref):
    z_all = jnp.concatenate([r[...] for r in z_refs], axis=0)
    adj_all = jnp.concatenate([r[...] for r in adj_refs], axis=0)
    up_ref[...] = product_first(m_ref[...], z_all).astype(bf16)
    down_ref[...] = product_first(q_ref[...], adj_all).astype(bf16)


def call(body, outs, mib, *operands):
    return pl.pallas_call(
        body,
        in_specs=[VM] * len(operands),
        out_specs=[VM] * len(outs),
        out_shape=[jax.ShapeDtypeStruct(s, d) for s, d in outs],
        compiler_params=params(mib),
    )(*operands)


def shards(
    carry_act,
    carry_act_tan,
    carry_adj,
    carry_adj_tan,
    fresh_act,
    loss_cot,
    stash_act,
    stash_act_tan,
    norm_gain,
    up_weight,
    down_weight,
    up_dir,
    down_dir,
):
    section_index = lax.axis_index("section")
    section_count = lax.axis_size("section")
    count = lax.axis_size("dp")
    at_first = section_index == 0
    at_last = section_index == section_count - 1
    up_local = up_weight[0]
    down_local = down_weight[0]
    up_direction = up_dir[0]
    down_direction = down_dir[0]
    rows, width = carry_act.shape[1:]
    hidden = up_local.shape[1]
    tokens = count * rows

    def arrival(moved_forward, moved_backward, tick):
        zero_rows = jnp.zeros((rows, width), bf16)
        edge = (
            (at_first, fresh_act[tick], moved_forward[:rows]),
            (at_first, zero_rows, moved_forward[rows:]),
            (at_last, loss_cot[tick], moved_backward[:rows]),
            (at_last, zero_rows, moved_backward[rows:]),
        )
        return jnp.concatenate([jnp.where(*e) for e in edge], axis=0)

    forward = jnp.concatenate([carry_act[0], carry_act_tan[0]], axis=0)
    backward = jnp.concatenate([carry_adj[0], carry_adj_tan[0]], axis=0)
    moved_forward = passed_along(forward, "section", 1)
    moved_backward = passed_along(backward, "section", -1)

    stash_own = jnp.concatenate(
        [x for t in range(TICKS) for x in (stash_act[0, t], stash_act_tan[0, t])], axis=0
    )
    stash_blocks = gather_blocks(stash_own)
    pairs = 2 * TICKS * tokens
    m_all, q_all, slope, bend = call(
        stash_kernel(count, rows),
        [
            ((pairs, width), bf16),
            ((pairs, hidden), bf16),
            ((TICKS * tokens, hidden), f32),
            ((TICKS * tokens, hidden), f32),
        ],
        16,
        *stash_blocks,
        norm_gain,
        up_local,
        up_direction,
    )
    z_list, adj_list = [], []
    for tick in range(TICKS):
        own = arrival(moved_forward, moved_backward, tick)
        blocks = gather_blocks(own)
        half = count // 2
        keep, send, z_pair, adj = call(
            tick_kernel(count, rows, tick),
            [
                ((half * 4 * rows, width), f32),
                ((half * 4 * rows, width), bf16),
                ((2 * tokens, hidden), bf16),
                ((2 * tokens, width), bf16),
            ],
            16,
            *blocks,
            norm_gain,
            up_local,
            down_local,
            up_direction,
            down_direction,
            slope,
            bend,
        )
        z_list.append(z_pair)
        adj_list.append(adj)
        bits = dp_bits()[::-1]
        for bit in bits[:-1]:
            got = swapped(send, bit)
            part = keep.shape[0] // 2
            keep, send = call(
                add_body, [((part, width), f32), ((part, width), bf16)], 8, keep, got
            )
        got = swapped(send, bits[-1])
        forward, backward = call(
            finish_kernel(rows),
            [((2 * rows, width), bf16), ((2 * rows, width), bf16)],
            8,
            keep,
            got,
            own,
            stash_act[0, tick],
            stash_act_tan[0, tick],
            norm_gain,
        )
        if tick + 1 < TICKS:
            moved_forward = passed_along(forward, "section", 1)
            moved_backward = passed_along(backward, "section", -1)

    def curvature(m_ref, *refs):
        curvature_body(
            m_ref, refs[:TICKS], refs[TICKS], refs[TICKS + 1 : 2 * TICKS + 1], *refs[2 * TICKS + 1 :]
        )

    steps = next(
        n for n in range(width // 256, 0, -1)
        if n == 1 or (width % (128 * n) == 0 and hidden % (128 * n) == 0)
    )
    lead = hidden // steps
    whole = lambda shape: pl.BlockSpec(shape, lambda i: (0, 0))
    total_up, total_down = pl.pallas_call(
        curvature,
        grid=(steps,),
        in_specs=[pl.BlockSpec((pairs, width // steps), lambda i: (0, i))]
        + [whole(z.shape) for z in z_list]
        + [pl.BlockSpec((pairs, lead), lambda i: (0, i))]
        + [whole(a.shape) for a in adj_list],
        out_specs=[
            pl.BlockSpec((width // steps, hidden), lambda i: (i, 0)),
            pl.BlockSpec((lead, width), lambda i: (i, 0)),
        ],
        out_shape=[
            jax.ShapeDtypeStruct((width, hidden), bf16),
            jax.ShapeDtypeStruct((hidden, width), bf16),
        ],
        compiler_params=params(24),
    )(m_all, *z_list, q_all, *adj_list)
    return (
        forward[:rows][None],
        forward[rows:][None],
        backward[:rows][None],
        backward[rows:][None],
        total_up[None],
        total_down[None],
    )


def solution(mesh):
    in_specs = (
        P("section", "dp", None),
        P("section", "dp", None),
        P("section", "dp", None),
        P("section", "dp", None),
        P(None, "dp", None),
        P(None, "dp", None),
        P("section", None, "dp", None),
        P("section", None, "dp", None),
        P("section", None),
        P("section", None, "dp"),
        P("section", "dp", None),
        P("section", None, "dp"),
        P("section", "dp", None),
    )
    out_specs = (
        P("section", "dp", None),
        P("section", "dp", None),
        P("section", "dp", None),
        P("section", "dp", None),
        P("section", None, "dp"),
        P("section", "dp", None),
    )
    return jax.shard_map(shards, mesh=mesh, in_specs=in_specs, out_specs=out_specs, check_vma=False)
```

time: 400 us -> 90.7 us (0.23)
  matrix products: 139 us -> 0 us
  waiting for transfers between devices: 130 us -> 21.4 us
  blocking collectives: 77.8 us -> 0 us
  Pallas kernels: 0 us -> 28.9 us
  local copies, waits for them, and re-layouts: 0.14 us -> 14.8 us
  between operations: 15.1 us -> 0.77 us
  other arithmetic: 11.1 us -> 3.22 us
    dot_general x36 -> x0, matrix products: 139 us -> none  [the longest x8 55.4 us: product_first(): lax.dot_general(left, right, (((0,), (0,)), ((), ())), preferred_element_...]
    reduce_scatter x8 -> x0, waiting for transfers between devices: 124 us -> none  [the longest x2 38.6 us: reduce_rows(): lax.psum_scatter(forward_term.astype(jnp.bfloat16), 'dp', scatter_dimensi...]
    all_gather x12 -> x0, blocking collectives: 77.8 us -> none  [the longest x2 22.4 us: gather_rows(): lax.all_gather(stash_rows, 'dp', axis=0, tiled=True)]
    pallas_call x0 -> x8, Pallas kernels: none -> 28.9 us  [the longest x7 22.1 us: call(): pl.pallas_call(body, in_specs=[VM] * len(operands), out_specs=[VM] * len(...]
    ppermute x0 -> x13, waiting for transfers between devices: none -> 16.7 us  [swapped(): lax.ppermute(value, 'dp', [(source, source ^ bit) for source in range(cou...]
    unnamed x50 -> x22, local copies, waits for them, and re-layouts: 0.14 us -> 12.7 us
    ppermute x8 -> x4, starting transfers between devices: 23.4 us -> 12.5 us  [passed_along(): lax.ppermute(value, axis, [(source, source + steps) for source in range(l...]
    ppermute x0 -> x13, starting transfers between devices: none -> 8.35 us  [swapped(): lax.ppermute(value, 'dp', [(source, source ^ bit) for source in range(cou...]
  transfers between devices with their start and end apart: 16 -> 17, of which waited for: 9 -> 9; matrix products, arithmetic and copies ran while one was open for 21% -> 4% of each run, Pallas kernels for 0% -> 10%
where the time goes in v1:
time: 90.7 us; the launch traced here: 90 us
  Pallas kernels  28.9 us (32%)
  waiting for transfers between devices  21.4 us (24%)
  starting transfers between devices  20.9 us (23%)
  local copies, waits for them, and re-layouts  14.8 us (16%)
  other arithmetic  3.22 us (4%)
    pallas_call x7, Pallas kernels, call(): pl.pallas_call(body, in_specs=[VM] * len(operands), out_specs=[VM] * len(...  22.1 us
    ppermute x13, waiting for transfers between devices, swapped(): lax.ppermute(value, 'dp', [(source, source ^ bit) for source in range(cou...  16.7 us
    unnamed x22, local copies, waits for them, and re-layouts  12.7 us
    ppermute x4, starting transfers between devices, passed_along(): lax.ppermute(value, axis, [(source, source + steps) for source in range(l...  12.5 us
    ppermute x13, starting transfers between devices, swapped(): lax.ppermute(value, 'dp', [(source, source ^ bit) for source in range(cou...  8.35 us
    pallas_call x1, Pallas kernels, shards(): pl.pallas_call(curvature, grid=(steps,), in_specs=[pl.BlockSpec((pairs, w...  6.87 us
    ppermute x4, waiting for transfers between devices, passed_along(): lax.ppermute(value, axis, [(source, source + steps) for source in range(l...  4.75 us
  transfers between devices with their start and end apart: 17, of which 9 were waited for; matrix products, arithmetic and copies ran while one was open for 4% of the time, Pallas kernels for 10%

profile of v1, /device:TPU:0, one launch (start us, length us, event | category | flops | bytes accessed | tf_op | source)
XLA Modules:
  0.0 90.0 jit_solution(13910339955483335638)
XLA Ops:
  0.6 0.8 pad_maximum_fusion.4
  1.4 1.3 %collective-permute-start.1 = (bf16[16,2304]{1,0:T(8,128)(2,1)S(1)}, bf16[16,2304]{1,0:T(8,128)(2,1)S(1)}, u32[]{:S(2)}, u32[]{:S(2)}) collective-permute-start(bf16[16,2304]{1,0:T(8,128)(2,1)S(1)} %pad_maximum_fusion.4), channel_id=1, source_target_pairs={{4,0},{8,4},{12,8},{16,12},{20,16},{24,20},{28,24},{5,1},{9,5},{13... | collective-permute-start | bytes 221192 | tf_op jit(solution)/shard_map/ppermute | solution.py:27
  2.7 0.8 pad_maximum_fusion.3
  3.5 5.5 %collective-permute-start = (bf16[16,2304]{1,0:T(8,128)(2,1)S(1)}, bf16[16,2304]{1,0:T(8,128)(2,1)S(1)}, u32[]{:S(2)}, u32[]{:S(2)}) collective-permute-start(bf16[16,2304]{1,0:T(8,128)(2,1)S(1)} %pad_maximum_fusion.3), channel_id=1, source_target_pairs={{0,4},{4,8},{8,12},{12,16},{16,20},{20,24},{24,28},{1,5},{5,9},{9,... | collective-permute-start | bytes 221192 | tf_op jit(solution)/shard_map/ppermute | solution.py:27
  9.0 0.8 slice_bitcast_fusion.6
  9.9 2.1 %collective-permute-start.5 = (bf16[32,2304]{1,0:T(8,128)(2,1)S(1)}, bf16[32,2304]{1,0:T(8,128)(2,1)S(1)}, u32[]{:S(2)}, u32[]{:S(2)}) collective-permute-start(bf16[32,2304]{1,0:T(8,128)(2,1)S(1)} %pad_maximum_fusion.1.refs_0_), channel_id=1, source_target_pairs={{0,2},{1,3},{2,0},{3,1},{4,6},{5,7},{6,4},{7,5},{8,10},{9,11},{10,... | collective-permute-start | bytes 442376 | tf_op jit(solution)/shard_map/ppermute | solution.py:32
  12.0 0.0 collective-permute-done.1
  12.0 0.8 slice_select_fusion.5
  12.8 0.0 collective-permute-done
  12.8 0.8 slice_select_fusion.7
  13.6 0.3 collective-permute-start.2
  13.9 0.0 collective-permute-start.6
  13.9 2.3 %collective-permute-done.5.refs_1_ = bf16[32,2304]{1,0:T(8,128)(2,1)S(1)} collective-permute-done((bf16[32,2304]{1,0:T(8,128)(2,1)S(1)}, bf16[32,2304]{1,0:T(8,128)(2,1)S(1)}, u32[]{:S(2)}, u32[]{:S(2)}) %collective-permute-start.5) | collective-permute-done | bytes 147488 | tf_op jit(solution)/shard_map/ppermute | solution.py:32
  16.2 0.0 collective-permute-start.7
  16.2 0.5 collective-permute-start.3
  16.7 2.0 %collective-permute-done.2.refs_1_ = bf16[32,2304]{1,0:T(8,128)(2,1)S(1)} collective-permute-done((bf16[32,2304]{1,0:T(8,128)(2,1)S(1)}, bf16[32,2304]{1,0:T(8,128)(2,1)S(1)}, u32[]{:S(2)}, u32[]{:S(2)}) %collective-permute-start.2) | collective-permute-done | bytes 147488 | tf_op jit(solution)/shard_map/ppermute | solution.py:32
  18.8 0.0 collective-permute-start.4
  18.8 0.0 collective-permute-done.6.refs_2_
  18.8 0.0 collective-permute-done.7.refs_3_
  18.8 0.0 copy-start
  18.8 2.5 %copy-done = bf16[1,2304,1152]{2,1,0:T(8,128)(2,1)S(1)} copy-done((bf16[1,2304,1152]{2,1,0:T(8,128)(2,1)S(1)}, bf16[1,2304,1152]{2,1,0:T(8,128)(2,1)}, u32[]{:S(2)}) %copy-start) | copy-done | bytes 5308440
  21.3 0.0 copy-start.2
  21.3 2.5 %copy-done.2 = bf16[1,2304,1152]{2,1,0:T(8,128)(2,1)S(1)} copy-done((bf16[1,2304,1152]{2,1,0:T(8,128)(2,1)S(1)}, bf16[1,2304,1152]{2,1,0:T(8,128)(2,1)}, u32[]{:S(2)}) %copy-start.2) | copy-done | bytes 5308440
  23.8 0.0 copy-start.7
  23.8 0.7 copy-done.7
  24.5 0.0 copy-start.1
  24.5 2.1 %shard_map.172 = (bf16[128,2304]{1,0:T(8,128)(2,1)S(1)}, bf16[128,1152]{1,0:T(8,128)(2,1)S(1)}, f32[64,1152]{1,0:T(8,128)S(1)}, f32[64,1152]{1,0:T(8,128)S(1)}) custom-call(bf16[32,2304]{1,0:T(8,128)(2,1)S(1)} %pad_maximum_fusion.1.refs_0_, bf16[32,2304]{1,0:T(8,128)(2,1)S(1)} %collective-permute-done.5.refs_1_, ...), custom_call_target="tpu_custom_call" | custom-call | tf_op jit(solution)/shard_map/pallas_call | solution.py:223
  26.6 0.0 collective-permute-done.3.refs_2_
  26.6 0.0 collective-permute-done.4.refs_3_
  26.7 0.3 copy-done.1
  27.0 1.6 %copy-done.3 = bf16[1,2304,1152]{2,1,0:T(8,128)(2,1)S(1)} copy-done((bf16[1,2304,1152]{2,1,0:T(8,128)(2,1)S(1)}, bf16[1,2304,1152]{2,1,0:T(8,128)(2,1)}, u32[]{:S(2)}) %copy-start.3) | copy-done | bytes 5308440
  28.6 0.0 copy-done.8
  28.6 2.5 %copy-done.4 = bf16[1,1152,2304]{2,1,0:T(8,128)(2,1)S(1)} copy-done((bf16[1,1152,2304]{2,1,0:T(8,128)(2,1)S(1)}, bf16[1,1152,2304]{2,1,0:T(8,128)(2,1)}, u32[]{:S(2)}) %copy-start.4) | copy-done | bytes 5308440
  31.1 2.5 %copy-done.6 = bf16[1,1152,2304]{2,1,0:T(8,128)(2,1)S(1)} copy-done((bf16[1,1152,2304]{2,1,0:T(8,128)(2,1)S(1)}, bf16[1,1152,2304]{2,1,0:T(8,128)(2,1)}, u32[]{:S(2)}) %copy-start.6) | copy-done | bytes 5308440
  33.6 9.7 %shard_map.173 = (f32[64,2304]{1,0:T(8,128)S(1)}, bf16[64,2304]{1,0:T(8,128)(2,1)S(1)}, bf16[64,1152]{1,0:T(8,128)(2,1)S(1)}, bf16[64,2304]{1,0:T(8,128)(2,1)S(1)}) custom-call(bf16[32,2304]{1,0:T(8,128)(2,1)S(1)} %pad_maximum_fusion.refs_0_.own_ref, bf16[32,2304]{1,0:T(8,128)(2,1)S(1)} %collective-permute-done.2.refs_1_, ...), custom_call_target="tpu_custom_call" | custom-call | tf_op jit(solution)/shard_map/pallas_call | solution.py:223
  43.3 0.5 collective-permute-start.8
  43.9 1.2 %collective-permute-done.8.got_ref = bf16[64,2304]{1,0:T(8,128)(2,1)S(1)} collective-permute-done((bf16[64,2304]{1,0:T(8,128)(2,1)S(1)}, bf16[64,2304]{1,0:T(8,128)(2,1)S(1)}, u32[]{:S(2)}, u32[]{:S(2)}) %collective-permute-start.8) | collective-permute-done | bytes 294944 | tf_op jit(solution)/shard_map/ppermute | solution.py:32
  45.1 0.1 shard_map.174
  45.2 1.6 %collective-permute-start.9 = (bf16[32,2304]{1,0:T(8,128)(2,1)S(1)}, bf16[32,2304]{1,0:T(8,128)(2,1)S(1)}, u32[]{:S(2)}, u32[]{:S(2)}) collective-permute-start(bf16[32,2304]{1,0:T(8,128)(2,1)S(1)} %get-tuple-element.33), channel_id=1, source_target_pairs={{0,2},{1,3},{2,0},{3,1},{4,6},{5,7},{6,4},{7,5},{8,10},{9,11},{10,... | collective-permute-start | bytes 442376 | tf_op jit(solution)/shard_map/ppermute | solution.py:32
  46.7 4.6 %collective-permute-done.9.got_ref = bf16[32,2304]{1,0:T(8,128)(2,1)S(1)} collective-permute-done((bf16[32,2304]{1,0:T(8,128)(2,1)S(1)}, bf16[32,2304]{1,0:T(8,128)(2,1)S(1)}, u32[]{:S(2)}, u32[]{:S(2)}) %collective-permute-start.9) | collective-permute-done | bytes 147488 | tf_op jit(solution)/shard_map/ppermute | solution.py:32
  51.3 0.2 shard_map.175
  51.5 4.3 %collective-permute-start.10 = (bf16[16,2304]{1,0:T(8,128)(2,1)S(1)}, bf16[16,2304]{1,0:T(8,128)(2,1)S(1)}, u32[]{:S(2)}, u32[]{:S(2)}) collective-permute-start(bf16[16,2304]{1,0:T(8,128)(2,1)S(1)} %get-tuple-element.34), channel_id=1, source_target_pairs={{0,4},{4,8},{8,12},{12,16},{16,20},{20,24},{24,28},{1,5},{5,9},{9,... | collective-permute-start | bytes 221192 | tf_op jit(solution)/shard_map/ppermute | solution.py:27
  55.8 1.5 %collective-permute-start.11 = (bf16[16,2304]{1,0:T(8,128)(2,1)S(1)}, bf16[16,2304]{1,0:T(8,128)(2,1)S(1)}, u32[]{:S(2)}, u32[]{:S(2)}) collective-permute-start(bf16[16,2304]{1,0:T(8,128)(2,1)S(1)} %get-tuple-element.35), channel_id=1, source_target_pairs={{4,0},{8,4},{12,8},{16,12},{20,16},{24,20},{28,24},{5,1},{9,5},{13... | collective-permute-start | bytes 221192 | tf_op jit(solution)/shard_map/ppermute | solution.py:27
  57.3 0.5 collective-permute-done.10
  57.8 0.0 copy-done.9
  57.8 4.3 %collective-permute-done.11 = bf16[16,2304]{1,0:T(8,128)(2,1)S(1)} collective-permute-done((bf16[16,2304]{1,0:T(8,128)(2,1)S(1)}, bf16[16,2304]{1,0:T(8,128)(2,1)S(1)}, u32[]{:S(2)}, u32[]{:S(2)}) %collective-permute-start.11) | collective-permute-done | bytes 73760 | tf_op jit(solution)/shard_map/ppermute | solution.py:27
  62.1 0.0 copy-done.10
  62.1 1.6 %collective-permute-start.12 = (bf16[32,2304]{1,0:T(8,128)(2,1)S(1)}, bf16[32,2304]{1,0:T(8,128)(2,1)S(1)}, u32[]{:S(2)}, u32[]{:S(2)}) collective-permute-start(bf16[32,2304]{1,0:T(8,128)(2,1)S(1)} %pad_maximum_fusion.2.refs_0_.own_ref), channel_id=1, source_target_pairs={{0,2},{1,3},{2,0},{3,1},{4,6},{5,7},{6,4},{7,5},{8,10},{9,11},{10,... | collective-permute-start | bytes 442376 | tf_op jit(solution)/shard_map/ppermute | solution.py:32
  63.7 0.0 collective-permute-start.13
  63.7 3.6 %collective-permute-done.12.refs_1_ = bf16[32,2304]{1,0:T(8,128)(2,1)S(1)} collective-permute-done((bf16[32,2304]{1,0:T(8,128)(2,1)S(1)}, bf16[32,2304]{1,0:T(8,128)(2,1)S(1)}, u32[]{:S(2)}, u32[]{:S(2)}) %collective-permute-start.12) | collective-permute-done | bytes 147488 | tf_op jit(solution)/shard_map/ppermute | solution.py:32
  67.3 0.0 collective-permute-start.14
  67.3 0.0 collective-permute-done.13.refs_2_
  67.3 1.4 %collective-permute-done.14.refs_3_ = bf16[32,2304]{1,0:T(8,128)(2,1)S(1)} collective-permute-done((bf16[32,2304]{1,0:T(8,128)(2,1)S(1)}, bf16[32,2304]{1,0:T(8,128)(2,1)S(1)}, u32[]{:S(2)}, u32[]{:S(2)}) %collective-permute-start.14) | collective-permute-done | bytes 147488 | tf_op jit(solution)/shard_map/ppermute | solution.py:32
  68.7 0.0 copy-done.5
  68.7 9.8 %shard_map.176 = (f32[64,2304]{1,0:T(8,128)S(1)}, bf16[64,2304]{1,0:T(8,128)(2,1)S(1)}, bf16[64,1152]{1,0:T(8,128)(2,1)S(1)}, bf16[64,2304]{1,0:T(8,128)(2,1)S(1)}) custom-call(bf16[32,2304]{1,0:T(8,128)(2,1)S(1)} %pad_maximum_fusion.2.refs_0_.own_ref, bf16[32,2304]{1,0:T(8,128)(2,1)S(1)} %collective-permute-done.12.refs_1_, ...), custom_call_target="tpu_custom_call" | custom-call | tf_op jit(solution)/shard_map/pallas_call | solution.py:223
  78.4 0.2 collective-permute-start.15
  78.6 1.4 %collective-permute-done.15.got_ref = bf16[64,2304]{1,0:T(8,128)(2,1)S(1)} collective-permute-done((bf16[64,2304]{1,0:T(8,128)(2,1)S(1)}, bf16[64,2304]{1,0:T(8,128)(2,1)S(1)}, u32[]{:S(2)}, u32[]{:S(2)}) %collective-permute-start.15) | collective-permute-done | bytes 294944 | tf_op jit(solution)/shard_map/ppermute | solution.py:32
  80.1 0.1 shard_map.177
  80.1 1.6 %collective-permute-start.16 = (bf16[32,2304]{1,0:T(8,128)(2,1)S(1)}, bf16[32,2304]{1,0:T(8,128)(2,1)S(1)}, u32[]{:S(2)}, u32[]{:S(2)}) collective-permute-start(bf16[32,2304]{1,0:T(8,128)(2,1)S(1)} %get-tuple-element.39), channel_id=1, source_target_pairs={{0,2},{1,3},{2,0},{3,1},{4,6},{5,7},{6,4},{7,5},{8,10},{9,11},{10,... | collective-permute-start | bytes 442376 | tf_op jit(solution)/shard_map/ppermute | solution.py:32
  81.7 6.9 %shard_map.179 = (bf16[2304,1152]{1,0:T(8,128)(2,1)}, bf16[1152,2304]{1,0:T(8,128)(2,1)}) custom-call(bf16[128,2304]{1,0:T(8,128)(2,1)S(1)} %get-tuple-element.42.m_ref, bf16[64,1152]{1,0:T(8,128)(2,1)S(1)} %get-tuple-element.43.refs_0_, bf16[64,1152]{1,0:T(8,128)(2,1)S(1)} %get-tuple-element.44.refs_1_, bf16[128,1152]{1,0:T(8,128)(2,1)S(1)} %get-tuple-element.45.refs_2_, ...), custom_call_target="tpu_custom_call" | custom-call | tf_op jit(solution)/shard_map/pallas_call | solution.py:353
  88.6 0.0 collective-permute-done.16.got_ref
  88.6 0.2 shard_map.178
  88.7 0.6 slice_bitcast_fusion.2
  89.4 0.6 slice_bitcast_fusion
  (12 shorter events, 0.1 us)
Async XLA Ops:
  1.4 10.6 %collective-permute-start.1 = (bf16[16,2304]{1,0:T(8,128)(2,1)S(1)}, bf16[16,2304]{1,0:T(8,128)(2,1)S(1)}, u32[]{:S(2)}, u32[]{:S(2)}) collective-permute-start(bf16[16,2304]{1,0:T(8,128)(2,1)S(1)} %pad_maximum_fusion.4), channel_id=1, source_target_pairs={{4,0},{8,4},{12,8},{16,12},{20,16},{24,20},{28,24},{5,1},{9,5},{13... | collective-permute-start | bytes 221192 | tf_op jit(solution)/shard_map/ppermute | solution.py:27
  3.5 9.3 %collective-permute-start = (bf16[16,2304]{1,0:T(8,128)(2,1)S(1)}, bf16[16,2304]{1,0:T(8,128)(2,1)S(1)}, u32[]{:S(2)}, u32[]{:S(2)}) collective-permute-start(bf16[16,2304]{1,0:T(8,128)(2,1)S(1)} %pad_maximum_fusion.3), channel_id=1, source_target_pairs={{0,4},{4,8},{8,12},{12,16},{16,20},{20,24},{24,28},{1,5},{5,9},{9,... | collective-permute-start | bytes 221192 | tf_op jit(solution)/shard_map/ppermute | solution.py:27
  9.9 6.3 %collective-permute-start.5 = (bf16[32,2304]{1,0:T(8,128)(2,1)S(1)}, bf16[32,2304]{1,0:T(8,128)(2,1)S(1)}, u32[]{:S(2)}, u32[]{:S(2)}) collective-permute-start(bf16[32,2304]{1,0:T(8,128)(2,1)S(1)} %pad_maximum_fusion.1.refs_0_), channel_id=1, source_target_pairs={{0,2},{1,3},{2,0},{3,1},{4,6},{5,7},{6,4},{7,5},{8,10},{9,11},{10,... | collective-permute-start | bytes 442376 | tf_op jit(solution)/shard_map/ppermute | solution.py:32
  13.6 5.2 %collective-permute-start.2 = (bf16[32,2304]{1,0:T(8,128)(2,1)S(1)}, bf16[32,2304]{1,0:T(8,128)(2,1)S(1)}, u32[]{:S(2)}, u32[]{:S(2)}) collective-permute-start(bf16[32,2304]{1,0:T(8,128)(2,1)S(1)} %pad_maximum_fusion.refs_0_.own_ref), channel_id=1, source_target_pairs={{0,2},{1,3},{2,0},{3,1},{4,6},{5,7},{6,4},{7,5},{8,10},{9,11},{10,... | collective-permute-start | bytes 442376 | tf_op jit(solution)/shard_map/ppermute | solution.py:32
  13.9 4.9 %collective-permute-start.6 = (bf16[32,2304]{1,0:T(8,128)(2,1)S(1)}, bf16[32,2304]{1,0:T(8,128)(2,1)S(1)}, u32[]{:S(2)}, u32[]{:S(2)}) collective-permute-start(bf16[32,2304]{1,0:T(8,128)(2,1)S(1)} %pad_maximum_fusion.1.refs_0_), channel_id=1, source_target_pairs={{0,1},{1,0},{2,3},{3,2},{4,5},{5,4},{6,7},{7,6},{8,9},{9,8},{10,11... | collective-permute-start | bytes 442376 | tf_op jit(solution)/shard_map/ppermute | solution.py:32
  16.2 2.6 %collective-permute-start.7 = (bf16[32,2304]{1,0:T(8,128)(2,1)S(1)}, bf16[32,2304]{1,0:T(8,128)(2,1)S(1)}, u32[]{:S(2)}, u32[]{:S(2)}) collective-permute-start(bf16[32,2304]{1,0:T(8,128)(2,1)S(1)} %collective-permute-done.5.refs_1_), channel_id=1, source_target_pairs={{0,1},{1,0},{2,3},{3,2},{4,5},{5,4},{6,7},{7,6},{8,9},{9,8},{10,11... | collective-permute-start | bytes 442376 | tf_op jit(solution)/shard_map/ppermute | solution.py:32
  16.2 10.4 %collective-permute-start.3 = (bf16[32,2304]{1,0:T(8,128)(2,1)S(1)}, bf16[32,2304]{1,0:T(8,128)(2,1)S(1)}, u32[]{:S(2)}, u32[]{:S(2)}) collective-permute-start(bf16[32,2304]{1,0:T(8,128)(2,1)S(1)} %pad_maximum_fusion.refs_0_.own_ref), channel_id=1, source_target_pairs={{0,1},{1,0},{2,3},{3,2},{4,5},{5,4},{6,7},{7,6},{8,9},{9,8},{10,11... | collective-permute-start | bytes 442376 | tf_op jit(solution)/shard_map/ppermute | solution.py:32
  18.8 7.9 %collective-permute-start.4 = (bf16[32,2304]{1,0:T(8,128)(2,1)S(1)}, bf16[32,2304]{1,0:T(8,128)(2,1)S(1)}, u32[]{:S(2)}, u32[]{:S(2)}) collective-permute-start(bf16[32,2304]{1,0:T(8,128)(2,1)S(1)} %collective-permute-done.2.refs_1_), channel_id=1, source_target_pairs={{0,1},{1,0},{2,3},{3,2},{4,5},{5,4},{6,7},{7,6},{8,9},{9,8},{10,11... | collective-permute-start | bytes 442376 | tf_op jit(solution)/shard_map/ppermute | solution.py:32
  18.8 2.5 %copy-start = (bf16[1,2304,1152]{2,1,0:T(8,128)(2,1)S(1)}, bf16[1,2304,1152]{2,1,0:T(8,128)(2,1)}, u32[]{:S(2)}) copy-start(bf16[1,2304,1152]{2,1,0:T(8,128)(2,1)} %param.22) | copy-start | bytes 15925252
  21.3 2.5 %copy-start.2 = (bf16[1,2304,1152]{2,1,0:T(8,128)(2,1)S(1)}, bf16[1,2304,1152]{2,1,0:T(8,128)(2,1)}, u32[]{:S(2)}) copy-start(bf16[1,2304,1152]{2,1,0:T(8,128)(2,1)} %param.24) | copy-start | bytes 15925252
  23.8 0.7 copy-start.7
  24.5 2.5 %copy-start.1 = (bf16[1,2304,1152]{2,1,0:T(8,128)(2,1)S(1)}, bf16[1,2304,1152]{2,1,0:T(8,128)(2,1)}, u32[]{:S(2)}) copy-start(bf16[1,2304,1152]{2,1,0:T(8,128)(2,1)} %param.22) | copy-start | bytes 15925252
  24.5 4.1 %copy-start.3 = (bf16[1,2304,1152]{2,1,0:T(8,128)(2,1)S(1)}, bf16[1,2304,1152]{2,1,0:T(8,128)(2,1)}, u32[]{:S(2)}) copy-start(bf16[1,2304,1152]{2,1,0:T(8,128)(2,1)} %param.24) | copy-start | bytes 15925252
  24.5 4.1 %copy-start.8 = (bf16[1,2304]{1,0:T(2,128)(2,1)S(1)}, bf16[1,2304]{1,0:T(2,128)(2,1)}, u32[]{:S(2)}) copy-start(bf16[1,2304]{1,0:T(2,128)(2,1)} %gain_ref.3) | copy-start | bytes 13828
  28.6 2.5 %copy-start.4 = (bf16[1,1152,2304]{2,1,0:T(8,128)(2,1)S(1)}, bf16[1,1152,2304]{2,1,0:T(8,128)(2,1)}, u32[]{:S(2)}) copy-start(bf16[1,1152,2304]{2,1,0:T(8,128)(2,1)} %param.23) | copy-start | bytes 15925252
  31.1 2.5 %copy-start.6 = (bf16[1,1152,2304]{2,1,0:T(8,128)(2,1)S(1)}, bf16[1,1152,2304]{2,1,0:T(8,128)(2,1)}, u32[]{:S(2)}) copy-start(bf16[1,1152,2304]{2,1,0:T(8,128)(2,1)} %param.25) | copy-start | bytes 15925252
  33.6 24.2 %copy-start.9 = (bf16[2,8,2304]{2,1,0:T(8,128)(2,1)S(1)}, bf16[2,8,2304]{2,1,0:T(8,128)(2,1)}, u32[]{:S(2)}) copy-start(bf16[2,8,2304]{2,1,0:T(8,128)(2,1)} %param.17) | copy-start | bytes 221188
  33.6 28.5 %copy-start.10 = (bf16[2,8,2304]{2,1,0:T(8,128)(2,1)S(1)}, bf16[2,8,2304]{2,1,0:T(8,128)(2,1)}, u32[]{:S(2)}) copy-start(bf16[2,8,2304]{2,1,0:T(8,128)(2,1)} %param.18) | copy-start | bytes 221188
  33.6 35.1 %copy-start.5 = (bf16[1,1152,2304]{2,1,0:T(8,128)(2,1)S(1)}, bf16[1,1152,2304]{2,1,0:T(8,128)(2,1)}, u32[]{:S(2)}) copy-start(bf16[1,1152,2304]{2,1,0:T(8,128)(2,1)} %param.23) | copy-start | bytes 15925252
  43.3 1.7 %collective-permute-start.8 = (bf16[64,2304]{1,0:T(8,128)(2,1)S(1)}, bf16[64,2304]{1,0:T(8,128)(2,1)S(1)}, u32[]{:S(2)}, u32[]{:S(2)}) collective-permute-start(bf16[64,2304]{1,0:T(8,128)(2,1)S(1)} %get-tuple-element.31), channel_id=1, source_target_pairs={{0,1},{1,0},{2,3},{3,2},{4,5},{5,4},{6,7},{7,6},{8,9},{9,8},{10,11... | collective-permute-start | bytes 884744 | tf_op jit(solution)/shard_map/ppermute | solution.py:32
  45.2 6.2 %collective-permute-start.9 = (bf16[32,2304]{1,0:T(8,128)(2,1)S(1)}, bf16[32,2304]{1,0:T(8,128)(2,1)S(1)}, u32[]{:S(2)}, u32[]{:S(2)}) collective-permute-start(bf16[32,2304]{1,0:T(8,128)(2,1)S(1)} %get-tuple-element.33), channel_id=1, source_target_pairs={{0,2},{1,3},{2,0},{3,1},{4,6},{5,7},{6,4},{7,5},{8,10},{9,11},{10,... | collective-permute-start | bytes 442376 | tf_op jit(solution)/shard_map/ppermute | solution.py:32
  51.5 6.3 %collective-permute-start.10 = (bf16[16,2304]{1,0:T(8,128)(2,1)S(1)}, bf16[16,2304]{1,0:T(8,128)(2,1)S(1)}, u32[]{:S(2)}, u32[]{:S(2)}) collective-permute-start(bf16[16,2304]{1,0:T(8,128)(2,1)S(1)} %get-tuple-element.34), channel_id=1, source_target_pairs={{0,4},{4,8},{8,12},{12,16},{16,20},{20,24},{24,28},{1,5},{5,9},{9,... | collective-permute-start | bytes 221192 | tf_op jit(solution)/shard_map/ppermute | solution.py:27
  55.8 6.2 %collective-permute-start.11 = (bf16[16,2304]{1,0:T(8,128)(2,1)S(1)}, bf16[16,2304]{1,0:T(8,128)(2,1)S(1)}, u32[]{:S(2)}, u32[]{:S(2)}) collective-permute-start(bf16[16,2304]{1,0:T(8,128)(2,1)S(1)} %get-tuple-element.35), channel_id=1, source_target_pairs={{4,0},{8,4},{12,8},{16,12},{20,16},{24,20},{28,24},{5,1},{9,5},{13... | collective-permute-start | bytes 221192 | tf_op jit(solution)/shard_map/ppermute | solution.py:27
  62.1 5.2 %collective-permute-start.12 = (bf16[32,2304]{1,0:T(8,128)(2,1)S(1)}, bf16[32,2304]{1,0:T(8,128)(2,1)S(1)}, u32[]{:S(2)}, u32[]{:S(2)}) collective-permute-start(bf16[32,2304]{1,0:T(8,128)(2,1)S(1)} %pad_maximum_fusion.2.refs_0_.own_ref), channel_id=1, source_target_pairs={{0,2},{1,3},{2,0},{3,1},{4,6},{5,7},{6,4},{7,5},{8,10},{9,11},{10,... | collective-permute-start | bytes 442376 | tf_op jit(solution)/shard_map/ppermute | solution.py:32
  63.7 3.6 %collective-permute-start.13 = (bf16[32,2304]{1,0:T(8,128)(2,1)S(1)}, bf16[32,2304]{1,0:T(8,128)(2,1)S(1)}, u32[]{:S(2)}, u32[]{:S(2)}) collective-permute-start(bf16[32,2304]{1,0:T(8,128)(2,1)S(1)} %pad_maximum_fusion.2.refs_0_.own_ref), channel_id=1, source_target_pairs={{0,1},{1,0},{2,3},{3,2},{4,5},{5,4},{6,7},{7,6},{8,9},{9,8},{10,11... | collective-permute-start | bytes 442376 | tf_op jit(solution)/shard_map/ppermute | solution.py:32
  67.3 1.4 %collective-permute-start.14 = (bf16[32,2304]{1,0:T(8,128)(2,1)S(1)}, bf16[32,2304]{1,0:T(8,128)(2,1)S(1)}, u32[]{:S(2)}, u32[]{:S(2)}) collective-permute-start(bf16[32,2304]{1,0:T(8,128)(2,1)S(1)} %collective-permute-done.12.refs_1_), channel_id=1, source_target_pairs={{0,1},{1,0},{2,3},{3,2},{4,5},{5,4},{6,7},{7,6},{8,9},{9,8},{10,11... | collective-permute-start | bytes 442376 | tf_op jit(solution)/shard_map/ppermute | solution.py:32
  78.4 1.6 %collective-permute-start.15 = (bf16[64,2304]{1,0:T(8,128)(2,1)S(1)}, bf16[64,2304]{1,0:T(8,128)(2,1)S(1)}, u32[]{:S(2)}, u32[]{:S(2)}) collective-permute-start(bf16[64,2304]{1,0:T(8,128)(2,1)S(1)} %get-tuple-element.37), channel_id=1, source_target_pairs={{0,1},{1,0},{2,3},{3,2},{4,5},{5,4},{6,7},{7,6},{8,9},{9,8},{10,11... | collective-permute-start | bytes 884744 | tf_op jit(solution)/shard_map/ppermute | solution.py:32
  80.1 8.5 %collective-permute-start.16 = (bf16[32,2304]{1,0:T(8,128)(2,1)S(1)}, bf16[32,2304]{1,0:T(8,128)(2,1)S(1)}, u32[]{:S(2)}, u32[]{:S(2)}) collective-permute-start(bf16[32,2304]{1,0:T(8,128)(2,1)S(1)} %get-tuple-element.39), channel_id=1, source_target_pairs={{0,2},{1,3},{2,0},{3,1},{4,6},{5,7},{6,4},{7,5},{8,10},{9,11},{10,... | collective-permute-start | bytes 442376 | tf_op jit(solution)/shard_map/ppermute | solution.py:32

commit v2 on v1

v2 whole, which is shorter than its diff:
```python
import jax
import jax.numpy as jnp
from jax import lax
from jax.experimental import pallas as pl
from jax.experimental.pallas import tpu as pltpu
from jax.sharding import PartitionSpec as P

TICKS = 2


sqrt_two_over_pi = 0.7978845608028654
cubic_coef = 0.044715
norm_eps = 1e-06

bf16 = jnp.bfloat16
f32 = jnp.float32
VM = pl.BlockSpec(memory_space=pltpu.VMEM)
HBM = pl.BlockSpec(memory_space=pltpu.HBM)


def params(mib):
    return pltpu.CompilerParams(vmem_limit_bytes=mib * 2**20)


def passed_along(value, axis, steps):
    count = lax.axis_size(axis)
    leading, last = (max(0, -steps), min(count, count - steps))
    return lax.ppermute(value, axis, [(source, source + steps) for source in range(leading, last)])


def swapped(value, bit):
    count = lax.axis_size("dp")
    return lax.ppermute(value, "dp", [(source, source ^ bit) for source in range(count)])


def dp_bits():
    count = lax.axis_size("dp")
    bits = []
    bit = count // 2
    while bit:
        bits.append(bit)
        bit //= 2
    return bits


def gather_blocks(block, bits):
    blocks = [block]
    for bit in bits:
        blocks = blocks + [swapped(b, bit) for b in blocks]
    return blocks


def parity_moved(value):
    sections, count = (lax.axis_size("section"), lax.axis_size("dp"))
    pairs = []
    for section in range(sections):
        for member in range(count):
            target = section + (1 if member % 2 == 0 else -1)
            if 0 <= target < sections:
                pairs.append((section * count + member, target * count + member))
    return lax.ppermute(value, ("section", "dp"), pairs)


def gelu_parts(linear):
    inner_arg = sqrt_two_over_pi * (linear + cubic_coef * linear * linear * linear)
    first_slope = sqrt_two_over_pi * (1.0 + 3.0 * cubic_coef * linear * linear)
    second_slope = 6.0 * sqrt_two_over_pi * cubic_coef * linear
    tanh_value = jnp.tanh(inner_arg)
    sech_square = 1.0 - tanh_value * tanh_value
    gelu_value = 0.5 * linear * (1.0 + tanh_value)
    gelu_first = 0.5 * (1.0 + tanh_value) + 0.5 * linear * sech_square * first_slope
    gelu_second = sech_square * (
        first_slope - linear * tanh_value * first_slope * first_slope + 0.5 * linear * second_slope
    )
    return (gelu_value, gelu_first, gelu_second)


def matrix_product(left, right):
    return jnp.dot(left, right, preferred_element_type=f32)


def product_last(left, right):
    return lax.dot_general(left, right, (((1,), (1,)), ((), ())), preferred_element_type=f32)


def product_first(left, right):
    return lax.dot_general(left, right, (((0,), (0,)), ((), ())), preferred_element_type=f32)


def norm_stats(values, values_tan):
    inverse = lax.rsqrt(jnp.mean(values * values, axis=-1, keepdims=True) + norm_eps)
    inverse_tan = -(inverse * inverse * inverse) * jnp.mean(
        values * values_tan, axis=-1, keepdims=True
    )
    return (inverse, inverse_tan)


def norm_rows(values, values_tan, gain_wide):
    inverse, inverse_tan = norm_stats(values, values_tan)
    normed = values * inverse * gain_wide
    normed_tan = (values_tan * inverse + values * inverse_tan) * gain_wide
    return (normed, normed_tan)


def piece(block, index, rows):
    return block[index * rows : (index + 1) * rows, :].astype(f32)


def pick(blocks, index, rows):
    return jnp.concatenate([piece(b, index, rows) for b in blocks], axis=0)


def pack_kernel(rows):
    later = TICKS - 1

    def body(*refs):
        act, act_tan, adj, adj_tan, fresh, loss, stash, stash_tan, gain = refs[:9]
        fwd, bwd, store, edge, gain_out = refs[9:14]
        late, sems = refs[14:]
        pairs = [
            (act.at[0], fwd.at[pl.ds(0, rows)]),
            (act_tan.at[0], fwd.at[pl.ds(rows, rows)]),
            (adj.at[0], bwd.at[pl.ds(0, rows)]),
            (adj_tan.at[0], bwd.at[pl.ds(rows, rows)]),
            (fresh.at[0], edge.at[pl.ds(0, rows)]),
            (loss.at[0], edge.at[pl.ds(rows, rows)]),
            (gain, gain_out),
        ]
        for tick in range(TICKS):
            pairs.append((stash.at[0, tick], store.at[pl.ds(2 * tick * rows, rows)]))
            pairs.append((stash_tan.at[0, tick], store.at[pl.ds((2 * tick + 1) * rows, rows)]))
        for tick in range(1, TICKS):
            pairs.append((fresh.at[tick], late.at[pl.ds(2 * (tick - 1) * rows, rows)]))
            pairs.append((loss.at[tick], late.at[pl.ds((2 * tick - 1) * rows, rows)]))
        copies = [pltpu.make_async_copy(a, b, sems.at[i]) for i, (a, b) in enumerate(pairs)]
        for copy in copies:
            copy.start()
        for copy in copies:
            copy.wait()
        section = lax.axis_index("section")
        at_first = section == 0
        at_last = section == lax.axis_size("section") - 1
        for k in range(2 * later):
            rows_late = late[k * rows : (k + 1) * rows, :].astype(f32)
            masked = jnp.where(at_first if k % 2 == 0 else at_last, rows_late, 0.0)
            base = (2 * TICKS + k) * rows
            store[base : base + rows, :] = masked.astype(bf16)

    return body


def arrive_kernel(rows):
    def body(fwd_ref, bwd_ref, edge_ref, token_ref, own_ref):
        section = lax.axis_index("section")
        at_first = section == 0
        at_last = section == lax.axis_size("section") - 1
        own_ref[:rows, :] = jnp.where(
            at_first, piece(edge_ref, 0, rows), piece(fwd_ref, 0, rows)
        ).astype(bf16)
        own_ref[rows : 2 * rows, :] = fwd_ref[rows:, :]
        own_ref[2 * rows : 3 * rows, :] = jnp.where(
            at_last, piece(edge_ref, 1, rows), piece(bwd_ref, 0, rows)
        ).astype(bf16)
        own_ref[3 * rows :, :] = bwd_ref[rows:, :]

    return body


def chunk_rows(total, limit):
    sizes = [c for c in range(128, limit + 1, 128) if total % c == 0]
    return sizes[-1] if sizes else total


def start_all(copies):
    for copy in copies:
        copy.start()


def load_down_kernel(step):
    def body(down_hbm, ddown_hbm, down_ref, down_t_ref, ddown_ref, ddown_t_ref, token, sems):
        token[...] = jnp.zeros_like(token)
        steps = down_hbm.shape[0] // step
        loads = ((down_hbm, down_ref, down_t_ref), (ddown_hbm, ddown_ref, ddown_t_ref))

        def copies(i):
            span = pl.ds(pl.multiple_of(i * step, step), step)
            return [
                pltpu.make_async_copy(src.at[span], dst.at[span], sems.at[2 * i + k])
                for k, (src, dst, _) in enumerate(loads)
            ]

        lax.fori_loop(0, steps, lambda i, c: start_all(copies(i)), None)

        def work(i, carry):
            span = pl.ds(pl.multiple_of(i * step, step), step)
            for copy, (_, dst, flip) in zip(copies(i), loads):
                copy.wait()
                flip[:, span] = dst[span, :].T

        lax.fori_loop(0, steps, work, None)

    return body


def stash_kernel(count, rows, step):
    tokens = count * rows

    def body(*refs):
        blocks = refs[:count]
        gain_ref, up_hbm, dup_hbm = refs[count : count + 3]
        (
            m_ref,
            q_ref,
            slope_ref,
            bend_ref,
            up_ref,
            dup_ref,
            stack,
            plain,
            both,
            side,
            sems,
        ) = refs[count + 3 :]
        steps = up_hbm.shape[0] // step
        loads = ((up_hbm, up_ref), (dup_hbm, dup_ref))

        def copies(i):
            span = pl.ds(pl.multiple_of(i * step, step), step)
            return [
                pltpu.make_async_copy(src.at[span], dst.at[span], sems.at[2 * i + k])
                for k, (src, dst) in enumerate(loads)
            ]

        lax.fori_loop(0, steps, lambda i, c: start_all(copies(i)), None)
        gain_wide = gain_ref[...].astype(f32)
        for tick in range(TICKS):
            normed, normed_tan = norm_rows(
                pick(blocks, 2 * tick, rows), pick(blocks, 2 * tick + 1, rows), gain_wide
            )
            base = 2 * tick * tokens
            stack[base : base + tokens, :] = normed_tan.astype(bf16)
            stack[base + tokens : base + 2 * tokens, :] = normed.astype(bf16)
            plain[tick * tokens : (tick + 1) * tokens, :] = normed.astype(bf16)
        m_ref[...] = stack[...].T
        both[...] = jnp.zeros_like(both)
        side[...] = jnp.zeros_like(side)

        def work(i, carry):
            span = pl.ds(pl.multiple_of(i * step, step), step)
            sides = zip(copies(i), loads, ((stack, both), (plain, side)))
            for copy, (_, dst), (left, total) in sides:
                copy.wait()
                total[...] += matrix_product(left[:, span], dst[span, :])

        lax.fori_loop(0, steps, work, None)
        for tick in range(TICKS):
            base = 2 * tick * tokens
            linear = both[base + tokens : base + 2 * tokens, :]
            linear_tan = (
                both[base : base + tokens, :] + side[tick * tokens : (tick + 1) * tokens, :]
            )
            value, first, second = gelu_parts(linear)
            q_pair = jnp.concatenate([first * linear_tan, value], axis=0).astype(bf16)
            q_ref[:, base : base + 2 * tokens] = q_pair.T
            slope_ref[tick * tokens : (tick + 1) * tokens, :] = first
            bend_ref[tick * tokens : (tick + 1) * tokens, :] = second * linear_tan

    return body


def tick_kernel(count, rows, tick):
    tokens = count * rows
    half = count // 2
    n_in = count if tick == 0 else 2 * count

    def body(*refs):
        blocks = refs[:n_in]
        (
            gain_ref,
            up_ref,
            dup_ref,
            down_ref,
            down_t_ref,
            ddown_ref,
            ddown_t_ref,
            slope_ref,
            bend_ref,
        ) = refs[n_in : n_in + 9]
        outs = refs[n_in + 9 : -2]
        pair_ref, hid_ref = refs[-2:]
        keep_ref, send_ref, z_ref, adj_ref = outs[:4]
        even = (lax.axis_index("dp") & 1) == 0
        gain_wide = gain_ref[...].astype(f32)
        if tick == 0:
            values = [pick(blocks, a, rows) for a in range(4)]
        else:
            mine, theirs, edges = (blocks[:half], blocks[half:count], blocks[count:])
            values = []
            for chain in range(2):
                for a in range(2):
                    here = [piece(u, 2 * b + a, rows) for b in (0, 1) for u in mine]
                    there = [piece(u, 2 * b + a, rows) for b in (1, 0) for u in theirs]
                    here = jnp.concatenate(here, axis=0)
                    there = jnp.concatenate(there, axis=0)
                    first, second = (here, there) if chain == 0 else (there, here)
                    value = jnp.where(even, first, second)
                    if a == 0:
                        value = value + pick(edges, 2 * TICKS + 2 * (tick - 1) + chain, rows)
                    values.append(value)
            if len(outs) > 4:
                for a in range(4):
                    outs[4][a * rows : (a + 1) * rows, :] = values[a][:rows].astype(bf16)
        normed, normed_tan = norm_rows(values[0], values[1], gain_wide)
        pair_ref[:tokens, :] = normed.astype(bf16)
        pair_ref[tokens:, :] = normed_tan.astype(bf16)
        adj_ref[:tokens, :] = values[2].astype(bf16)
        adj_ref[tokens:, :] = values[3].astype(bf16)
        hidden, width = up_ref.shape[1], up_ref.shape[0]
        size = 384 if hidden % 384 == 0 else hidden
        base = tick * tokens

        def inner(i, carry):
            at = i * size if hidden % size == 0 else jnp.minimum(i * size, hidden - size)
            span = pl.ds(pl.multiple_of(at, 128) if size != hidden else 0, size)
            both = matrix_product(pair_ref[...], up_ref[:, span])
            side = matrix_product(pair_ref[:tokens, :], dup_ref[:, span])
            e_both = matrix_product(adj_ref[...], down_t_ref[:, span])
            e_side = matrix_product(adj_ref[:tokens, :], ddown_t_ref[:, span])
            value, first, _ = gelu_parts(both[:tokens])
            hid_ref[:tokens, span] = value.astype(bf16)
            hid_ref[tokens:, span] = (first * (both[tokens:] + side)).astype(bf16)
            upstream = e_both[:tokens]
            slope = slope_ref[base : base + tokens, span]
            bend = bend_ref[base : base + tokens, span]
            z_ref[:tokens, span] = (upstream * slope).astype(bf16)
            z_ref[tokens:, span] = ((e_both[tokens:] + e_side) * slope + upstream * bend).astype(
                bf16
            )

        lax.fori_loop(0, -(-hidden // size), inner, None)
        size_out = 1152 if width % 1152 == 0 else width
        order = [k for j in range(half) for k in (j, j + half)]

        def outer(i, carry):
            span = pl.ds(pl.multiple_of(i * size_out, size_out), size_out)
            p_both = matrix_product(hid_ref[...], down_ref[:, span])
            p_side = matrix_product(hid_ref[:tokens, :], ddown_ref[:, span])
            t_both = product_last(z_ref[...], up_ref[span, :])
            t_side = product_last(z_ref[:tokens, :], dup_ref[span, :])
            parts = (
                p_both[:tokens],
                p_both[tokens:] + p_side,
                t_both[:tokens],
                t_both[tokens:] + t_side,
            )
            if tick + 1 == TICKS:
                for k in range(count):
                    for a in range(4):
                        part = parts[a][k * rows : (k + 1) * rows]
                        if k < half:
                            at = (4 * k + a) * rows
                            keep_ref[at : at + rows, span] = part
                        else:
                            at = (4 * (k - half) + a) * rows
                            send_ref[at : at + rows, span] = part.astype(bf16)
            else:
                kept = [jnp.where(even, parts[a], parts[a + 2]) for a in range(2)]
                sent = [jnp.where(even, parts[a + 2], parts[a]) for a in range(2)]
                for i, k in enumerate(order):
                    for a in range(2):
                        at = (2 * i + a) * rows
                        keep_ref[at : at + rows, span] = kept[a][k * rows : (k + 1) * rows]
                        at = (2 * (i ^ 1) + a) * rows
                        send_ref[at : at + rows, span] = sent[a][k * rows : (k + 1) * rows].astype(
                            bf16
                        )

        lax.fori_loop(0, width // size_out, outer, None)

    return body


def add_body(keep_ref, got_ref, low_ref, high_ref):
    half = keep_ref.shape[0] // 2
    low_ref[...] = keep_ref[:half, :] + got_ref[:half, :].astype(f32)
    high_ref[...] = (keep_ref[half:, :] + got_ref[half:, :].astype(f32)).astype(bf16)


def norm_back(values, values_tan, gain_wide, arriving, arriving_tan, summed, summed_tan):
    inverse, inverse_tan = norm_stats(values, values_tan)
    weighted = summed * gain_wide
    weighted_tan = summed_tan * gain_wide
    moment = jnp.mean(values * weighted, axis=-1, keepdims=True)
    moment_tan = jnp.mean(values_tan * weighted + values * weighted_tan, axis=-1, keepdims=True)
    inverse_cube = inverse * inverse * inverse
    returned = arriving + inverse * weighted - inverse_cube * values * moment
    returned_tan = (
        arriving_tan
        + inverse_tan * weighted
        + inverse * weighted_tan
        - 3.0 * inverse * inverse * inverse_tan * values * moment
        - inverse_cube * values_tan * moment
        - inverse_cube * values * moment_tan
    )
    return (returned, returned_tan)


def unit_kernel(rows, tick):
    def body(keep_ref, got_ref, own_ref, other_ref, stash_ref, stash_other_ref, gain_ref, out_ref):
        even = (lax.axis_index("dp") & 1) == 0
        total = keep_ref[...] + got_ref[...].astype(f32)
        sources = ((own_ref, stash_ref), (other_ref, stash_other_ref))

        @pl.when(even)
        def _():
            for b, (block, _) in enumerate(sources):
                for a in range(2):
                    at = (2 * b + a) * rows
                    out_ref[at : at + rows, :] = (
                        piece(block, a, rows) + total[at : at + rows]
                    ).astype(bf16)

        @pl.when(jnp.logical_not(even))
        def _():
            gain_wide = gain_ref[...].astype(f32)
            for b, (block, store) in enumerate(sources):
                at = 2 * b * rows
                returned = norm_back(
                    piece(store, 2 * tick, rows),
                    piece(store, 2 * tick + 1, rows),
                    gain_wide,
                    piece(block, 2, rows),
                    piece(block, 3, rows),
                    total[at : at + rows],
                    total[at + rows : at + 2 * rows],
                )
                for a in range(2):
                    out_ref[at + a * rows : at + (a + 1) * rows, :] = returned[a].astype(bf16)

    return body


def last_kernel(rows, tick):
    def body(keep_ref, got_ref, own_ref, stash_ref, gain_ref, *outs):
        total = keep_ref[...] + got_ref[...].astype(f32)
        parts = [total[a * rows : (a + 1) * rows] for a in range(4)]
        for a in range(2):
            outs[a][0] = (piece(own_ref, a, rows) + parts[a]).astype(bf16)
        returned = norm_back(
            piece(stash_ref, 2 * tick, rows),
            piece(stash_ref, 2 * tick + 1, rows),
            gain_ref[...].astype(f32),
            piece(own_ref, 2, rows),
            piece(own_ref, 3, rows),
            parts[2],
            parts[3],
        )
        for a in range(2):
            outs[2 + a][0] = returned[a].astype(bf16)

    return body


def curvature_kernel(steps):
    def body(*refs):
        m_ref, q_ref = refs[:2]
        z_refs, adj_refs = refs[2 : 2 + TICKS], refs[2 + TICKS : 2 + 2 * TICKS]
        up_hbm, down_hbm, up_ref, down_ref, sems = refs[2 + 2 * TICKS :]
        jobs = ((m_ref, z_refs, up_ref, up_hbm), (q_ref, adj_refs, down_ref, down_hbm))

        def copies(i):
            made = []
            for k, (_, _, ref, hbm) in enumerate(jobs):
                size = ref.shape[0] // steps
                span = pl.ds(pl.multiple_of(i * size, size), size)
                made.append(pltpu.make_async_copy(ref.at[span], hbm.at[span], sems.at[2 * i + k]))
            return made

        def work(i, carry):
            for copy, (left, rights, ref, _) in zip(copies(i), jobs):
                size = ref.shape[0] // steps
                span = pl.ds(pl.multiple_of(i * size, size), size)
                right = jnp.concatenate([r[...] for r in rights], axis=0)
                ref[span, :] = matrix_product(left[span, :], right).astype(bf16)
                copy.start()

        lax.fori_loop(0, steps, work, None)

        def finish(i, carry):
            for copy in copies(i):
                copy.wait()

        lax.fori_loop(0, steps, finish, None)

    return body


def call(body, outs, mib, *operands, specs=None, scratch=()):
    operands = [
        pltpu.with_memory_space_constraint(x, pltpu.HBM) if specs and specs[i] is HBM else x
        for i, x in enumerate(operands)
    ]
    return pl.pallas_call(
        body,
        in_specs=specs or [VM] * len(operands),
        out_specs=[VM] * len(outs),
        out_shape=[jax.ShapeDtypeStruct(*o) if isinstance(o, tuple) else o for o in outs],
        scratch_shapes=scratch,
        compiler_params=params(mib),
    )(*operands)


def shards(
    carry_act,
    carry_act_tan,
    carry_adj,
    carry_adj_tan,
    fresh_act,
    loss_cot,
    stash_act,
    stash_act_tan,
    norm_gain,
    up_weight,
    down_weight,
    up_dir,
    down_dir,
):
    count = lax.axis_size("dp")
    half = count // 2
    bits = dp_bits()
    rows, width = carry_act.shape[1:]
    hidden = up_weight.shape[2]
    tokens = count * rows
    pairs = 2 * TICKS * tokens
    late = 2 * (TICKS - 1) * rows
    grant = max(6, tokens // 5)

    n_copies = 7 + 2 * TICKS + 2 * (TICKS - 1)
    forward, backward, store, edge, gain = call(
        pack_kernel(rows),
        [
            ((2 * rows, width), bf16),
            ((2 * rows, width), bf16),
            ((2 * TICKS * rows + late, width), bf16),
            ((2 * rows, width), bf16),
            ((1, width), bf16),
        ],
        4,
        carry_act,
        carry_act_tan,
        carry_adj,
        carry_adj_tan,
        fresh_act,
        loss_cot,
        stash_act,
        stash_act_tan,
        norm_gain,
        specs=[HBM] * 9,
        scratch=[pltpu.VMEM((max(late, rows), width), bf16), pltpu.SemaphoreType.DMA((n_copies,))],
    )
    moved_forward = passed_along(forward, "section", 1)
    moved_backward = passed_along(backward, "section", -1)
    far = swapped(store, bits[0])

    step = chunk_rows(hidden, 128)
    down_local, down_flip, ddown_local, ddown_flip, token = call(
        load_down_kernel(step),
        [
            pltpu.VMEM((hidden, width), bf16),
            pltpu.VMEM((width, hidden), bf16),
            pltpu.VMEM((hidden, width), bf16),
            pltpu.VMEM((width, hidden), bf16),
            ((8, 128), f32),
        ],
        grant,
        down_weight[0],
        down_dir[0],
        specs=[HBM, HBM],
        scratch=[pltpu.SemaphoreType.DMA((2 * (hidden // step),))],
    )
    moved_forward, moved_backward, far, token = lax.optimization_barrier(
        (moved_forward, moved_backward, far, token)
    )
    stores = [store, far]
    for bit in bits[1:]:
        stores = stores + [swapped(b, bit) for b in stores]
    own = call(
        arrive_kernel(rows),
        [((4 * rows, width), bf16)],
        4,
        moved_forward,
        moved_backward,
        edge,
        token,
    )[0]
    own_far = swapped(own, bits[0])
    step = chunk_rows(width, 768)
    m_all, q_all, slope, bend, up_local, dup_local = call(
        stash_kernel(count, rows, step),
        [
            ((width, pairs), bf16),
            ((hidden, pairs), bf16),
            ((TICKS * tokens, hidden), f32),
            ((TICKS * tokens, hidden), f32),
            pltpu.VMEM((width, hidden), bf16),
            pltpu.VMEM((width, hidden), bf16),
        ],
        grant,
        *stores,
        gain,
        up_weight[0],
        up_dir[0],
        specs=[VM] * (count + 1) + [HBM, HBM],
        scratch=[
            pltpu.VMEM((pairs, width), bf16),
            pltpu.VMEM((TICKS * tokens, width), bf16),
            pltpu.VMEM((pairs, hidden), f32),
            pltpu.VMEM((TICKS * tokens, hidden), f32),
            pltpu.SemaphoreType.DMA((2 * (width // step),)),
        ],
    )
    weights = (
        up_local,
        dup_local,
        down_local,
        down_flip,
        ddown_local,
        ddown_flip,
    )
    own_far, slope = lax.optimization_barrier((own_far, slope))
    blocks = [own, own_far]
    for bit in bits[1:]:
        blocks = blocks + [swapped(b, bit) for b in blocks]
    own_now, other_now = blocks[0], blocks[half]
    z_list, adj_list = [], []
    for tick in range(TICKS):
        last = tick + 1 == TICKS
        split = half if last else count
        width_of = 4 if last else 2
        outs = [
            ((split * width_of * rows, width), f32),
            ((split * width_of * rows, width), bf16),
            ((2 * tokens, hidden), bf16),
            ((2 * tokens, width), bf16),
        ]
        if tick:
            outs.append(((4 * rows, width), bf16))
        keep, send, z_pair, adj, *rest = call(
            tick_kernel(count, rows, tick),
            outs,
            grant,
            *blocks,
            gain,
            *weights,
            slope,
            bend,
            scratch=[pltpu.VMEM((2 * tokens, width), bf16), pltpu.VMEM((2 * tokens, hidden), bf16)],
        )
        if tick:
            own_now = rest[0]
        z_list.append(z_pair)
        adj_list.append(adj)
        for bit in bits[::-1][:-1]:
            got = swapped(send, bit)
            part = keep.shape[0] // 2
            keep, send = call(
                add_body, [((part, width), f32), ((part, width), bf16)], 4, keep, got
            )
        got = swapped(send, bits[0])
        if last:
            ended = call(
                last_kernel(rows, tick),
                [((1, rows, width), bf16)] * 4,
                4,
                keep,
                got,
                own_now,
                store,
                gain,
            )
        else:
            unit = call(
                unit_kernel(rows, tick),
                [((4 * rows, width), bf16)],
                4,
                keep,
                got,
                own_now,
                other_now,
                store,
                stores[half],
                gain,
            )[0]
            arrived = parity_moved(unit)
            mine = gather_blocks(arrived, bits[:-1])
            theirs = [swapped(u, bits[-1]) for u in mine]
            blocks = mine + theirs + stores

    steps = next(
        n for n in range(6, 0, -1) if width % (8 * n) == 0 and hidden % (8 * n) == 0
    )
    total_up, total_down = pl.pallas_call(
        curvature_kernel(steps),
        in_specs=[VM] * (2 + 2 * TICKS),
        out_specs=[HBM, HBM],
        out_shape=[
            jax.ShapeDtypeStruct((width, hidden), bf16),
            jax.ShapeDtypeStruct((hidden, width), bf16),
        ],
        scratch_shapes=[
            pltpu.VMEM((width, hidden), bf16),
            pltpu.VMEM((hidden, width), bf16),
            pltpu.SemaphoreType.DMA((2 * steps,)),
        ],
        compiler_params=params(11),
    )(m_all, q_all, *z_list, *adj_list)
    return (*ended, total_up[None], total_down[None])


def solution(mesh):
    in_specs = (
        P("section", "dp", None),
        P("section", "dp", None),
        P("section", "dp", None),
        P("section", "dp", None),
        P(None, "dp", None),
        P(None, "dp", None),
        P("section", None, "dp", None),
        P("section", None, "dp", None),
        P("section", None),
        P("section", None, "dp"),
        P("section", "dp", None),
        P("section", None, "dp"),
        P("section", "dp", None),
    )
    out_specs = (
        P("section", "dp", None),
        P("section", "dp", None),
        P("section", "dp", None),
        P("section", "dp", None),
        P("section", None, "dp"),
        P("section", "dp", None),
    )
    return jax.shard_map(shards, mesh=mesh, in_specs=in_specs, out_specs=out_specs, check_vma=False)
```

time: 90.7 us -> 72.2 us (0.80)
  local copies, waits for them, and re-layouts: 14.8 us -> 0 us
  Pallas kernels: 28.9 us -> 34.6 us
  other arithmetic: 3.22 us -> 0 us
  waiting for transfers between devices: 21.4 us -> 18.3 us
  starting transfers between devices: 20.9 us -> 18.2 us
    unnamed x22 -> x0, local copies, waits for them, and re-layouts: 12.7 us -> none
    ppermute x4 -> x2, starting transfers between devices: 12.5 us -> 4.68 us  [passed_along(): lax.ppermute(value, axis, [(source, source + steps) for source in range(l...]
    pallas_call x8 -> x11, Pallas kernels: 28.9 us -> 34.6 us  [the longest x10 29.8 us: call(): pl.pallas_call(body, in_specs=specs or [VM] * len(operands), out_specs=[V...]
    ppermute x4 -> x2, waiting for transfers between devices: 4.75 us -> 0.01 us  [passed_along(): lax.ppermute(value, axis, [(source, source + steps) for source in range(l...]
    ppermute x0 -> x1, starting transfers between devices: none -> 4.56 us  [parity_moved(): return lax.ppermute(value, ('section', 'dp'), pairs)]
    ppermute x0 -> x1, waiting for transfers between devices: none -> 3.86 us  [parity_moved(): return lax.ppermute(value, ('section', 'dp'), pairs)]
    ppermute x13, waiting for transfers between devices: 16.7 us -> 14.4 us  [swapped(): lax.ppermute(value, 'dp', [(source, source ^ bit) for source in range(cou...]
    concatenate x5 -> x0, other arithmetic: 1.64 us -> none  [the longest x1 0.79 us: shards(): forward = jnp.concatenate([carry_act[0], carry_act_tan[0]], axis=0)]
  transfers between devices with their start and end apart: 17 -> 16, of which waited for: 9 -> 8; matrix products, arithmetic and copies ran while one was open for 4% -> 0% of each run, Pallas kernels for 10% -> 21%
where the time goes in v2:
time: 72.2 us; the launch traced here: 71.8 us
  Pallas kernels  34.6 us (48%)
  waiting for transfers between devices  18.3 us (25%)
  starting transfers between devices  18.2 us (25%)
  between operations  0.77 us (1%)
    pallas_call x10, Pallas kernels, call(): pl.pallas_call(body, in_specs=specs or [VM] * len(operands), out_specs=[V...  29.8 us
    ppermute x13, waiting for transfers between devices, swapped(): lax.ppermute(value, 'dp', [(source, source ^ bit) for source in range(cou...  14.4 us
    ppermute x13, starting transfers between devices, swapped(): lax.ppermute(value, 'dp', [(source, source ^ bit) for source in range(cou...  8.97 us
    pallas_call x1, Pallas kernels, shards(): pl.pallas_call(curvature_kernel(steps), in_specs=[VM] * (2 + 2 * TICKS),...  4.79 us
    ppermute x2, starting transfers between devices, passed_along(): lax.ppermute(value, axis, [(source, source + steps) for source in range(l...  4.68 us
    ppermute x1, starting transfers between devices, parity_moved(): return lax.ppermute(value, ('section', 'dp'), pairs)  4.56 us
    ppermute x1, waiting for transfers between devices, parity_moved(): return lax.ppermute(value, ('section', 'dp'), pairs)  3.86 us
  transfers between devices with their start and end apart: 16, of which 8 were waited for; matrix products, arithmetic and copies ran while one was open for 0% of the time, Pallas kernels for 21%

profile of v2, /device:TPU:0, one launch (start us, length us, event | category | flops | bytes accessed | tf_op | source)
XLA Modules:
  0.0 71.8 jit_solution(5193252294523324508)
XLA Ops:
  0.6 1.1 %shard_map.172 = (bf16[16,2304]{1,0:T(8,128)(2,1)S(1)}, bf16[16,2304]{1,0:T(8,128)(2,1)S(1)}, bf16[48,2304]{1,0:T(8,128)(2,1)S(1)}, bf16[16,2304]{1,0:T(8,128)(2,1)S(1)}, bf16[1,2304]{1,0:T(2,128)(2,1)S(1)}) custom-call(bf16[1,8,2304]{2,1,0:T(8,128)(2,1)} %refs_0_.1, bf16[1,8,2304]{2,1,0:T(8,128)(2,1)} %refs_1_.1, bf16[1,8,2304]{2,1,0:T(8,128)(2,1)} %refs_2_.1, ...), custom_call_target="tpu_custom_call" | custom-call | tf_op jit(solution)/shard_map/pallas_call | solution.py:503
  1.8 3.1 %collective-permute-start.2 = (bf16[48,2304]{1,0:T(8,128)(2,1)S(1)}, bf16[48,2304]{1,0:T(8,128)(2,1)S(1)}, u32[]{:S(2)}, u32[]{:S(2)}) collective-permute-start(bf16[48,2304]{1,0:T(8,128)(2,1)S(1)} %get-tuple-element.49.refs_0_.stash_ref.refs_4_), channel_id=1, source_target_pairs={{0,2},{1,3},{2,0},{3,1},{4,6},{5,7},{6,4},{7,5},{8,10},{9,11},{10,... | collective-permute-start | bytes 663560 | tf_op jit(solution)/shard_map/ppermute | solution.py:33
  4.8 3.4 %collective-permute-start = (bf16[16,2304]{1,0:T(8,128)(2,1)S(1)}, bf16[16,2304]{1,0:T(8,128)(2,1)S(1)}, u32[]{:S(2)}, u32[]{:S(2)}) collective-permute-start(bf16[16,2304]{1,0:T(8,128)(2,1)S(1)} %get-tuple-element.47), channel_id=1, source_target_pairs={{0,4},{4,8},{8,12},{12,16},{16,20},{20,24},{24,28},{1,5},{5,9},{9,... | collective-permute-start | bytes 221192 | tf_op jit(solution)/shard_map/ppermute | solution.py:28
  8.2 1.3 %collective-permute-start.1 = (bf16[16,2304]{1,0:T(8,128)(2,1)S(1)}, bf16[16,2304]{1,0:T(8,128)(2,1)S(1)}, u32[]{:S(2)}, u32[]{:S(2)}) collective-permute-start(bf16[16,2304]{1,0:T(8,128)(2,1)S(1)} %get-tuple-element.48), channel_id=1, source_target_pairs={{4,0},{8,4},{12,8},{16,12},{20,16},{24,20},{28,24},{5,1},{9,5},{13... | collective-permute-start | bytes 221192 | tf_op jit(solution)/shard_map/ppermute | solution.py:28
  9.5 0.1 collective-permute-start.4
  9.6 5.0 %shard_map.173 = (bf16[1152,2304]{1,0:T(8,128)(2,1)S(1)}, bf16[2304,1152]{1,0:T(8,128)(2,1)S(1)}, bf16[1152,2304]{1,0:T(8,128)(2,1)S(1)}, bf16[2304,1152]{1,0:T(8,128)(2,1)S(1)}, f32[8,128]{1,0:T(8,128)S(1)}) custom-call(bf16[1152,2304]{1,0:T(8,128)(2,1)} %bitcast.8, bf16[1152,2304]{1,0:T(8,128)(2,1)} %bitcast.9), custom_call_target="tpu_custom_call" | custom-call | tf_op jit(solution)/shard_map/pallas_call | solution.py:503
  14.6 0.0 collective-permute-done.fwd_ref
  14.6 0.0 collective-permute-done.1.bwd_ref
  14.6 0.0 collective-permute-done.2.refs_1_.refs_5_
  14.6 0.6 collective-permute-start.5
  15.2 0.6 collective-permute-start.3
  15.8 0.0 collective-permute-start.6
  15.8 0.0 collective-permute-done.4.refs_2_.stash_other_ref.refs_6_
  15.8 0.5 collective-permute-done.5.refs_3_.refs_7_
  16.2 5.1 %shard_map.175 = (bf16[2304,128]{1,0:T(8,128)(2,1)S(1)}, bf16[1152,128]{1,0:T(8,128)(2,1)S(1)}, f32[64,1152]{1,0:T(8,128)S(1)}, f32[64,1152]{1,0:T(8,128)S(1)}, ...) custom-call(bf16[48,2304]{1,0:T(8,128)(2,1)S(1)} %get-tuple-element.49.refs_0_.stash_ref.refs_4_, ...), custom_call_target="tpu_custom_call" | custom-call | tf_op jit(solution)/shard_map/pallas_call | solution.py:503
  21.4 0.0 collective-permute-done.3.refs_1_
  21.4 0.4 collective-permute-start.7
  21.8 0.0 collective-permute-done.6.refs_2_.other_ref
  21.8 1.0 %collective-permute-done.7.refs_3_ = bf16[32,2304]{1,0:T(8,128)(2,1)S(1)} collective-permute-done((bf16[32,2304]{1,0:T(8,128)(2,1)S(1)}, bf16[32,2304]{1,0:T(8,128)(2,1)S(1)}, u32[]{:S(2)}, u32[]{:S(2)}) %collective-permute-start.7) | collective-permute-done | bytes 147488 | tf_op jit(solution)/shard_map/ppermute | solution.py:33
  22.8 8.7 %shard_map.176 = (f32[64,2304]{1,0:T(8,128)S(1)}, bf16[64,2304]{1,0:T(8,128)(2,1)S(1)}, bf16[64,1152]{1,0:T(8,128)(2,1)S(1)}, bf16[64,2304]{1,0:T(8,128)(2,1)S(1)}) custom-call(bf16[32,2304]{1,0:T(8,128)(2,1)S(1)} %shard_map.174.refs_0_.own_ref, bf16[32,2304]{1,0:T(8,128)(2,1)S(1)} %collective-permute-done.3.refs_1_, ...), custom_call_target="tpu_custom_call" | custom-call | tf_op jit(solution)/shard_map/pallas_call | solution.py:503
  31.6 0.4 collective-permute-start.8
  32.0 1.2 %collective-permute-done.8.got_ref = bf16[64,2304]{1,0:T(8,128)(2,1)S(1)} collective-permute-done((bf16[64,2304]{1,0:T(8,128)(2,1)S(1)}, bf16[64,2304]{1,0:T(8,128)(2,1)S(1)}, u32[]{:S(2)}, u32[]{:S(2)}) %collective-permute-start.8) | collective-permute-done | bytes 294944 | tf_op jit(solution)/shard_map/ppermute | solution.py:33
  33.2 0.1 shard_map.177
  33.3 1.2 %collective-permute-start.9 = (bf16[32,2304]{1,0:T(8,128)(2,1)S(1)}, bf16[32,2304]{1,0:T(8,128)(2,1)S(1)}, u32[]{:S(2)}, u32[]{:S(2)}) collective-permute-start(bf16[32,2304]{1,0:T(8,128)(2,1)S(1)} %get-tuple-element.70), channel_id=1, source_target_pairs={{0,2},{1,3},{2,0},{3,1},{4,6},{5,7},{6,4},{7,5},{8,10},{9,11},{10,... | collective-permute-start | bytes 442376 | tf_op jit(solution)/shard_map/ppermute | solution.py:33
  34.5 5.0 %collective-permute-done.9.got_ref = bf16[32,2304]{1,0:T(8,128)(2,1)S(1)} collective-permute-done((bf16[32,2304]{1,0:T(8,128)(2,1)S(1)}, bf16[32,2304]{1,0:T(8,128)(2,1)S(1)}, u32[]{:S(2)}, u32[]{:S(2)}) %collective-permute-start.9) | collective-permute-done | bytes 147488 | tf_op jit(solution)/shard_map/ppermute | solution.py:33
  39.4 0.1 shard_map.178
  39.5 4.6 %collective-permute-start.10 = (bf16[32,2304]{1,0:T(8,128)(2,1)S(1)}, bf16[32,2304]{1,0:T(8,128)(2,1)S(1)}, u32[]{:S(2)}, u32[]{:S(2)}) collective-permute-start(bf16[32,2304]{1,0:T(8,128)(2,1)S(1)} %shard_map.178), channel_id=1, source_target_pairs={{0,4},{2,6},{4,8},{5,1},{6,10},{7,3},{8,12},{9,5},{10,14},{11,7},{... | collective-permute-start | bytes 442376 | tf_op jit(solution)/shard_map/ppermute | solution.py:61
  44.1 3.9 %collective-permute-done.10.refs_0_ = bf16[32,2304]{1,0:T(8,128)(2,1)S(1)} collective-permute-done((bf16[32,2304]{1,0:T(8,128)(2,1)S(1)}, bf16[32,2304]{1,0:T(8,128)(2,1)S(1)}, u32[]{:S(2)}, u32[]{:S(2)}) %collective-permute-start.10) | collective-permute-done | bytes 147488 | tf_op jit(solution)/shard_map/ppermute | solution.py:61
  47.9 1.2 %collective-permute-start.11 = (bf16[32,2304]{1,0:T(8,128)(2,1)S(1)}, bf16[32,2304]{1,0:T(8,128)(2,1)S(1)}, u32[]{:S(2)}, u32[]{:S(2)}) collective-permute-start(bf16[32,2304]{1,0:T(8,128)(2,1)S(1)} %collective-permute-done.10.refs_0_), channel_id=1, source_target_pairs={{0,2},{1,3},{2,0},{3,1},{4,6},{5,7},{6,4},{7,5},{8,10},{9,11},{10,... | collective-permute-start | bytes 442376 | tf_op jit(solution)/shard_map/ppermute | solution.py:33
  49.1 0.0 collective-permute-start.12
  49.1 4.0 %collective-permute-done.11.refs_1_ = bf16[32,2304]{1,0:T(8,128)(2,1)S(1)} collective-permute-done((bf16[32,2304]{1,0:T(8,128)(2,1)S(1)}, bf16[32,2304]{1,0:T(8,128)(2,1)S(1)}, u32[]{:S(2)}, u32[]{:S(2)}) %collective-permute-start.11) | collective-permute-done | bytes 147488 | tf_op jit(solution)/shard_map/ppermute | solution.py:33
  53.1 0.0 collective-permute-start.13
  53.1 0.0 collective-permute-done.12.refs_2_
  53.1 1.4 %collective-permute-done.13.refs_3_ = bf16[32,2304]{1,0:T(8,128)(2,1)S(1)} collective-permute-done((bf16[32,2304]{1,0:T(8,128)(2,1)S(1)}, bf16[32,2304]{1,0:T(8,128)(2,1)S(1)}, u32[]{:S(2)}, u32[]{:S(2)}) %collective-permute-start.13) | collective-permute-done | bytes 147488 | tf_op jit(solution)/shard_map/ppermute | solution.py:33
  54.5 8.9 %shard_map.179 = (f32[64,2304]{1,0:T(8,128)S(1)}, bf16[64,2304]{1,0:T(8,128)(2,1)S(1)}, bf16[64,1152]{1,0:T(8,128)(2,1)S(1)}, bf16[64,2304]{1,0:T(8,128)(2,1)S(1)}, bf16[32,2304]{1,0:T(8,128)(2,1)S(1)}) custom-call(bf16[32,2304]{1,0:T(8,128)(2,1)S(1)} %collective-permute-done.10.refs_0_, bf16[32,2304]{1,0:T(8,128)(2,1)S(1)} %collective-permute-done.11.refs_1_, ...), custom_call_target="tpu_custom_call" | custom-call | tf_op jit(solution)/shard_map/pallas_call | solution.py:503
  63.3 0.2 collective-permute-start.14
  63.5 1.4 %collective-permute-done.14.got_ref = bf16[64,2304]{1,0:T(8,128)(2,1)S(1)} collective-permute-done((bf16[64,2304]{1,0:T(8,128)(2,1)S(1)}, bf16[64,2304]{1,0:T(8,128)(2,1)S(1)}, u32[]{:S(2)}, u32[]{:S(2)}) %collective-permute-start.14) | collective-permute-done | bytes 294944 | tf_op jit(solution)/shard_map/ppermute | solution.py:33
  65.0 0.1 shard_map.180
  65.0 1.2 %collective-permute-start.15 = (bf16[32,2304]{1,0:T(8,128)(2,1)S(1)}, bf16[32,2304]{1,0:T(8,128)(2,1)S(1)}, u32[]{:S(2)}, u32[]{:S(2)}) collective-permute-start(bf16[32,2304]{1,0:T(8,128)(2,1)S(1)} %get-tuple-element.74), channel_id=1, source_target_pairs={{0,2},{1,3},{2,0},{3,1},{4,6},{5,7},{6,4},{7,5},{8,10},{9,11},{10,... | collective-permute-start | bytes 442376 | tf_op jit(solution)/shard_map/ppermute | solution.py:33
  66.2 4.8 %shard_map.182 = (bf16[2304,1152]{1,0:T(8,128)(2,1)}, bf16[1152,2304]{1,0:T(8,128)(2,1)}) custom-call(bf16[2304,128]{1,0:T(8,128)(2,1)S(1)} %get-tuple-element.80.refs_0_, bf16[1152,128]{1,0:T(8,128)(2,1)S(1)} %get-tuple-element.81.refs_1_, bf16[64,1152]{1,0:T(8,128)(2,1)S(1)} %get-tuple-element.82.refs_2_, bf16[64,1152]{1,0:T(8,128)(2,1)S(1)} %get-tuple-element.83.refs_3_, ...), custom_call_target="tpu_custom_call" | custom-call | tf_op jit(solution)/shard_map/pallas_call | solution.py:702
  71.0 0.0 collective-permute-done.15.got_ref
  71.0 0.8 %shard_map.181 = (bf16[1,8,2304]{2,1,0:T(8,128)(2,1)}, bf16[1,8,2304]{2,1,0:T(8,128)(2,1)}, bf16[1,8,2304]{2,1,0:T(8,128)(2,1)}, bf16[1,8,2304]{2,1,0:T(8,128)(2,1)}) custom-call(f32[32,2304]{1,0:T(8,128)S(1)} %get-tuple-element.73.keep_ref, bf16[32,2304]{1,0:T(8,128)(2,1)S(1)} %collective-permute-done.15.got_ref, ...), custom_call_target="tpu_custom_call" | custom-call | tf_op jit(solution)/shard_map/pallas_call | solution.py:503
  (1 shorter events, 0.0 us)
Async XLA Ops:
  1.8 12.8 %collective-permute-start.2 = (bf16[48,2304]{1,0:T(8,128)(2,1)S(1)}, bf16[48,2304]{1,0:T(8,128)(2,1)S(1)}, u32[]{:S(2)}, u32[]{:S(2)}) collective-permute-start(bf16[48,2304]{1,0:T(8,128)(2,1)S(1)} %get-tuple-element.49.refs_0_.stash_ref.refs_4_), channel_id=1, source_target_pairs={{0,2},{1,3},{2,0},{3,1},{4,6},{5,7},{6,4},{7,5},{8,10},{9,11},{10,... | collective-permute-start | bytes 663560 | tf_op jit(solution)/shard_map/ppermute | solution.py:33
  4.8 9.7 %collective-permute-start = (bf16[16,2304]{1,0:T(8,128)(2,1)S(1)}, bf16[16,2304]{1,0:T(8,128)(2,1)S(1)}, u32[]{:S(2)}, u32[]{:S(2)}) collective-permute-start(bf16[16,2304]{1,0:T(8,128)(2,1)S(1)} %get-tuple-element.47), channel_id=1, source_target_pairs={{0,4},{4,8},{8,12},{12,16},{16,20},{20,24},{24,28},{1,5},{5,9},{9,... | collective-permute-start | bytes 221192 | tf_op jit(solution)/shard_map/ppermute | solution.py:28
  8.2 6.4 %collective-permute-start.1 = (bf16[16,2304]{1,0:T(8,128)(2,1)S(1)}, bf16[16,2304]{1,0:T(8,128)(2,1)S(1)}, u32[]{:S(2)}, u32[]{:S(2)}) collective-permute-start(bf16[16,2304]{1,0:T(8,128)(2,1)S(1)} %get-tuple-element.48), channel_id=1, source_target_pairs={{4,0},{8,4},{12,8},{16,12},{20,16},{24,20},{28,24},{5,1},{9,5},{13... | collective-permute-start | bytes 221192 | tf_op jit(solution)/shard_map/ppermute | solution.py:28
  9.5 6.2 %collective-permute-start.4 = (bf16[48,2304]{1,0:T(8,128)(2,1)S(1)}, bf16[48,2304]{1,0:T(8,128)(2,1)S(1)}, u32[]{:S(2)}, u32[]{:S(2)}) collective-permute-start(bf16[48,2304]{1,0:T(8,128)(2,1)S(1)} %get-tuple-element.49.refs_0_.stash_ref.refs_4_), channel_id=1, source_target_pairs={{0,1},{1,0},{2,3},{3,2},{4,5},{5,4},{6,7},{7,6},{8,9},{9,8},{10,11... | collective-permute-start | bytes 663560 | tf_op jit(solution)/shard_map/ppermute | solution.py:33
  14.6 1.7 %collective-permute-start.5 = (bf16[48,2304]{1,0:T(8,128)(2,1)S(1)}, bf16[48,2304]{1,0:T(8,128)(2,1)S(1)}, u32[]{:S(2)}, u32[]{:S(2)}) collective-permute-start(bf16[48,2304]{1,0:T(8,128)(2,1)S(1)} %collective-permute-done.2.refs_1_.refs_5_), channel_id=1, source_target_pairs={{0,1},{1,0},{2,3},{3,2},{4,5},{5,4},{6,7},{7,6},{8,9},{9,8},{10,11... | collective-permute-start | bytes 663560 | tf_op jit(solution)/shard_map/ppermute | solution.py:33
  15.2 6.2 %collective-permute-start.3 = (bf16[32,2304]{1,0:T(8,128)(2,1)S(1)}, bf16[32,2304]{1,0:T(8,128)(2,1)S(1)}, u32[]{:S(2)}, u32[]{:S(2)}) collective-permute-start(bf16[32,2304]{1,0:T(8,128)(2,1)S(1)} %shard_map.174.refs_0_.own_ref), channel_id=1, source_target_pairs={{0,2},{1,3},{2,0},{3,1},{4,6},{5,7},{6,4},{7,5},{8,10},{9,11},{10,... | collective-permute-start | bytes 442376 | tf_op jit(solution)/shard_map/ppermute | solution.py:33
  15.8 6.1 %collective-permute-start.6 = (bf16[32,2304]{1,0:T(8,128)(2,1)S(1)}, bf16[32,2304]{1,0:T(8,128)(2,1)S(1)}, u32[]{:S(2)}, u32[]{:S(2)}) collective-permute-start(bf16[32,2304]{1,0:T(8,128)(2,1)S(1)} %shard_map.174.refs_0_.own_ref), channel_id=1, source_target_pairs={{0,1},{1,0},{2,3},{3,2},{4,5},{5,4},{6,7},{7,6},{8,9},{9,8},{10,11... | collective-permute-start | bytes 442376 | tf_op jit(solution)/shard_map/ppermute | solution.py:33
  21.4 1.4 %collective-permute-start.7 = (bf16[32,2304]{1,0:T(8,128)(2,1)S(1)}, bf16[32,2304]{1,0:T(8,128)(2,1)S(1)}, u32[]{:S(2)}, u32[]{:S(2)}) collective-permute-start(bf16[32,2304]{1,0:T(8,128)(2,1)S(1)} %collective-permute-done.3.refs_1_), channel_id=1, source_target_pairs={{0,1},{1,0},{2,3},{3,2},{4,5},{5,4},{6,7},{7,6},{8,9},{9,8},{10,11... | collective-permute-start | bytes 442376 | tf_op jit(solution)/shard_map/ppermute | solution.py:33
  31.6 1.6 %collective-permute-start.8 = (bf16[64,2304]{1,0:T(8,128)(2,1)S(1)}, bf16[64,2304]{1,0:T(8,128)(2,1)S(1)}, u32[]{:S(2)}, u32[]{:S(2)}) collective-permute-start(bf16[64,2304]{1,0:T(8,128)(2,1)S(1)} %get-tuple-element.68), channel_id=1, source_target_pairs={{0,1},{1,0},{2,3},{3,2},{4,5},{5,4},{6,7},{7,6},{8,9},{9,8},{10,11... | collective-permute-start | bytes 884744 | tf_op jit(solution)/shard_map/ppermute | solution.py:33
  33.3 6.2 %collective-permute-start.9 = (bf16[32,2304]{1,0:T(8,128)(2,1)S(1)}, bf16[32,2304]{1,0:T(8,128)(2,1)S(1)}, u32[]{:S(2)}, u32[]{:S(2)}) collective-permute-start(bf16[32,2304]{1,0:T(8,128)(2,1)S(1)} %get-tuple-element.70), channel_id=1, source_target_pairs={{0,2},{1,3},{2,0},{3,1},{4,6},{5,7},{6,4},{7,5},{8,10},{9,11},{10,... | collective-permute-start | bytes 442376 | tf_op jit(solution)/shard_map/ppermute | solution.py:33
  39.5 8.4 %collective-permute-start.10 = (bf16[32,2304]{1,0:T(8,128)(2,1)S(1)}, bf16[32,2304]{1,0:T(8,128)(2,1)S(1)}, u32[]{:S(2)}, u32[]{:S(2)}) collective-permute-start(bf16[32,2304]{1,0:T(8,128)(2,1)S(1)} %shard_map.178), channel_id=1, source_target_pairs={{0,4},{2,6},{4,8},{5,1},{6,10},{7,3},{8,12},{9,5},{10,14},{11,7},{... | collective-permute-start | bytes 442376 | tf_op jit(solution)/shard_map/ppermute | solution.py:61
  47.9 5.1 %collective-permute-start.11 = (bf16[32,2304]{1,0:T(8,128)(2,1)S(1)}, bf16[32,2304]{1,0:T(8,128)(2,1)S(1)}, u32[]{:S(2)}, u32[]{:S(2)}) collective-permute-start(bf16[32,2304]{1,0:T(8,128)(2,1)S(1)} %collective-permute-done.10.refs_0_), channel_id=1, source_target_pairs={{0,2},{1,3},{2,0},{3,1},{4,6},{5,7},{6,4},{7,5},{8,10},{9,11},{10,... | collective-permute-start | bytes 442376 | tf_op jit(solution)/shard_map/ppermute | solution.py:33
  49.1 4.0 %collective-permute-start.12 = (bf16[32,2304]{1,0:T(8,128)(2,1)S(1)}, bf16[32,2304]{1,0:T(8,128)(2,1)S(1)}, u32[]{:S(2)}, u32[]{:S(2)}) collective-permute-start(bf16[32,2304]{1,0:T(8,128)(2,1)S(1)} %collective-permute-done.10.refs_0_), channel_id=1, source_target_pairs={{0,1},{1,0},{2,3},{3,2},{4,5},{5,4},{6,7},{7,6},{8,9},{9,8},{10,11... | collective-permute-start | bytes 442376 | tf_op jit(solution)/shard_map/ppermute | solution.py:33
  53.1 1.4 %collective-permute-start.13 = (bf16[32,2304]{1,0:T(8,128)(2,1)S(1)}, bf16[32,2304]{1,0:T(8,128)(2,1)S(1)}, u32[]{:S(2)}, u32[]{:S(2)}) collective-permute-start(bf16[32,2304]{1,0:T(8,128)(2,1)S(1)} %collective-permute-done.11.refs_1_), channel_id=1, source_target_pairs={{0,1},{1,0},{2,3},{3,2},{4,5},{5,4},{6,7},{7,6},{8,9},{9,8},{10,11... | collective-permute-start | bytes 442376 | tf_op jit(solution)/shard_map/ppermute | solution.py:33
  63.3 1.6 %collective-permute-start.14 = (bf16[64,2304]{1,0:T(8,128)(2,1)S(1)}, bf16[64,2304]{1,0:T(8,128)(2,1)S(1)}, u32[]{:S(2)}, u32[]{:S(2)}) collective-permute-start(bf16[64,2304]{1,0:T(8,128)(2,1)S(1)} %get-tuple-element.72), channel_id=1, source_target_pairs={{0,1},{1,0},{2,3},{3,2},{4,5},{5,4},{6,7},{7,6},{8,9},{9,8},{10,11... | collective-permute-start | bytes 884744 | tf_op jit(solution)/shard_map/ppermute | solution.py:33
  65.0 6.0 %collective-permute-start.15 = (bf16[32,2304]{1,0:T(8,128)(2,1)S(1)}, bf16[32,2304]{1,0:T(8,128)(2,1)S(1)}, u32[]{:S(2)}, u32[]{:S(2)}) collective-permute-start(bf16[32,2304]{1,0:T(8,128)(2,1)S(1)} %get-tuple-element.74), channel_id=1, source_target_pairs={{0,2},{1,3},{2,0},{3,1},{4,6},{5,7},{6,4},{7,5},{8,10},{9,11},{10,... | collective-permute-start | bytes 442376 | tf_op jit(solution)/shard_map/ppermute | solution.py:33

commit v3 on v2

--- a/solution.py
+++ b/solution.py
@@ -111,69 +111,61 @@
 
 
 def pack_kernel(rows):
-    later = TICKS - 1
-
     def body(*refs):
         act, act_tan, adj, adj_tan, fresh, loss, stash, stash_tan, gain = refs[:9]
-        fwd, bwd, store, edge, gain_out = refs[9:14]
-        late, sems = refs[14:]
+        keep, send, store, gain_out = refs[9:13]
+        fwd, bwd, edge, sems = refs[13:]
         pairs = [
             (act.at[0], fwd.at[pl.ds(0, rows)]),
             (act_tan.at[0], fwd.at[pl.ds(rows, rows)]),
             (adj.at[0], bwd.at[pl.ds(0, rows)]),
             (adj_tan.at[0], bwd.at[pl.ds(rows, rows)]),
-            (fresh.at[0], edge.at[pl.ds(0, rows)]),
-            (loss.at[0], edge.at[pl.ds(rows, rows)]),
             (gain, gain_out),
         ]
         for tick in range(TICKS):
-            pairs.append((stash.at[0, tick], store.at[pl.ds(2 * tick * rows, rows)]))
-            pairs.append((stash_tan.at[0, tick], store.at[pl.ds((2 * tick + 1) * rows, rows)]))
-        for tick in range(1, TICKS):
-            pairs.append((fresh.at[tick], late.at[pl.ds(2 * (tick - 1) * rows, rows)]))
-            pairs.append((loss.at[tick], late.at[pl.ds((2 * tick - 1) * rows, rows)]))
+            at = 2 * tick * rows
+            pairs.append((stash.at[0, tick], store.at[pl.ds(at, rows)]))
+            pairs.append((stash_tan.at[0, tick], store.at[pl.ds(at + rows, rows)]))
+            pairs.append((fresh.at[tick], edge.at[pl.ds(at, rows)]))
+            pairs.append((loss.at[tick], edge.at[pl.ds(at + rows, rows)]))
         copies = [pltpu.make_async_copy(a, b, sems.at[i]) for i, (a, b) in enumerate(pairs)]
-        for copy in copies:
-            copy.start()
+        start_all(copies)
         for copy in copies:
             copy.wait()
+        even = (lax.axis_index("dp") & 1) == 0
+        ahead, behind = (fwd[...].astype(f32), bwd[...].astype(f32))
+        keep[...] = jnp.where(even, ahead, behind).astype(bf16)
+        send[...] = jnp.where(even, behind, ahead).astype(bf16)
         section = lax.axis_index("section")
         at_first = section == 0
         at_last = section == lax.axis_size("section") - 1
-        for k in range(2 * later):
-            rows_late = late[k * rows : (k + 1) * rows, :].astype(f32)
-            masked = jnp.where(at_first if k % 2 == 0 else at_last, rows_late, 0.0)
+        for k in range(2 * TICKS):
+            masked = jnp.where(at_first if k % 2 == 0 else at_last, piece(edge, k, rows), 0.0)
             base = (2 * TICKS + k) * rows
             store[base : base + rows, :] = masked.astype(bf16)
 
     return body
 
 
-def arrive_kernel(rows):
-    def body(fwd_ref, bwd_ref, edge_ref, token_ref, own_ref):
-        section = lax.axis_index("section")
-        at_first = section == 0
-        at_last = section == lax.axis_size("section") - 1
-        own_ref[:rows, :] = jnp.where(
-            at_first, piece(edge_ref, 0, rows), piece(fwd_ref, 0, rows)
-        ).astype(bf16)
-        own_ref[rows : 2 * rows, :] = fwd_ref[rows:, :]
-        own_ref[2 * rows : 3 * rows, :] = jnp.where(
-            at_last, piece(edge_ref, 1, rows), piece(bwd_ref, 0, rows)
-        ).astype(bf16)
-        own_ref[3 * rows :, :] = bwd_ref[rows:, :]
-
-    return body
+def join_body(keep_ref, got_ref, unit_ref):
+    half = keep_ref.shape[0]
+    unit_ref[:half, :] = keep_ref[...]
+    unit_ref[half:, :] = got_ref[...]
+
+
+def pass_body(unit_ref, far_ref, token_ref, out_ref, far_out_ref):
+    out_ref[...] = unit_ref[...]
+    far_out_ref[...] = far_ref[...]
+
+
+def start_all(copies):
+    for copy in copies:
+        copy.start()
 
 
 def chunk_rows(total, limit):
     sizes = [c for c in range(128, limit + 1, 128) if total % c == 0]
     return sizes[-1] if sizes else total
-
-
-def start_all(copies):
-    for copy in copies:
-        copy.start()
 
 
 def load_down_kernel(step):
@@ -271,7 +263,7 @@
 def tick_kernel(count, rows, tick):
     tokens = count * rows
     half = count // 2
-    n_in = count if tick == 0 else 2 * count
+    n_in = 2 * count
 
     def body(*refs):
         blocks = refs[:n_in]
@@ -291,32 +283,31 @@
         keep_ref, send_ref, z_ref, adj_ref = outs[:4]
         even = (lax.axis_index("dp") & 1) == 0
         gain_wide = gain_ref[...].astype(f32)
-        if tick == 0:
-            values = [pick(blocks, a, rows) for a in range(4)]
-        else:
-            mine, theirs, edges = (blocks[:half], blocks[half:count], blocks[count:])
-            values = []
-            for chain in range(2):
-                for a in range(2):
-                    here = [piece(u, 2 * b + a, rows) for b in (0, 1) for u in mine]
-                    there = [piece(u, 2 * b + a, rows) for b in (1, 0) for u in theirs]
-                    here = jnp.concatenate(here, axis=0)
-                    there = jnp.concatenate(there, axis=0)
-                    first, second = (here, there) if chain == 0 else (there, here)
-                    value = jnp.where(even, first, second)
-                    if a == 0:
-                        value = value + pick(edges, 2 * TICKS + 2 * (tick - 1) + chain, rows)
-                    values.append(value)
-            if len(outs) > 4:
-                for a in range(4):
-                    outs[4][a * rows : (a + 1) * rows, :] = values[a][:rows].astype(bf16)
+        mine, theirs, edges = (blocks[:half], blocks[half:count], blocks[count:])
+        values = []
+        for chain in range(2):
+            for a in range(2):
+                here = [piece(u, 2 * b + a, rows) for b in (0, 1) for u in mine]
+                there = [piece(u, 2 * b + a, rows) for b in (1, 0) for u in theirs]
+                here = jnp.concatenate(here, axis=0)
+                there = jnp.concatenate(there, axis=0)
+                first, second = (here, there) if chain == 0 else (there, here)
+                value = jnp.where(even, first, second)
+                if a == 0:
+                    value = value + pick(edges, 2 * TICKS + 2 * tick + chain, rows)
+                values.append(value)
+        for out, k in zip(outs[4:], (0, half)):
+            for a in range(4):
+                out[a * rows : (a + 1) * rows, :] = values[a][k * rows : (k + 1) * rows].astype(
+                    bf16
+                )
         normed, normed_tan = norm_rows(values[0], values[1], gain_wide)
         pair_ref[:tokens, :] = normed.astype(bf16)
         pair_ref[tokens:, :] = normed_tan.astype(bf16)
         adj_ref[:tokens, :] = values[2].astype(bf16)
         adj_ref[tokens:, :] = values[3].astype(bf16)
         hidden, width = up_ref.shape[1], up_ref.shape[0]
-        size = 384 if hidden % 384 == 0 else hidden
+        size = hidden
         base = tick * tokens
 
         def inner(i, carry):
@@ -532,20 +523,17 @@
     hidden = up_weight.shape[2]
     tokens = count * rows
     pairs = 2 * TICKS * tokens
-    late = 2 * (TICKS - 1) * rows
     grant = max(6, tokens // 5)
 
-    n_copies = 7 + 2 * TICKS + 2 * (TICKS - 1)
-    forward, backward, store, edge, gain = call(
+    keep, send, store, gain = call(
         pack_kernel(rows),
         [
             ((2 * rows, width), bf16),
             ((2 * rows, width), bf16),
-            ((2 * TICKS * rows + late, width), bf16),
-            ((2 * rows, width), bf16),
+            ((4 * TICKS * rows, width), bf16),
             ((1, width), bf16),
         ],
-        4,
+        grant,
         carry_act,
         carry_act_tan,
         carry_adj,
@@ -556,10 +544,16 @@
         stash_act_tan,
         norm_gain,
         specs=[HBM] * 9,
-        scratch=[pltpu.VMEM((max(late, rows), width), bf16), pltpu.SemaphoreType.DMA((n_copies,))],
-    )
-    moved_forward = passed_along(forward, "section", 1)
-    moved_backward = passed_along(backward, "section", -1)
+        scratch=[
+            pltpu.VMEM((2 * rows, width), bf16),
+            pltpu.VMEM((2 * rows, width), bf16),
+            pltpu.VMEM((2 * TICKS * rows, width), bf16),
+            pltpu.SemaphoreType.DMA((5 + 4 * TICKS,)),
+        ],
+    )
+    got = swapped(send, bits[-1])
+    unit = call(join_body, [((4 * rows, width), bf16)], grant, keep, got)[0]
+    arrived = parity_moved(unit)
     far = swapped(store, bits[0])
 
     step = chunk_rows(hidden, 128)
@@ -578,22 +572,13 @@
         specs=[HBM, HBM],
         scratch=[pltpu.SemaphoreType.DMA((2 * (hidden // step),))],
     )
-    moved_forward, moved_backward, far, token = lax.optimization_barrier(
-        (moved_forward, moved_backward, far, token)
+    arrived, far = call(
+        pass_body, [(arrived.shape, bf16), (far.shape, bf16)], grant, arrived, far, token
     )
     stores = [store, far]
     for bit in bits[1:]:
         stores = stores + [swapped(b, bit) for b in stores]
-    own = call(
-        arrive_kernel(rows),
-        [((4 * rows, width), bf16)],
-        4,
-        moved_forward,
-        moved_backward,
-        edge,
-        token,
-    )[0]
-    own_far = swapped(own, bits[0])
+    mine = gather_blocks(arrived, bits[:-1])
     step = chunk_rows(width, 768)
     m_all, q_all, slope, bend, up_local, dup_local = call(
         stash_kernel(count, rows, step),
@@ -627,11 +612,10 @@
         ddown_local,
         ddown_flip,
     )
-    own_far, slope = lax.optimization_barrier((own_far, slope))
-    blocks = [own, own_far]
-    for bit in bits[1:]:
-        blocks = blocks + [swapped(b, bit) for b in blocks]
-    own_now, other_now = blocks[0], blocks[half]
+    last_mine, slope = lax.optimization_barrier((mine[-1], slope))
+    mine = mine[:-1] + [last_mine]
+    theirs = [swapped(u, bits[-1]) for u in mine]
+    blocks = mine + theirs + stores
     z_list, adj_list = [], []
     for tick in range(TICKS):
         last = tick + 1 == TICKS
@@ -643,8 +627,7 @@
             ((2 * tokens, hidden), bf16),
             ((2 * tokens, width), bf16),
         ]
-        if tick:
-            outs.append(((4 * rows, width), bf16))
+        outs = outs + [((4 * rows, width), bf16)] * (1 if last else 2)
         keep, send, z_pair, adj, *rest = call(
             tick_kernel(count, rows, tick),
             outs,
@@ -656,8 +639,7 @@
             bend,
             scratch=[pltpu.VMEM((2 * tokens, width), bf16), pltpu.VMEM((2 * tokens, hidden), bf16)],
         )
-        if tick:
-            own_now = rest[0]
+        own_now = rest[0]
         z_list.append(z_pair)
         adj_list.append(adj)
         for bit in bits[::-1][:-1]:
@@ -686,7 +668,7 @@
                 keep,
                 got,
                 own_now,
-                other_now,
+                rest[1],
                 store,
                 stores[half],
                 gain,

time: 72.2 us -> 70.4 us (0.975)
  starting transfers between devices: 18.2 us -> 15.3 us
  waiting for transfers between devices: 18.3 us -> 20.1 us
    ppermute x2 -> x0, starting transfers between devices: 4.68 us -> none  [passed_along(): lax.ppermute(value, axis, [(source, source + steps) for source in range(l...]
    ppermute x1 -> x2, starting transfers between devices: 4.56 us -> 7.04 us  [parity_moved(): return lax.ppermute(value, ('section', 'dp'), pairs)]
    ppermute x13 -> x14, waiting for transfers between devices: 14.4 us -> 16.4 us  [swapped(): lax.ppermute(value, 'dp', [(source, source ^ bit) for source in range(cou...]
    ppermute x13 -> x14, starting transfers between devices: 8.97 us -> 8.29 us  [swapped(): lax.ppermute(value, 'dp', [(source, source ^ bit) for source in range(cou...]
    pallas_call x10 -> x11, Pallas kernels: 29.8 us -> 29.1 us  [call(): pl.pallas_call(body, in_specs=specs or [VM] * len(operands), out_specs=[V...]
    ppermute x1 -> x2, waiting for transfers between devices: 3.86 us -> 3.67 us  [parity_moved(): return lax.ppermute(value, ('section', 'dp'), pairs)]
  transfers between devices with their start and end apart: 16 -> 16, of which waited for: 8 -> 10; matrix products, arithmetic and copies ran while one was open for 0% -> 0% of each run, Pallas kernels for 21% -> 21%
where the time goes in v3:
time: 70.4 us; the launch traced here: 70.1 us
  Pallas kernels  33.9 us (48%)
  waiting for transfers between devices  20.1 us (29%)
  starting transfers between devices  15.3 us (22%)
  between operations  0.76 us (1%)
    pallas_call x11, Pallas kernels, call(): pl.pallas_call(body, in_specs=specs or [VM] * len(operands), out_specs=[V...  29.1 us
    ppermute x14, waiting for transfers between devices, swapped(): lax.ppermute(value, 'dp', [(source, source ^ bit) for source in range(cou...  16.4 us
    ppermute x14, starting transfers between devices, swapped(): lax.ppermute(value, 'dp', [(source, source ^ bit) for source in range(cou...  8.29 us
    ppermute x2, starting transfers between devices, parity_moved(): return lax.ppermute(value, ('section', 'dp'), pairs)  7.04 us
    pallas_call x1, Pallas kernels, shards(): pl.pallas_call(curvature_kernel(steps), in_specs=[VM] * (2 + 2 * TICKS),...  4.81 us
    ppermute x2, waiting for transfers between devices, parity_moved(): return lax.ppermute(value, ('section', 'dp'), pairs)  3.67 us
  transfers between devices with their start and end apart: 16, of which 10 were waited for; matrix products, arithmetic and copies ran while one was open for 0% of the time, Pallas kernels for 21%

profile of v3, /device:TPU:0, one launch (start us, length us, event | category | flops | bytes accessed | tf_op | source)
XLA Modules:
  0.0 70.1 jit_solution(9854941566696864022)
XLA Ops:
  0.6 1.2 %shard_map.172 = (bf16[16,2304]{1,0:T(8,128)(2,1)S(1)}, bf16[16,2304]{1,0:T(8,128)(2,1)S(1)}, bf16[64,2304]{1,0:T(8,128)(2,1)S(1)}, bf16[1,2304]{1,0:T(2,128)(2,1)S(1)}) custom-call(bf16[1,8,2304]{2,1,0:T(8,128)(2,1)} %refs_0_.1, bf16[1,8,2304]{2,1,0:T(8,128)(2,1)} %refs_1_.1, bf16[1,8,2304]{2,1,0:T(8,128)(2,1)} %refs_2_.1, bf16[1,8,2304]{2,1,0:T(8,128)(2,1)} %refs_3_.1, ...), custom_call_target="tpu_custom_call" | custom-call | tf_op jit(solution)/shard_map/pallas_call | solution.py:494
  1.8 3.1 %collective-permute-start.2 = (bf16[64,2304]{1,0:T(8,128)(2,1)S(1)}, bf16[64,2304]{1,0:T(8,128)(2,1)S(1)}, u32[]{:S(2)}, u32[]{:S(2)}) collective-permute-start(bf16[64,2304]{1,0:T(8,128)(2,1)S(1)} %get-tuple-element.48.refs_0_.refs_4_.stash_ref), channel_id=1, source_target_pairs={{0,2},{1,3},{2,0},{3,1},{4,6},{5,7},{6,4},{7,5},{8,10},{9,11},{10,... | collective-permute-start | bytes 884744 | tf_op jit(solution)/shard_map/ppermute | solution.py:33
  4.9 0.0 collective-permute-start
  4.9 1.3 %collective-permute-done.got_ref = bf16[16,2304]{1,0:T(8,128)(2,1)S(1)} collective-permute-done((bf16[16,2304]{1,0:T(8,128)(2,1)S(1)}, bf16[16,2304]{1,0:T(8,128)(2,1)S(1)}, u32[]{:S(2)}, u32[]{:S(2)}) %collective-permute-start) | collective-permute-done | bytes 73760 | tf_op jit(solution)/shard_map/ppermute | solution.py:33
  6.1 3.4 %collective-permute-start.1 = (bf16[32,2304]{1,0:T(8,128)(2,1)S(1)}, bf16[32,2304]{1,0:T(8,128)(2,1)S(1)}, u32[]{:S(2)}, u32[]{:S(2)}) collective-permute-start(bf16[32,2304]{1,0:T(8,128)(2,1)S(1)} %shard_map.173), channel_id=1, source_target_pairs={{0,4},{2,6},{4,8},{5,1},{6,10},{7,3},{8,12},{9,5},{10,14},{11,7},{... | collective-permute-start | bytes 442376 | tf_op jit(solution)/shard_map/ppermute | solution.py:61
  9.5 0.1 collective-permute-start.4
  9.6 5.0 %shard_map.174 = (bf16[1152,2304]{1,0:T(8,128)(2,1)S(1)}, bf16[2304,1152]{1,0:T(8,128)(2,1)S(1)}, bf16[1152,2304]{1,0:T(8,128)(2,1)S(1)}, bf16[2304,1152]{1,0:T(8,128)(2,1)S(1)}, f32[8,128]{1,0:T(8,128)S(1)}) custom-call(bf16[1152,2304]{1,0:T(8,128)(2,1)} %bitcast.6, bf16[1152,2304]{1,0:T(8,128)(2,1)} %bitcast.7), custom_call_target="tpu_custom_call" | custom-call | tf_op jit(solution)/shard_map/pallas_call | solution.py:494
  14.6 0.0 collective-permute-done.1.unit_ref
  14.6 0.0 collective-permute-done.2.far_ref
  14.7 0.6 collective-permute-start.5
  15.2 0.5 collective-permute-start.3
  15.7 0.0 collective-permute-start.6
  15.7 0.0 collective-permute-done.4.refs_2_.refs_6_.stash_other_ref
  15.7 0.7 collective-permute-done.5.refs_3_.refs_7_
  16.4 5.1 %shard_map.176 = (bf16[2304,128]{1,0:T(8,128)(2,1)S(1)}, bf16[1152,128]{1,0:T(8,128)(2,1)S(1)}, f32[64,1152]{1,0:T(8,128)S(1)}, f32[64,1152]{1,0:T(8,128)S(1)}, ...) custom-call(bf16[64,2304]{1,0:T(8,128)(2,1)S(1)} %get-tuple-element.48.refs_0_.refs_4_.stash_ref, ...), custom_call_target="tpu_custom_call" | custom-call | tf_op jit(solution)/shard_map/pallas_call | solution.py:494
  21.6 0.0 collective-permute-done.3.refs_1_
  21.6 0.4 collective-permute-start.7
  22.0 0.0 collective-permute-done.6.refs_2_
  22.0 1.0 %collective-permute-done.7.refs_3_ = bf16[32,2304]{1,0:T(8,128)(2,1)S(1)} collective-permute-done((bf16[32,2304]{1,0:T(8,128)(2,1)S(1)}, bf16[32,2304]{1,0:T(8,128)(2,1)S(1)}, u32[]{:S(2)}, u32[]{:S(2)}) %collective-permute-start.7) | collective-permute-done | bytes 147488 | tf_op jit(solution)/shard_map/ppermute | solution.py:33
  23.0 8.4 %shard_map.177 = (f32[64,2304]{1,0:T(8,128)S(1)}, bf16[64,2304]{1,0:T(8,128)(2,1)S(1)}, bf16[64,1152]{1,0:T(8,128)(2,1)S(1)}, bf16[64,2304]{1,0:T(8,128)(2,1)S(1...) custom-call(bf16[32,2304]{1,0:T(8,128)(2,1)S(1)} %get-tuple-element.50.refs_0_, ...), custom_call_target="tpu_custom_call" | custom-call | tf_op jit(solution)/shard_map/pallas_call | solution.py:494
  31.5 0.4 collective-permute-start.8
  31.9 1.2 %collective-permute-done.8.got_ref = bf16[64,2304]{1,0:T(8,128)(2,1)S(1)} collective-permute-done((bf16[64,2304]{1,0:T(8,128)(2,1)S(1)}, bf16[64,2304]{1,0:T(8,128)(2,1)S(1)}, u32[]{:S(2)}, u32[]{:S(2)}) %collective-permute-start.8) | collective-permute-done | bytes 294944 | tf_op jit(solution)/shard_map/ppermute | solution.py:33
  33.1 0.1 shard_map.178
  33.2 1.0 %collective-permute-start.9 = (bf16[32,2304]{1,0:T(8,128)(2,1)S(1)}, bf16[32,2304]{1,0:T(8,128)(2,1)S(1)}, u32[]{:S(2)}, u32[]{:S(2)}) collective-permute-start(bf16[32,2304]{1,0:T(8,128)(2,1)S(1)} %get-tuple-element.66), channel_id=1, source_target_pairs={{0,2},{1,3},{2,0},{3,1},{4,6},{5,7},{6,4},{7,5},{8,10},{9,11},{10,... | collective-permute-start | bytes 442376 | tf_op jit(solution)/shard_map/ppermute | solution.py:33
  34.2 5.2 %collective-permute-done.9.got_ref = bf16[32,2304]{1,0:T(8,128)(2,1)S(1)} collective-permute-done((bf16[32,2304]{1,0:T(8,128)(2,1)S(1)}, bf16[32,2304]{1,0:T(8,128)(2,1)S(1)}, u32[]{:S(2)}, u32[]{:S(2)}) %collective-permute-start.9) | collective-permute-done | bytes 147488 | tf_op jit(solution)/shard_map/ppermute | solution.py:33
  39.3 0.1 shard_map.179
  39.4 3.6 %collective-permute-start.10 = (bf16[32,2304]{1,0:T(8,128)(2,1)S(1)}, bf16[32,2304]{1,0:T(8,128)(2,1)S(1)}, u32[]{:S(2)}, u32[]{:S(2)}) collective-permute-start(bf16[32,2304]{1,0:T(8,128)(2,1)S(1)} %shard_map.179), channel_id=1, source_target_pairs={{0,4},{2,6},{4,8},{5,1},{6,10},{7,3},{8,12},{9,5},{10,14},{11,7},{... | collective-permute-start | bytes 442376 | tf_op jit(solution)/shard_map/ppermute | solution.py:61
  43.1 3.7 %collective-permute-done.10.refs_0_ = bf16[32,2304]{1,0:T(8,128)(2,1)S(1)} collective-permute-done((bf16[32,2304]{1,0:T(8,128)(2,1)S(1)}, bf16[32,2304]{1,0:T(8,128)(2,1)S(1)}, u32[]{:S(2)}, u32[]{:S(2)}) %collective-permute-start.10) | collective-permute-done | bytes 147488 | tf_op jit(solution)/shard_map/ppermute | solution.py:61
  46.7 1.0 %collective-permute-start.11 = (bf16[32,2304]{1,0:T(8,128)(2,1)S(1)}, bf16[32,2304]{1,0:T(8,128)(2,1)S(1)}, u32[]{:S(2)}, u32[]{:S(2)}) collective-permute-start(bf16[32,2304]{1,0:T(8,128)(2,1)S(1)} %collective-permute-done.10.refs_0_), channel_id=1, source_target_pairs={{0,2},{1,3},{2,0},{3,1},{4,6},{5,7},{6,4},{7,5},{8,10},{9,11},{10,... | collective-permute-start | bytes 442376 | tf_op jit(solution)/shard_map/ppermute | solution.py:33
  47.7 0.0 collective-permute-start.12
  47.7 4.2 %collective-permute-done.11.refs_1_ = bf16[32,2304]{1,0:T(8,128)(2,1)S(1)} collective-permute-done((bf16[32,2304]{1,0:T(8,128)(2,1)S(1)}, bf16[32,2304]{1,0:T(8,128)(2,1)S(1)}, u32[]{:S(2)}, u32[]{:S(2)}) %collective-permute-start.11) | collective-permute-done | bytes 147488 | tf_op jit(solution)/shard_map/ppermute | solution.py:33
  51.9 0.0 collective-permute-start.13
  51.9 0.0 collective-permute-done.12.refs_2_
  51.9 1.4 %collective-permute-done.13.refs_3_ = bf16[32,2304]{1,0:T(8,128)(2,1)S(1)} collective-permute-done((bf16[32,2304]{1,0:T(8,128)(2,1)S(1)}, bf16[32,2304]{1,0:T(8,128)(2,1)S(1)}, u32[]{:S(2)}, u32[]{:S(2)}) %collective-permute-start.13) | collective-permute-done | bytes 147488 | tf_op jit(solution)/shard_map/ppermute | solution.py:33
  53.2 8.4 %shard_map.180 = (f32[64,2304]{1,0:T(8,128)S(1)}, bf16[64,2304]{1,0:T(8,128)(2,1)S(1)}, bf16[64,1152]{1,0:T(8,128)(2,1)S(1)}, bf16[64,2304]{1,0:T(8,128)(2,1)S(1)}, bf16[32,2304]{1,0:T(8,128)(2,1)S(1)}) custom-call(bf16[32,2304]{1,0:T(8,128)(2,1)S(1)} %collective-permute-done.10.refs_0_, bf16[32,2304]{1,0:T(8,128)(2,1)S(1)} %collective-permute-done.11.refs_1_, ...), custom_call_target="tpu_custom_call" | custom-call | tf_op jit(solution)/shard_map/pallas_call | solution.py:494
  61.7 0.2 collective-permute-start.14
  61.9 1.4 %collective-permute-done.14.got_ref = bf16[64,2304]{1,0:T(8,128)(2,1)S(1)} collective-permute-done((bf16[64,2304]{1,0:T(8,128)(2,1)S(1)}, bf16[64,2304]{1,0:T(8,128)(2,1)S(1)}, u32[]{:S(2)}, u32[]{:S(2)}) %collective-permute-start.14) | collective-permute-done | bytes 294944 | tf_op jit(solution)/shard_map/ppermute | solution.py:33
  63.3 0.1 shard_map.181
  63.4 1.0 %collective-permute-start.15 = (bf16[32,2304]{1,0:T(8,128)(2,1)S(1)}, bf16[32,2304]{1,0:T(8,128)(2,1)S(1)}, u32[]{:S(2)}, u32[]{:S(2)}) collective-permute-start(bf16[32,2304]{1,0:T(8,128)(2,1)S(1)} %get-tuple-element.72), channel_id=1, source_target_pairs={{0,2},{1,3},{2,0},{3,1},{4,6},{5,7},{6,4},{7,5},{8,10},{9,11},{10,... | collective-permute-start | bytes 442376 | tf_op jit(solution)/shard_map/ppermute | solution.py:33
  64.4 4.8 %shard_map.183 = (bf16[2304,1152]{1,0:T(8,128)(2,1)}, bf16[1152,2304]{1,0:T(8,128)(2,1)}) custom-call(bf16[2304,128]{1,0:T(8,128)(2,1)S(1)} %get-tuple-element.78.refs_0_, bf16[1152,128]{1,0:T(8,128)(2,1)S(1)} %get-tuple-element.79.refs_1_, bf16[64,1152]{1,0:T(8,128)(2,1)S(1)} %get-tuple-element.80.refs_2_, bf16[64,1152]{1,0:T(8,128)(2,1)S(1)} %get-tuple-element.81.refs_3_, ...), custom_call_target="tpu_custom_call" | custom-call | tf_op jit(solution)/shard_map/pallas_call | solution.py:684
  69.2 0.1 collective-permute-done.15.got_ref
  69.3 0.8 %shard_map.182 = (bf16[1,8,2304]{2,1,0:T(8,128)(2,1)}, bf16[1,8,2304]{2,1,0:T(8,128)(2,1)}, bf16[1,8,2304]{2,1,0:T(8,128)(2,1)}, bf16[1,8,2304]{2,1,0:T(8,128)(2,1)}) custom-call(f32[32,2304]{1,0:T(8,128)S(1)} %get-tuple-element.71.keep_ref, bf16[32,2304]{1,0:T(8,128)(2,1)S(1)} %collective-permute-done.15.got_ref, ...), custom_call_target="tpu_custom_call" | custom-call | tf_op jit(solution)/shard_map/pallas_call | solution.py:494
  (2 shorter events, 0.0 us)
Async XLA Ops:
  1.8 12.8 %collective-permute-start.2 = (bf16[64,2304]{1,0:T(8,128)(2,1)S(1)}, bf16[64,2304]{1,0:T(8,128)(2,1)S(1)}, u32[]{:S(2)}, u32[]{:S(2)}) collective-permute-start(bf16[64,2304]{1,0:T(8,128)(2,1)S(1)} %get-tuple-element.48.refs_0_.refs_4_.stash_ref), channel_id=1, source_target_pairs={{0,2},{1,3},{2,0},{3,1},{4,6},{5,7},{6,4},{7,5},{8,10},{9,11},{10,... | collective-permute-start | bytes 884744 | tf_op jit(solution)/shard_map/ppermute | solution.py:33
  4.9 1.3 %collective-permute-start = (bf16[16,2304]{1,0:T(8,128)(2,1)S(1)}, bf16[16,2304]{1,0:T(8,128)(2,1)S(1)}, u32[]{:S(2)}, u32[]{:S(2)}) collective-permute-start(bf16[16,2304]{1,0:T(8,128)(2,1)S(1)} %get-tuple-element.47), channel_id=1, source_target_pairs={{0,1},{1,0},{2,3},{3,2},{4,5},{5,4},{6,7},{7,6},{8,9},{9,8},{10,11... | collective-permute-start | bytes 221192 | tf_op jit(solution)/shard_map/ppermute | solution.py:33
  6.1 8.5 %collective-permute-start.1 = (bf16[32,2304]{1,0:T(8,128)(2,1)S(1)}, bf16[32,2304]{1,0:T(8,128)(2,1)S(1)}, u32[]{:S(2)}, u32[]{:S(2)}) collective-permute-start(bf16[32,2304]{1,0:T(8,128)(2,1)S(1)} %shard_map.173), channel_id=1, source_target_pairs={{0,4},{2,6},{4,8},{5,1},{6,10},{7,3},{8,12},{9,5},{10,14},{11,7},{... | collective-permute-start | bytes 442376 | tf_op jit(solution)/shard_map/ppermute | solution.py:61
  9.5 6.2 %collective-permute-start.4 = (bf16[64,2304]{1,0:T(8,128)(2,1)S(1)}, bf16[64,2304]{1,0:T(8,128)(2,1)S(1)}, u32[]{:S(2)}, u32[]{:S(2)}) collective-permute-start(bf16[64,2304]{1,0:T(8,128)(2,1)S(1)} %get-tuple-element.48.refs_0_.refs_4_.stash_ref), channel_id=1, source_target_pairs={{0,1},{1,0},{2,3},{3,2},{4,5},{5,4},{6,7},{7,6},{8,9},{9,8},{10,11... | collective-permute-start | bytes 884744 | tf_op jit(solution)/shard_map/ppermute | solution.py:33
  14.7 1.8 %collective-permute-start.5 = (bf16[64,2304]{1,0:T(8,128)(2,1)S(1)}, bf16[64,2304]{1,0:T(8,128)(2,1)S(1)}, u32[]{:S(2)}, u32[]{:S(2)}) collective-permute-start(bf16[64,2304]{1,0:T(8,128)(2,1)S(1)} %get-tuple-element.51.refs_1_.refs_5_), channel_id=1, source_target_pairs={{0,1},{1,0},{2,3},{3,2},{4,5},{5,4},{6,7},{7,6},{8,9},{9,8},{10,11... | collective-permute-start | bytes 884744 | tf_op jit(solution)/shard_map/ppermute | solution.py:33
  15.2 6.4 %collective-permute-start.3 = (bf16[32,2304]{1,0:T(8,128)(2,1)S(1)}, bf16[32,2304]{1,0:T(8,128)(2,1)S(1)}, u32[]{:S(2)}, u32[]{:S(2)}) collective-permute-start(bf16[32,2304]{1,0:T(8,128)(2,1)S(1)} %get-tuple-element.50.refs_0_), channel_id=1, source_target_pairs={{0,2},{1,3},{2,0},{3,1},{4,6},{5,7},{6,4},{7,5},{8,10},{9,11},{10,... | collective-permute-start | bytes 442376 | tf_op jit(solution)/shard_map/ppermute | solution.py:33
  15.7 6.3 %collective-permute-start.6 = (bf16[32,2304]{1,0:T(8,128)(2,1)S(1)}, bf16[32,2304]{1,0:T(8,128)(2,1)S(1)}, u32[]{:S(2)}, u32[]{:S(2)}) collective-permute-start(bf16[32,2304]{1,0:T(8,128)(2,1)S(1)} %get-tuple-element.50.refs_0_), channel_id=1, source_target_pairs={{0,1},{1,0},{2,3},{3,2},{4,5},{5,4},{6,7},{7,6},{8,9},{9,8},{10,11... | collective-permute-start | bytes 442376 | tf_op jit(solution)/shard_map/ppermute | solution.py:33
  21.6 1.4 %collective-permute-start.7 = (bf16[32,2304]{1,0:T(8,128)(2,1)S(1)}, bf16[32,2304]{1,0:T(8,128)(2,1)S(1)}, u32[]{:S(2)}, u32[]{:S(2)}) collective-permute-start(bf16[32,2304]{1,0:T(8,128)(2,1)S(1)} %collective-permute-done.3.refs_1_), channel_id=1, source_target_pairs={{0,1},{1,0},{2,3},{3,2},{4,5},{5,4},{6,7},{7,6},{8,9},{9,8},{10,11... | collective-permute-start | bytes 442376 | tf_op jit(solution)/shard_map/ppermute | solution.py:33
  31.5 1.6 %collective-permute-start.8 = (bf16[64,2304]{1,0:T(8,128)(2,1)S(1)}, bf16[64,2304]{1,0:T(8,128)(2,1)S(1)}, u32[]{:S(2)}, u32[]{:S(2)}) collective-permute-start(bf16[64,2304]{1,0:T(8,128)(2,1)S(1)} %get-tuple-element.64), channel_id=1, source_target_pairs={{0,1},{1,0},{2,3},{3,2},{4,5},{5,4},{6,7},{7,6},{8,9},{9,8},{10,11... | collective-permute-start | bytes 884744 | tf_op jit(solution)/shard_map/ppermute | solution.py:33
  33.2 6.2 %collective-permute-start.9 = (bf16[32,2304]{1,0:T(8,128)(2,1)S(1)}, bf16[32,2304]{1,0:T(8,128)(2,1)S(1)}, u32[]{:S(2)}, u32[]{:S(2)}) collective-permute-start(bf16[32,2304]{1,0:T(8,128)(2,1)S(1)} %get-tuple-element.66), channel_id=1, source_target_pairs={{0,2},{1,3},{2,0},{3,1},{4,6},{5,7},{6,4},{7,5},{8,10},{9,11},{10,... | collective-permute-start | bytes 442376 | tf_op jit(solution)/shard_map/ppermute | solution.py:33
  39.4 7.3 %collective-permute-start.10 = (bf16[32,2304]{1,0:T(8,128)(2,1)S(1)}, bf16[32,2304]{1,0:T(8,128)(2,1)S(1)}, u32[]{:S(2)}, u32[]{:S(2)}) collective-permute-start(bf16[32,2304]{1,0:T(8,128)(2,1)S(1)} %shard_map.179), channel_id=1, source_target_pairs={{0,4},{2,6},{4,8},{5,1},{6,10},{7,3},{8,12},{9,5},{10,14},{11,7},{... | collective-permute-start | bytes 442376 | tf_op jit(solution)/shard_map/ppermute | solution.py:61
  46.7 5.1 %collective-permute-start.11 = (bf16[32,2304]{1,0:T(8,128)(2,1)S(1)}, bf16[32,2304]{1,0:T(8,128)(2,1)S(1)}, u32[]{:S(2)}, u32[]{:S(2)}) collective-permute-start(bf16[32,2304]{1,0:T(8,128)(2,1)S(1)} %collective-permute-done.10.refs_0_), channel_id=1, source_target_pairs={{0,2},{1,3},{2,0},{3,1},{4,6},{5,7},{6,4},{7,5},{8,10},{9,11},{10,... | collective-permute-start | bytes 442376 | tf_op jit(solution)/shard_map/ppermute | solution.py:33
  47.7 4.2 %collective-permute-start.12 = (bf16[32,2304]{1,0:T(8,128)(2,1)S(1)}, bf16[32,2304]{1,0:T(8,128)(2,1)S(1)}, u32[]{:S(2)}, u32[]{:S(2)}) collective-permute-start(bf16[32,2304]{1,0:T(8,128)(2,1)S(1)} %collective-permute-done.10.refs_0_), channel_id=1, source_target_pairs={{0,1},{1,0},{2,3},{3,2},{4,5},{5,4},{6,7},{7,6},{8,9},{9,8},{10,11... | collective-permute-start | bytes 442376 | tf_op jit(solution)/shard_map/ppermute | solution.py:33
  51.9 1.4 %collective-permute-start.13 = (bf16[32,2304]{1,0:T(8,128)(2,1)S(1)}, bf16[32,2304]{1,0:T(8,128)(2,1)S(1)}, u32[]{:S(2)}, u32[]{:S(2)}) collective-permute-start(bf16[32,2304]{1,0:T(8,128)(2,1)S(1)} %collective-permute-done.11.refs_1_), channel_id=1, source_target_pairs={{0,1},{1,0},{2,3},{3,2},{4,5},{5,4},{6,7},{7,6},{8,9},{9,8},{10,11... | collective-permute-start | bytes 442376 | tf_op jit(solution)/shard_map/ppermute | solution.py:33
  61.7 1.6 %collective-permute-start.14 = (bf16[64,2304]{1,0:T(8,128)(2,1)S(1)}, bf16[64,2304]{1,0:T(8,128)(2,1)S(1)}, u32[]{:S(2)}, u32[]{:S(2)}) collective-permute-start(bf16[64,2304]{1,0:T(8,128)(2,1)S(1)} %get-tuple-element.70), channel_id=1, source_target_pairs={{0,1},{1,0},{2,3},{3,2},{4,5},{5,4},{6,7},{7,6},{8,9},{9,8},{10,11... | collective-permute-start | bytes 884744 | tf_op jit(solution)/shard_map/ppermute | solution.py:33
  63.4 6.0 %collective-permute-start.15 = (bf16[32,2304]{1,0:T(8,128)(2,1)S(1)}, bf16[32,2304]{1,0:T(8,128)(2,1)S(1)}, u32[]{:S(2)}, u32[]{:S(2)}) collective-permute-start(bf16[32,2304]{1,0:T(8,128)(2,1)S(1)} %get-tuple-element.72), channel_id=1, source_target_pairs={{0,2},{1,3},{2,0},{3,1},{4,6},{5,7},{6,4},{7,5},{8,10},{9,11},{10,... | collective-permute-start | bytes 442376 | tf_op jit(solution)/shard_map/ppermute | solution.py:33

commit v4 on v3

--- a/solution.py
+++ b/solution.py
@@ -158,6 +158,10 @@
     far_out_ref[...] = far_ref[...]
 
 
+def wait_body(unit_ref, token_ref, out_ref):
+    out_ref[...] = unit_ref[...]
+
+
 def start_all(copies):
     for copy in copies:
         copy.start()
@@ -194,25 +198,33 @@
     return body
 
 
+def stash_rows(blocks, gain_ref, tick, rows, stack, plain):
+    gain_wide = gain_ref[...].astype(f32)
+    normed, normed_tan = norm_rows(
+        pick(blocks, 2 * tick, rows), pick(blocks, 2 * tick + 1, rows), gain_wide
+    )
+    tokens = normed.shape[0]
+    stack[:tokens, :] = normed_tan.astype(bf16)
+    stack[tokens:, :] = normed.astype(bf16)
+    plain[...] = normed.astype(bf16)
+
+
+def stash_hidden(both, side, slope_ref, bend_ref):
+    tokens = side.shape[0]
+    linear_tan = both[:tokens] + side
+    value, first, second = gelu_parts(both[tokens:])
+    slope_ref[...] = first
+    bend_ref[...] = second * linear_tan
+    return jnp.concatenate([first * linear_tan, value], axis=0).astype(bf16)
+
+
 def stash_kernel(count, rows, step):
-    tokens = count * rows
-
     def body(*refs):
         blocks = refs[:count]
         gain_ref, up_hbm, dup_hbm = refs[count : count + 3]
-        (
-            m_ref,
-            q_ref,
-            slope_ref,
-            bend_ref,
-            up_ref,
-            dup_ref,
-            stack,
-            plain,
-            both,
-            side,
-            sems,
-        ) = refs[count + 3 :]
+        m_ref, q_ref, slope_ref, bend_ref, up_ref, dup_ref, plain, both, side, sems = refs[
+            count + 3 :
+        ]
         steps = up_hbm.shape[0] // step
         loads = ((up_hbm, up_ref), (dup_hbm, dup_ref))
 
@@ -224,38 +236,43 @@
             ]
 
         lax.fori_loop(0, steps, lambda i, c: start_all(copies(i)), None)
-        gain_wide = gain_ref[...].astype(f32)
-        for tick in range(TICKS):
-            normed, normed_tan = norm_rows(
-                pick(blocks, 2 * tick, rows), pick(blocks, 2 * tick + 1, rows), gain_wide
-            )
-            base = 2 * tick * tokens
-            stack[base : base + tokens, :] = normed_tan.astype(bf16)
-            stack[base + tokens : base + 2 * tokens, :] = normed.astype(bf16)
-            plain[tick * tokens : (tick + 1) * tokens, :] = normed.astype(bf16)
-        m_ref[...] = stack[...].T
+        stash_rows(blocks, gain_ref, 0, rows, m_ref, plain)
         both[...] = jnp.zeros_like(both)
         side[...] = jnp.zeros_like(side)
 
         def work(i, carry):
             span = pl.ds(pl.multiple_of(i * step, step), step)
-            sides = zip(copies(i), loads, ((stack, both), (plain, side)))
+            sides = zip(copies(i), loads, ((m_ref, both), (plain, side)))
             for copy, (_, dst), (left, total) in sides:
                 copy.wait()
                 total[...] += matrix_product(left[:, span], dst[span, :])
 
         lax.fori_loop(0, steps, work, None)
-        for tick in range(TICKS):
-            base = 2 * tick * tokens
-            linear = both[base + tokens : base + 2 * tokens, :]
-            linear_tan = (
-                both[base : base + tokens, :] + side[tick * tokens : (tick + 1) * tokens, :]
-            )
-            value, first, second = gelu_parts(linear)
-            q_pair = jnp.concatenate([first * linear_tan, value], axis=0).astype(bf16)
-            q_ref[:, base : base + 2 * tokens] = q_pair.T
-            slope_ref[tick * tokens : (tick + 1) * tokens, :] = first
-            bend_ref[tick * tokens : (tick + 1) * tokens, :] = second * linear_tan
+        q_ref[...] = stash_hidden(both[...], side[...], slope_ref, bend_ref)
+
+    return body
+
+
+def later_kernel(count, rows):
+    later = TICKS - 1
+
+    def body(*refs):
+        blocks = refs[:count]
+        gain_ref, up_ref, dup_ref, m_ref, q_ref, _ = refs[count : count + 6]
+        m_out, q_out = refs[count + 6 : count + 8]
+        slopes = refs[count + 8 : count + 8 + later]
+        bends = refs[count + 8 + later : count + 8 + 2 * later]
+        stack, plain = refs[count + 8 + 2 * later :]
+        size = m_ref.shape[0]
+        m_out[:, :size] = m_ref[...].T
+        q_out[:, :size] = q_ref[...].T
+        for tick in range(1, TICKS):
+            stash_rows(blocks, gain_ref, tick, rows, stack, plain)
+            both = matrix_product(stack[...], up_ref[...])
+            side = matrix_product(plain[...], dup_ref[...])
+            q_pair = stash_hidden(both, side, slopes[tick - 1], bends[tick - 1])
+            m_out[:, tick * size : (tick + 1) * size] = stack[...].T
+            q_out[:, tick * size : (tick + 1) * size] = q_pair.T
 
     return body
 
@@ -308,7 +325,7 @@
         adj_ref[tokens:, :] = values[3].astype(bf16)
         hidden, width = up_ref.shape[1], up_ref.shape[0]
         size = hidden
-        base = tick * tokens
+        base = 0
 
         def inner(i, carry):
             at = i * size if hidden % size == 0 else jnp.minimum(i * size, hidden - size)
@@ -556,7 +573,7 @@
     arrived = parity_moved(unit)
     far = swapped(store, bits[0])
 
-    step = chunk_rows(hidden, 128)
+    step = chunk_rows(hidden, 384)
     down_local, down_flip, ddown_local, ddown_flip, token = call(
         load_down_kernel(step),
         [
@@ -580,13 +597,13 @@
         stores = stores + [swapped(b, bit) for b in stores]
     mine = gather_blocks(arrived, bits[:-1])
     step = chunk_rows(width, 768)
-    m_all, q_all, slope, bend, up_local, dup_local = call(
+    first_m, first_q, slope, bend, up_local, dup_local = call(
         stash_kernel(count, rows, step),
         [
-            ((width, pairs), bf16),
-            ((hidden, pairs), bf16),
-            ((TICKS * tokens, hidden), f32),
-            ((TICKS * tokens, hidden), f32),
+            ((2 * tokens, width), bf16),
+            ((2 * tokens, hidden), bf16),
+            ((tokens, hidden), f32),
+            ((tokens, hidden), f32),
             pltpu.VMEM((width, hidden), bf16),
             pltpu.VMEM((width, hidden), bf16),
         ],
@@ -597,10 +614,9 @@
         up_dir[0],
         specs=[VM] * (count + 1) + [HBM, HBM],
         scratch=[
-            pltpu.VMEM((pairs, width), bf16),
-            pltpu.VMEM((TICKS * tokens, width), bf16),
-            pltpu.VMEM((pairs, hidden), f32),
-            pltpu.VMEM((TICKS * tokens, hidden), f32),
+            pltpu.VMEM((tokens, width), bf16),
+            pltpu.VMEM((2 * tokens, hidden), f32),
+            pltpu.VMEM((tokens, hidden), f32),
             pltpu.SemaphoreType.DMA((2 * (width // step),)),
         ],
     )
@@ -674,6 +690,28 @@
                 gain,
             )[0]
             arrived = parity_moved(unit)
+            if tick == 0:
+                m_all, q_all, *curves = call(
+                    later_kernel(count, rows),
+                    [((width, pairs), bf16), ((hidden, pairs), bf16)]
+                    + [((tokens, hidden), f32)] * (2 * (TICKS - 1)),
+                    grant,
+                    *stores,
+                    gain,
+                    up_local,
+                    dup_local,
+                    first_m,
+                    first_q,
+                    unit,
+                    scratch=[
+                        pltpu.VMEM((2 * tokens, width), bf16),
+                        pltpu.VMEM((tokens, width), bf16),
+                    ],
+                )
+                arrived = call(
+                    wait_body, [((4 * rows, width), bf16)], grant, arrived, curves[0]
+                )[0]
+            slope, bend = curves[tick], curves[tick + TICKS - 1]
             mine = gather_blocks(arrived, bits[:-1])
             theirs = [swapped(u, bits[-1]) for u in mine]
             blocks = mine + theirs + stores

time: 70.4 us -> 69.7 us (0.990)
  waiting for transfers between devices: 20.1 us -> 17.6 us
  Pallas kernels: 33.9 us -> 35.4 us
    ppermute x2, waiting for transfers between devices: 3.67 us -> 1.42 us  [parity_moved(): return lax.ppermute(value, ('section', 'dp'), pairs)]
    pallas_call x11 -> x13, Pallas kernels: 29.1 us -> 30.6 us  [call(): pl.pallas_call(body, in_specs=specs or [VM] * len(operands), out_specs=[V...]
  transfers between devices with their start and end apart: 16 -> 16, of which waited for: 10 -> 9; matrix products, arithmetic and copies ran while one was open for 0% -> 0% of each run, Pallas kernels for 21% -> 24%
where the time goes in v4:
time: 69.7 us; the launch traced here: 69.5 us
  Pallas kernels  35.4 us (51%)
  waiting for transfers between devices  17.6 us (25%)
  starting transfers between devices  15.7 us (23%)
  between operations  0.76 us (1%)
    pallas_call x13, Pallas kernels, call(): pl.pallas_call(body, in_specs=specs or [VM] * len(operands), out_specs=[V...  30.6 us
    ppermute x14, waiting for transfers between devices, swapped(): lax.ppermute(value, 'dp', [(source, source ^ bit) for source in range(cou...  16.2 us
    ppermute x14, starting transfers between devices, swapped(): lax.ppermute(value, 'dp', [(source, source ^ bit) for source in range(cou...  8.63 us
    ppermute x2, starting transfers between devices, parity_moved(): return lax.ppermute(value, ('section', 'dp'), pairs)  7.04 us
    pallas_call x1, Pallas kernels, shards(): pl.pallas_call(curvature_kernel(steps), in_specs=[VM] * (2 + 2 * TICKS),...  4.79 us
    ppermute x2, waiting for transfers between devices, parity_moved(): return lax.ppermute(value, ('section', 'dp'), pairs)  1.42 us
  transfers between devices with their start and end apart: 16, of which 9 were waited for; matrix products, arithmetic and copies ran while one was open for 0% of the time, Pallas kernels for 24%

profile of v4, /device:TPU:0, one launch (start us, length us, event | category | flops | bytes accessed | tf_op | source)
XLA Modules:
  0.0 69.5 jit_solution(11108870691153331260)
XLA Ops:
  0.6 1.2 %shard_map.172 = (bf16[16,2304]{1,0:T(8,128)(2,1)S(1)}, bf16[16,2304]{1,0:T(8,128)(2,1)S(1)}, bf16[64,2304]{1,0:T(8,128)(2,1)S(1)}, bf16[1,2304]{1,0:T(2,128)(2,1)S(1)}) custom-call(bf16[1,8,2304]{2,1,0:T(8,128)(2,1)} %refs_0_.1, bf16[1,8,2304]{2,1,0:T(8,128)(2,1)} %refs_1_.1, bf16[1,8,2304]{2,1,0:T(8,128)(2,1)} %refs_2_.1, bf16[1,8,2304]{2,1,0:T(8,128)(2,1)} %refs_3_.1, ...), custom_call_target="tpu_custom_call" | custom-call | tf_op jit(solution)/shard_map/pallas_call | solution.py:511
  1.8 3.1 %collective-permute-start.2 = (bf16[64,2304]{1,0:T(8,128)(2,1)S(1)}, bf16[64,2304]{1,0:T(8,128)(2,1)S(1)}, u32[]{:S(2)}, u32[]{:S(2)}) collective-permute-start(bf16[64,2304]{1,0:T(8,128)(2,1)S(1)} %get-tuple-element.52.refs_0_.refs_4_.stash_ref), channel_id=1, source_target_pairs={{0,2},{1,3},{2,0},{3,1},{4,6},{5,7},{6,4},{7,5},{8,10},{9,11},{10,... | collective-permute-start | bytes 884744 | tf_op jit(solution)/shard_map/ppermute | solution.py:33
  4.9 0.0 collective-permute-start
  4.9 1.3 %collective-permute-done.got_ref = bf16[16,2304]{1,0:T(8,128)(2,1)S(1)} collective-permute-done((bf16[16,2304]{1,0:T(8,128)(2,1)S(1)}, bf16[16,2304]{1,0:T(8,128)(2,1)S(1)}, u32[]{:S(2)}, u32[]{:S(2)}) %collective-permute-start) | collective-permute-done | bytes 73760 | tf_op jit(solution)/shard_map/ppermute | solution.py:33
  6.1 3.4 %collective-permute-start.1 = (bf16[32,2304]{1,0:T(8,128)(2,1)S(1)}, bf16[32,2304]{1,0:T(8,128)(2,1)S(1)}, u32[]{:S(2)}, u32[]{:S(2)}) collective-permute-start(bf16[32,2304]{1,0:T(8,128)(2,1)S(1)} %shard_map.173), channel_id=1, source_target_pairs={{0,4},{2,6},{4,8},{5,1},{6,10},{7,3},{8,12},{9,5},{10,14},{11,7},{... | collective-permute-start | bytes 442376 | tf_op jit(solution)/shard_map/ppermute | solution.py:61
  9.5 0.1 collective-permute-start.4
  9.6 4.8 %shard_map.174 = (bf16[1152,2304]{1,0:T(8,128)(2,1)S(1)}, bf16[2304,1152]{1,0:T(8,128)(2,1)S(1)}, bf16[1152,2304]{1,0:T(8,128)(2,1)S(1)}, bf16[2304,1152]{1,0:T(8,128)(2,1)S(1)}, f32[8,128]{1,0:T(8,128)S(1)}) custom-call(bf16[1152,2304]{1,0:T(8,128)(2,1)} %bitcast.6, bf16[1152,2304]{1,0:T(8,128)(2,1)} %bitcast.7), custom_call_target="tpu_custom_call" | custom-call | tf_op jit(solution)/shard_map/pallas_call | solution.py:511
  14.4 0.0 collective-permute-done.1.unit_ref
  14.4 0.0 collective-permute-done.2.far_ref
  14.5 0.6 collective-permute-start.5
  15.0 0.5 collective-permute-start.3
  15.5 0.0 collective-permute-start.6
  15.5 0.0 collective-permute-done.4.refs_2_.refs_6_.stash_other_ref
  15.5 0.7 %collective-permute-done.5.refs_3_.refs_7_ = bf16[64,2304]{1,0:T(8,128)(2,1)S(1)} collective-permute-done((bf16[64,2304]{1,0:T(8,128)(2,1)S(1)}, bf16[64,2304]{1,0:T(8,128)(2,1)S(1)}, u32[]{:S(2)}, u32[]{:S(2)}) %collective-permute-start.5) | collective-permute-done | bytes 294944 | tf_op jit(solution)/shard_map/ppermute | solution.py:33
  16.2 4.7 %shard_map.176 = (bf16[64,2304]{1,0:T(8,128)(2,1)S(1)}, bf16[64,1152]{1,0:T(8,128)(2,1)S(1)}, f32[32,1152]{1,0:T(8,128)S(1)}, f32[32,1152]{1,0:T(8,128)S(1)}, bf...) custom-call(bf16[64,2304]{1,0:T(8,128)(2,1)S(1)} %get-tuple-element.52.refs_0_.refs_4_.stash_ref, ...), custom_call_target="tpu_custom_call" | custom-call | tf_op jit(solution)/shard_map/pallas_call | solution.py:511
  21.0 0.0 collective-permute-done.3.refs_1_
  21.0 0.4 collective-permute-start.7
  21.4 0.0 collective-permute-done.6.refs_2_
  21.4 1.0 %collective-permute-done.7.refs_3_ = bf16[32,2304]{1,0:T(8,128)(2,1)S(1)} collective-permute-done((bf16[32,2304]{1,0:T(8,128)(2,1)S(1)}, bf16[32,2304]{1,0:T(8,128)(2,1)S(1)}, u32[]{:S(2)}, u32[]{:S(2)}) %collective-permute-start.7) | collective-permute-done | bytes 147488 | tf_op jit(solution)/shard_map/ppermute | solution.py:33
  22.4 8.4 %shard_map.177 = (f32[64,2304]{1,0:T(8,128)S(1)}, bf16[64,2304]{1,0:T(8,128)(2,1)S(1)}, bf16[64,1152]{1,0:T(8,128)(2,1)S(1)}, bf16[64,2304]{1,0:T(8,128)(2,1)S(1...) custom-call(bf16[32,2304]{1,0:T(8,128)(2,1)S(1)} %get-tuple-element.54.refs_0_, ...), custom_call_target="tpu_custom_call" | custom-call | tf_op jit(solution)/shard_map/pallas_call | solution.py:511
  30.9 0.4 collective-permute-start.8
  31.3 1.2 %collective-permute-done.8.got_ref = bf16[64,2304]{1,0:T(8,128)(2,1)S(1)} collective-permute-done((bf16[64,2304]{1,0:T(8,128)(2,1)S(1)}, bf16[64,2304]{1,0:T(8,128)(2,1)S(1)}, u32[]{:S(2)}, u32[]{:S(2)}) %collective-permute-start.8) | collective-permute-done | bytes 294944 | tf_op jit(solution)/shard_map/ppermute | solution.py:33
  32.5 0.1 shard_map.178
  32.6 1.0 %collective-permute-start.9 = (bf16[32,2304]{1,0:T(8,128)(2,1)S(1)}, bf16[32,2304]{1,0:T(8,128)(2,1)S(1)}, u32[]{:S(2)}, u32[]{:S(2)}) collective-permute-start(bf16[32,2304]{1,0:T(8,128)(2,1)S(1)} %get-tuple-element.70), channel_id=1, source_target_pairs={{0,2},{1,3},{2,0},{3,1},{4,6},{5,7},{6,4},{7,5},{8,10},{9,11},{10,... | collective-permute-start | bytes 442376 | tf_op jit(solution)/shard_map/ppermute | solution.py:33
  33.6 5.1 %collective-permute-done.9.got_ref = bf16[32,2304]{1,0:T(8,128)(2,1)S(1)} collective-permute-done((bf16[32,2304]{1,0:T(8,128)(2,1)S(1)}, bf16[32,2304]{1,0:T(8,128)(2,1)S(1)}, u32[]{:S(2)}, u32[]{:S(2)}) %collective-permute-start.9) | collective-permute-done | bytes 147488 | tf_op jit(solution)/shard_map/ppermute | solution.py:33
  38.7 0.1 shard_map.179.refs_9_
  38.8 3.6 %collective-permute-start.10 = (bf16[32,2304]{1,0:T(8,128)(2,1)S(1)}, bf16[32,2304]{1,0:T(8,128)(2,1)S(1)}, u32[]{:S(2)}, u32[]{:S(2)}) collective-permute-start(bf16[32,2304]{1,0:T(8,128)(2,1)S(1)} %shard_map.179.refs_9_), channel_id=1, source_target_pairs={{0,4},{2,6},{4,8},{5,1},{6,10},{7,3},{8,12},{9,5},{10,14},{11,7},{... | collective-permute-start | bytes 442376 | tf_op jit(solution)/shard_map/ppermute | solution.py:61
  42.5 2.1 %shard_map.180 = (bf16[2304,128]{1,0:T(8,128)(2,1)S(1)}, bf16[1152,128]{1,0:T(8,128)(2,1)S(1)}, f32[32,1152]{1,0:T(8,128)S(1)}, f32[32,1152]{1,0:T(8,128)S(1)}) custom-call(bf16[64,2304]{1,0:T(8,128)(2,1)S(1)} %get-tuple-element.52.refs_0_.refs_4_.stash_ref, bf16[64,2304]{1,0:T(8,128)(2,1)S(1)} %get-tuple-element.55.refs_1_.refs_5_, ...), custom_call_target="tpu_custom_call" | custom-call | tf_op jit(solution)/shard_map/pallas_call | solution.py:511
  44.6 1.4 %collective-permute-done.10.unit_ref = bf16[32,2304]{1,0:T(8,128)(2,1)S(1)} collective-permute-done((bf16[32,2304]{1,0:T(8,128)(2,1)S(1)}, bf16[32,2304]{1,0:T(8,128)(2,1)S(1)}, u32[]{:S(2)}, u32[]{:S(2)}) %collective-permute-start.10) | collective-permute-done | bytes 147488 | tf_op jit(solution)/shard_map/ppermute | solution.py:61
  46.0 1.2 %collective-permute-start.11 = (bf16[32,2304]{1,0:T(8,128)(2,1)S(1)}, bf16[32,2304]{1,0:T(8,128)(2,1)S(1)}, u32[]{:S(2)}, u32[]{:S(2)}) collective-permute-start(bf16[32,2304]{1,0:T(8,128)(2,1)S(1)} %shard_map.181.refs_0_), channel_id=1, source_target_pairs={{0,2},{1,3},{2,0},{3,1},{4,6},{5,7},{6,4},{7,5},{8,10},{9,11},{10,... | collective-permute-start | bytes 442376 | tf_op jit(solution)/shard_map/ppermute | solution.py:33
  47.2 0.0 collective-permute-start.12
  47.2 4.0 %collective-permute-done.11.refs_1_ = bf16[32,2304]{1,0:T(8,128)(2,1)S(1)} collective-permute-done((bf16[32,2304]{1,0:T(8,128)(2,1)S(1)}, bf16[32,2304]{1,0:T(8,128)(2,1)S(1)}, u32[]{:S(2)}, u32[]{:S(2)}) %collective-permute-start.11) | collective-permute-done | bytes 147488 | tf_op jit(solution)/shard_map/ppermute | solution.py:33
  51.2 0.0 collective-permute-start.13
  51.2 0.0 collective-permute-done.12.refs_2_
  51.2 1.4 %collective-permute-done.13.refs_3_ = bf16[32,2304]{1,0:T(8,128)(2,1)S(1)} collective-permute-done((bf16[32,2304]{1,0:T(8,128)(2,1)S(1)}, bf16[32,2304]{1,0:T(8,128)(2,1)S(1)}, u32[]{:S(2)}, u32[]{:S(2)}) %collective-permute-start.13) | collective-permute-done | bytes 147488 | tf_op jit(solution)/shard_map/ppermute | solution.py:33
  52.6 8.4 %shard_map.182 = (f32[64,2304]{1,0:T(8,128)S(1)}, bf16[64,2304]{1,0:T(8,128)(2,1)S(1)}, bf16[64,1152]{1,0:T(8,128)(2,1)S(1)}, bf16[64,2304]{1,0:T(8,128)(2,1)S(1)}, bf16[32,2304]{1,0:T(8,128)(2,1)S(1)}) custom-call(bf16[32,2304]{1,0:T(8,128)(2,1)S(1)} %shard_map.181.refs_0_, bf16[32,2304]{1,0:T(8,128)(2,1)S(1)} %collective-permute-done.11.refs_1_, ...), custom_call_target="tpu_custom_call" | custom-call | tf_op jit(solution)/shard_map/pallas_call | solution.py:511
  61.0 0.2 collective-permute-start.14
  61.2 1.4 %collective-permute-done.14.got_ref = bf16[64,2304]{1,0:T(8,128)(2,1)S(1)} collective-permute-done((bf16[64,2304]{1,0:T(8,128)(2,1)S(1)}, bf16[64,2304]{1,0:T(8,128)(2,1)S(1)}, u32[]{:S(2)}, u32[]{:S(2)}) %collective-permute-start.14) | collective-permute-done | bytes 294944 | tf_op jit(solution)/shard_map/ppermute | solution.py:33
  62.6 0.1 shard_map.183
  62.7 1.2 %collective-permute-start.15 = (bf16[32,2304]{1,0:T(8,128)(2,1)S(1)}, bf16[32,2304]{1,0:T(8,128)(2,1)S(1)}, u32[]{:S(2)}, u32[]{:S(2)}) collective-permute-start(bf16[32,2304]{1,0:T(8,128)(2,1)S(1)} %get-tuple-element.80), channel_id=1, source_target_pairs={{0,2},{1,3},{2,0},{3,1},{4,6},{5,7},{6,4},{7,5},{8,10},{9,11},{10,... | collective-permute-start | bytes 442376 | tf_op jit(solution)/shard_map/ppermute | solution.py:33
  63.9 4.8 %shard_map.185 = (bf16[2304,1152]{1,0:T(8,128)(2,1)}, bf16[1152,2304]{1,0:T(8,128)(2,1)}) custom-call(bf16[2304,128]{1,0:T(8,128)(2,1)S(1)} %get-tuple-element.86.refs_0_, bf16[1152,128]{1,0:T(8,128)(2,1)S(1)} %get-tuple-element.87.refs_1_, bf16[64,1152]{1,0:T(8,128)(2,1)S(1)} %get-tuple-element.88.refs_2_, bf16[64,1152]{1,0:T(8,128)(2,1)S(1)} %get-tuple-element.89.refs_3_, ...), custom_call_target="tpu_custom_call" | custom-call | tf_op jit(solution)/shard_map/pallas_call | solution.py:722
  68.7 0.0 collective-permute-done.15.got_ref
  68.7 0.8 %shard_map.184 = (bf16[1,8,2304]{2,1,0:T(8,128)(2,1)}, bf16[1,8,2304]{2,1,0:T(8,128)(2,1)}, bf16[1,8,2304]{2,1,0:T(8,128)(2,1)}, bf16[1,8,2304]{2,1,0:T(8,128)(2,1)}) custom-call(f32[32,2304]{1,0:T(8,128)S(1)} %get-tuple-element.79.keep_ref, bf16[32,2304]{1,0:T(8,128)(2,1)S(1)} %collective-permute-done.15.got_ref, ...), custom_call_target="tpu_custom_call" | custom-call | tf_op jit(solution)/shard_map/pallas_call | solution.py:511
  (3 shorter events, 0.1 us)
Async XLA Ops:
  1.8 12.6 %collective-permute-start.2 = (bf16[64,2304]{1,0:T(8,128)(2,1)S(1)}, bf16[64,2304]{1,0:T(8,128)(2,1)S(1)}, u32[]{:S(2)}, u32[]{:S(2)}) collective-permute-start(bf16[64,2304]{1,0:T(8,128)(2,1)S(1)} %get-tuple-element.52.refs_0_.refs_4_.stash_ref), channel_id=1, source_target_pairs={{0,2},{1,3},{2,0},{3,1},{4,6},{5,7},{6,4},{7,5},{8,10},{9,11},{10,... | collective-permute-start | bytes 884744 | tf_op jit(solution)/shard_map/ppermute | solution.py:33
  4.9 1.3 %collective-permute-start = (bf16[16,2304]{1,0:T(8,128)(2,1)S(1)}, bf16[16,2304]{1,0:T(8,128)(2,1)S(1)}, u32[]{:S(2)}, u32[]{:S(2)}) collective-permute-start(bf16[16,2304]{1,0:T(8,128)(2,1)S(1)} %get-tuple-element.51), channel_id=1, source_target_pairs={{0,1},{1,0},{2,3},{3,2},{4,5},{5,4},{6,7},{7,6},{8,9},{9,8},{10,11... | collective-permute-start | bytes 221192 | tf_op jit(solution)/shard_map/ppermute | solution.py:33
  6.1 8.3 %collective-permute-start.1 = (bf16[32,2304]{1,0:T(8,128)(2,1)S(1)}, bf16[32,2304]{1,0:T(8,128)(2,1)S(1)}, u32[]{:S(2)}, u32[]{:S(2)}) collective-permute-start(bf16[32,2304]{1,0:T(8,128)(2,1)S(1)} %shard_map.173), channel_id=1, source_target_pairs={{0,4},{2,6},{4,8},{5,1},{6,10},{7,3},{8,12},{9,5},{10,14},{11,7},{... | collective-permute-start | bytes 442376 | tf_op jit(solution)/shard_map/ppermute | solution.py:61
  9.5 6.0 %collective-permute-start.4 = (bf16[64,2304]{1,0:T(8,128)(2,1)S(1)}, bf16[64,2304]{1,0:T(8,128)(2,1)S(1)}, u32[]{:S(2)}, u32[]{:S(2)}) collective-permute-start(bf16[64,2304]{1,0:T(8,128)(2,1)S(1)} %get-tuple-element.52.refs_0_.refs_4_.stash_ref), channel_id=1, source_target_pairs={{0,1},{1,0},{2,3},{3,2},{4,5},{5,4},{6,7},{7,6},{8,9},{9,8},{10,11... | collective-permute-start | bytes 884744 | tf_op jit(solution)/shard_map/ppermute | solution.py:33
  14.5 1.8 %collective-permute-start.5 = (bf16[64,2304]{1,0:T(8,128)(2,1)S(1)}, bf16[64,2304]{1,0:T(8,128)(2,1)S(1)}, u32[]{:S(2)}, u32[]{:S(2)}) collective-permute-start(bf16[64,2304]{1,0:T(8,128)(2,1)S(1)} %get-tuple-element.55.refs_1_.refs_5_), channel_id=1, source_target_pairs={{0,1},{1,0},{2,3},{3,2},{4,5},{5,4},{6,7},{7,6},{8,9},{9,8},{10,11... | collective-permute-start | bytes 884744 | tf_op jit(solution)/shard_map/ppermute | solution.py:33
  15.0 5.9 %collective-permute-start.3 = (bf16[32,2304]{1,0:T(8,128)(2,1)S(1)}, bf16[32,2304]{1,0:T(8,128)(2,1)S(1)}, u32[]{:S(2)}, u32[]{:S(2)}) collective-permute-start(bf16[32,2304]{1,0:T(8,128)(2,1)S(1)} %get-tuple-element.54.refs_0_), channel_id=1, source_target_pairs={{0,2},{1,3},{2,0},{3,1},{4,6},{5,7},{6,4},{7,5},{8,10},{9,11},{10,... | collective-permute-start | bytes 442376 | tf_op jit(solution)/shard_map/ppermute | solution.py:33
  15.5 5.9 %collective-permute-start.6 = (bf16[32,2304]{1,0:T(8,128)(2,1)S(1)}, bf16[32,2304]{1,0:T(8,128)(2,1)S(1)}, u32[]{:S(2)}, u32[]{:S(2)}) collective-permute-start(bf16[32,2304]{1,0:T(8,128)(2,1)S(1)} %get-tuple-element.54.refs_0_), channel_id=1, source_target_pairs={{0,1},{1,0},{2,3},{3,2},{4,5},{5,4},{6,7},{7,6},{8,9},{9,8},{10,11... | collective-permute-start | bytes 442376 | tf_op jit(solution)/shard_map/ppermute | solution.py:33
  21.0 1.4 %collective-permute-start.7 = (bf16[32,2304]{1,0:T(8,128)(2,1)S(1)}, bf16[32,2304]{1,0:T(8,128)(2,1)S(1)}, u32[]{:S(2)}, u32[]{:S(2)}) collective-permute-start(bf16[32,2304]{1,0:T(8,128)(2,1)S(1)} %collective-permute-done.3.refs_1_), channel_id=1, source_target_pairs={{0,1},{1,0},{2,3},{3,2},{4,5},{5,4},{6,7},{7,6},{8,9},{9,8},{10,11... | collective-permute-start | bytes 442376 | tf_op jit(solution)/shard_map/ppermute | solution.py:33
  30.9 1.6 %collective-permute-start.8 = (bf16[64,2304]{1,0:T(8,128)(2,1)S(1)}, bf16[64,2304]{1,0:T(8,128)(2,1)S(1)}, u32[]{:S(2)}, u32[]{:S(2)}) collective-permute-start(bf16[64,2304]{1,0:T(8,128)(2,1)S(1)} %get-tuple-element.68), channel_id=1, source_target_pairs={{0,1},{1,0},{2,3},{3,2},{4,5},{5,4},{6,7},{7,6},{8,9},{9,8},{10,11... | collective-permute-start | bytes 884744 | tf_op jit(solution)/shard_map/ppermute | solution.py:33
  32.6 6.2 %collective-permute-start.9 = (bf16[32,2304]{1,0:T(8,128)(2,1)S(1)}, bf16[32,2304]{1,0:T(8,128)(2,1)S(1)}, u32[]{:S(2)}, u32[]{:S(2)}) collective-permute-start(bf16[32,2304]{1,0:T(8,128)(2,1)S(1)} %get-tuple-element.70), channel_id=1, source_target_pairs={{0,2},{1,3},{2,0},{3,1},{4,6},{5,7},{6,4},{7,5},{8,10},{9,11},{10,... | collective-permute-start | bytes 442376 | tf_op jit(solution)/shard_map/ppermute | solution.py:33
  38.8 7.2 %collective-permute-start.10 = (bf16[32,2304]{1,0:T(8,128)(2,1)S(1)}, bf16[32,2304]{1,0:T(8,128)(2,1)S(1)}, u32[]{:S(2)}, u32[]{:S(2)}) collective-permute-start(bf16[32,2304]{1,0:T(8,128)(2,1)S(1)} %shard_map.179.refs_9_), channel_id=1, source_target_pairs={{0,4},{2,6},{4,8},{5,1},{6,10},{7,3},{8,12},{9,5},{10,14},{11,7},{... | collective-permute-start | bytes 442376 | tf_op jit(solution)/shard_map/ppermute | solution.py:61
  46.0 5.2 %collective-permute-start.11 = (bf16[32,2304]{1,0:T(8,128)(2,1)S(1)}, bf16[32,2304]{1,0:T(8,128)(2,1)S(1)}, u32[]{:S(2)}, u32[]{:S(2)}) collective-permute-start(bf16[32,2304]{1,0:T(8,128)(2,1)S(1)} %shard_map.181.refs_0_), channel_id=1, source_target_pairs={{0,2},{1,3},{2,0},{3,1},{4,6},{5,7},{6,4},{7,5},{8,10},{9,11},{10,... | collective-permute-start | bytes 442376 | tf_op jit(solution)/shard_map/ppermute | solution.py:33
  47.2 4.0 %collective-permute-start.12 = (bf16[32,2304]{1,0:T(8,128)(2,1)S(1)}, bf16[32,2304]{1,0:T(8,128)(2,1)S(1)}, u32[]{:S(2)}, u32[]{:S(2)}) collective-permute-start(bf16[32,2304]{1,0:T(8,128)(2,1)S(1)} %shard_map.181.refs_0_), channel_id=1, source_target_pairs={{0,1},{1,0},{2,3},{3,2},{4,5},{5,4},{6,7},{7,6},{8,9},{9,8},{10,11... | collective-permute-start | bytes 442376 | tf_op jit(solution)/shard_map/ppermute | solution.py:33
  51.2 1.4 %collective-permute-start.13 = (bf16[32,2304]{1,0:T(8,128)(2,1)S(1)}, bf16[32,2304]{1,0:T(8,128)(2,1)S(1)}, u32[]{:S(2)}, u32[]{:S(2)}) collective-permute-start(bf16[32,2304]{1,0:T(8,128)(2,1)S(1)} %collective-permute-done.11.refs_1_), channel_id=1, source_target_pairs={{0,1},{1,0},{2,3},{3,2},{4,5},{5,4},{6,7},{7,6},{8,9},{9,8},{10,11... | collective-permute-start | bytes 442376 | tf_op jit(solution)/shard_map/ppermute | solution.py:33
  61.0 1.6 %collective-permute-start.14 = (bf16[64,2304]{1,0:T(8,128)(2,1)S(1)}, bf16[64,2304]{1,0:T(8,128)(2,1)S(1)}, u32[]{:S(2)}, u32[]{:S(2)}) collective-permute-start(bf16[64,2304]{1,0:T(8,128)(2,1)S(1)} %get-tuple-element.78), channel_id=1, source_target_pairs={{0,1},{1,0},{2,3},{3,2},{4,5},{5,4},{6,7},{7,6},{8,9},{9,8},{10,11... | collective-permute-start | bytes 884744 | tf_op jit(solution)/shard_map/ppermute | solution.py:33
  62.7 6.0 %collective-permute-start.15 = (bf16[32,2304]{1,0:T(8,128)(2,1)S(1)}, bf16[32,2304]{1,0:T(8,128)(2,1)S(1)}, u32[]{:S(2)}, u32[]{:S(2)}) collective-permute-start(bf16[32,2304]{1,0:T(8,128)(2,1)S(1)} %get-tuple-element.80), channel_id=1, source_target_pairs={{0,2},{1,3},{2,0},{3,1},{4,6},{5,7},{6,4},{7,5},{8,10},{9,11},{10,... | collective-permute-start | bytes 442376 | tf_op jit(solution)/shard_map/ppermute | solution.py:33
